TPU v7x, 256 devices: a whole 4x4x8 slice. The times are simulated.
256 devices in a mesh: dp: 256 (over y, x, z, core).
Axes of the slice: x: 4, y: 4, z: 8, core: 2. Of those that a mesh axis runs over, the one named last changes fastest.
Arguments:
- image_emb: bfloat16 [2048, 1152], P('dp'), may hold values from -0.4375 to 0.4375
- text_tokens: bfloat16 [65536, 1152], P('dp'), may hold values from -0.078125 to 0.078125
- caption_ids: int32 [65536], P('dp'), may hold values from 0 to 2047, as said below
- groups: int32 [2048], P('dp'), may hold values from 0 to 511
- text_gain: float32 [1152], replicated, may hold values from 0.5 to 1.5
- log_scale: float32 [1], replicated, may hold values from 2 to 3
- logit_bias: float32 [1], replicated, may hold values from -3 to -1
Outputs:
- image_grad: float32 [2048, 1152], P('dp')
- token_grad: float32 [65536, 1152], P('dp')
- gain_grad: float32 [1152], replicated
- scalars: float32 [3], replicated
Inputs may be any that keep to these rules, and one draw needn't show every extreme that they name: `caption_ids`: caption ids never fall along the rows and every caption 0 .. 2047 has at least one row; the captions of the pairs of device d (ids 8 d to 8 (d + 1) - 1) all begin within the 256 rows of device d; the rows of device d before its first caption all belong to the last caption of device d - 1; device 0 begins with caption 0. `groups`: group ids of the pairs; equal ids mark matching pairs.
All inputs are finite; a program needn't handle non-finite values.
Results may differ from a plain program's by a relative error of at most 0.005.
Values may be sent and summed in bfloat16 or wider, within the bound.
No kernel may reach another device: no remote copies, remote signals or barrier semaphores. Data moves between devices by JAX's collectives and lax.ppermute only.
A program may use at most 64 MiB of HBM per device.

v0:
```python
import jax
import jax.numpy as jnp
from jax import lax
from jax.sharding import Mesh
from jax.sharding import PartitionSpec as P

DP = ("dp_0", "dp_1", "dp_2", "dp_3")


def from_behind(value, axis, by):
    count = lax.axis_size(axis)
    pairs = [(i, i + by) for i in range(count) if 0 <= i + by < count]
    return lax.ppermute(value, axis, pairs)


def side_by_side(arrays, axis, dim, along):
    ends, at = ([], 0)
    for a in arrays[:-1]:
        at += a.shape[along]
        ends.append(at)
    both = jnp.concatenate(arrays, axis=along)
    return tuple(jnp.split(lax.all_gather(both, axis, axis=dim, tiled=True), ends, axis=along))


def over_axes(value, axes):
    for axis in axes:
        value = lax.psum(value, axis)
    return value


def unit_rows(values):
    length = jnp.sqrt(jnp.sum(values * values, axis=1, keepdims=True))
    return (values / length, length)


def pair_margin(scaled, bias_value, row_groups, column_groups):
    labels = jnp.where(row_groups[:, None] == column_groups[None, :], 1.0, -1.0).astype(jnp.float32)
    margin = -labels * (scaled + bias_value)
    coeffs = -labels * jax.nn.sigmoid(margin)
    return (margin, coeffs)


def per_device(image_emb, text_tokens, caption_ids, groups, text_gain, log_scale, logit_bias):
    pairs_here = image_emb.shape[0]
    width_features = image_emb.shape[1]
    devices = lax.axis_size(DP)
    total_pairs = pairs_here * devices
    first_pair = lax.axis_index(DP) * pairs_here
    raw_image = image_emb.astype(jnp.float32)
    unit_image, image_norm = unit_rows(raw_image)
    image_low = unit_image.astype(jnp.bfloat16)
    local_ids = caption_ids - first_pair
    slot_index = lax.broadcasted_iota(jnp.int32, (1, pairs_here), 1)
    member = (local_ids[:, None] == slot_index).astype(jnp.bfloat16)
    pooled = lax.dot_general(
        member, text_tokens, (((0,), (0,)), ((), ())), preferred_element_type=jnp.float32
    )
    spilled = (local_ids == -1).astype(jnp.bfloat16)[None, :]
    spill_part = jnp.dot(spilled, text_tokens, preferred_element_type=jnp.float32)
    arrived = from_behind(spill_part, DP, -1)
    pooled = pooled.at[pairs_here - 1].add(arrived[0])
    embedded = pooled * text_gain[None, :]
    unit_text, text_norm = unit_rows(embedded)
    text_low = unit_text.astype(jnp.bfloat16)
    all_groups = lax.all_gather(groups, DP, axis=0, tiled=True)
    scale_value = jnp.exp(log_scale[0])
    bias_value = logit_bias[0]
    stored_width = 0
    initial = (
        jnp.zeros((pairs_here, width_features), jnp.float32),
        jnp.zeros((3,), jnp.float32),
        jnp.zeros((pairs_here, stored_width), jnp.bfloat16),
        jnp.zeros((pairs_here, width_features), jnp.float32),
    )
    block_rows, block_images = side_by_side((text_low, image_low), DP, 0, 1)
    scaled = scale_value * lax.dot_general(
        image_low, block_rows, (((1,), (1,)), ((), ())), preferred_element_type=jnp.float32
    )
    margin, coeffs = pair_margin(scaled, bias_value, groups, all_groups)
    coeff_low = coeffs.astype(jnp.bfloat16)
    image_acc = jnp.dot(coeff_low, block_rows, preferred_element_type=jnp.float32)
    sum_terms = jnp.stack(
        [jnp.sum(jax.nn.softplus(margin)), jnp.sum(coeffs * scaled), jnp.sum(coeffs)]
    )
    stored = initial[2]
    back_scaled = scale_value * lax.dot_general(
        block_images, text_low, (((1,), (1,)), ((), ())), preferred_element_type=jnp.float32
    )
    back_margin, back_coeffs = pair_margin(back_scaled, bias_value, all_groups, groups)
    back_low = back_coeffs.astype(jnp.bfloat16)
    carried = lax.dot_general(
        back_low, block_images, (((0,), (0,)), ((), ())), preferred_element_type=jnp.float32
    )
    image_acc, sum_terms, stored, carried = (image_acc, sum_terms, stored, carried)
    image_unit_grad = scale_value * image_acc
    text_unit_grad = scale_value * carried
    image_grad = (
        image_unit_grad - unit_image * jnp.sum(unit_image * image_unit_grad, axis=1, keepdims=True)
    ) / image_norm
    embed_grad = (
        text_unit_grad - unit_text * jnp.sum(unit_text * text_unit_grad, axis=1, keepdims=True)
    ) / text_norm
    gain_part = jnp.sum(embed_grad * pooled, axis=0)
    pooled_grad = embed_grad * text_gain[None, :]
    behind = from_behind(pooled_grad[pairs_here - 1 :], DP, 1)
    grad_table = jnp.concatenate([behind, pooled_grad], axis=0)
    token_grad = jnp.take(grad_table, local_ids + 1, axis=0)
    sum_terms, gain_grad = (over_axes(sum_terms, DP), over_axes(gain_part, DP))
    scalars = sum_terms / float(total_pairs * total_pairs)
    return (image_grad, token_grad, gain_grad, scalars)


def solution(mesh):
    finer = Mesh(mesh.devices.reshape(4, 4, 8, 2), ("dp_0", "dp_1", "dp_2", "dp_3"))
    placed = (P(DP, None), P(DP, None), P(DP), P(DP), P(), P(), P())
    return jax.shard_map(
        per_device,
        mesh=finer,
        in_specs=placed,
        out_specs=(P(DP, None), P(DP, None), P(), P()),
        check_vma=False,
    )
```

profile of v0, /device:TPU:8, one launch (start us, length us, event | category | flops | bytes accessed | tf_op | source)
XLA Modules:
  0.0 207.0 jit_solution(15179221970684075022)
XLA Ops:
  7.2 0.0 copy-start
  7.2 0.0 all-gather.2.cloned.1.call-start
  7.2 0.7 compare_and_fusion
  8.0 0.3 copy-done
  8.3 0.2 fusion.67
  8.4 9.3 %collective-permute-start = (f32[1,1152]{1,0:T(1,128)S(1)}, f32[1,1152]{1,0:T(1,128)S(1)}, u32[]{:S(2)}, u32[]{:S(2)}) collective-permute-start(f32[1,1152]{1,0:T(1,128)S(1)} %fusion.67), channel_id=1, source_target_pairs={{1,0},{2,1},{3,2},{4,3},{5,4},{6,5},{7,6},{8,7},{9,8},{10,9},{11,1... | collective-permute-start | bytes 13832 | tf_op jit(solution)/shard_map/ppermute | solution.py:13
  17.7 0.3 fusion.55
  18.0 0.9 fusion.58
  18.9 0.1 collective-permute-done
  19.1 0.1 scatter-add.4
  19.2 0.8 multiply_reduce_fusion.4
  20.0 0.8 fusion.62
  20.8 0.6 pad_maximum_fusion.1
  21.4 0.0 all-gather.2.cloned.1.call-update
  22.8 0.9 dynamic-update-slice.3
  23.7 77.3 %all-reduce = s32[2048]{0:T(1024)S(1)} all-reduce(s32[2048]{0:T(1024)S(1)} %dynamic-update-slice.3), channel_id=1, replica_groups=mesh['dp_0'=4,'dp_1'=4,'dp_2'=8,'dp_3'=2] {'dp_0','dp_1','dp_2','dp_3'}, use_global_device_ids=true, to_apply=%add | all-reduce | flops 2048 | bytes 16384
  101.0 38.2 %all-gather.2.cloned.1.call-done = bf16[2048,2304]{1,0:T(8,128)(2,1)} async-done(((bf16[8,2304]{1,0:T(8,128)(2,1)}), bf16[2048,2304]{1,0:T(8,128)(2,1)}) %all-gather.2.cloned.1.call-update) | async-done | bytes 9437200 | tf_op jit(solution)/shard_map/all_gather | solution.py:22
  139.3 6.7 %multiply_reduce_fusion.2 = (f32[8]{0:T(128)S(1)}, f32[8,1152]{1,0:T(8,128)S(1)}) fusion(f32[8]{0:T(128)S(1)} %sqrt.17, f32[8,1152]{1,0:T(8,128)S(1)} %scatter-add.4, f32[1152]{0:T(1024)} %param.13, bf16[2048,2304]{1,0:T(8,128)(2,1)} %all-gather.2.cloned.1.call-done, bf16[8,1152]{1,0:T(8,128)(2,1)S(1)} %get-tuple-element.37, f32[]{:T(128)} %bitcast.11, ...), kind=kOutput, calls=%fused_computation.47 | convolution fusion | flops 75723768 | bytes 9547840 | tf_op jit(solution)/shard_map/dot_general | solution.py:91
  146.0 0.1 multiply_reduce_fusion.1
  146.1 2.2 %collective-permute-start.1 = (f32[1,1152]{1,0:T(1,128)S(1)}, f32[1,1152]{1,0:T(1,128)S(1)}, u32[]{:S(2)}, u32[]{:S(2)}) collective-permute-start(f32[1,1152]{1,0:T(1,128)S(1)} %slice.25), channel_id=1, source_target_pairs={{0,1},{1,2},{2,3},{3,4},{4,5},{5,6},{6,7},{7,8},{8,9},{9,10},{10,1... | collective-permute-start | bytes 13832 | tf_op jit(solution)/shard_map/ppermute | solution.py:13
  148.3 4.4 %fusion.56 = (f32[]{:T(128)}, f32[]{:T(128)}, f32[]{:T(128)}, f32[8,2048]{1,0:T(8,128)S(1)}) fusion(f32[]{:T(128)} %bitcast.12, s32[2048]{0:T(1024)S(1)} %all-reduce, s32[8]{0:T(128)S(1)} %copy-done.3, bf16[8,1152]{1,0:T(8,128)(2,1)S(1)} %get-tuple-element.36, bf16[2048,2304]{1,0:T(8,128)(2,1)} %all-gather.2.cloned.1.call-done, f32[]{:T(128)} %bitcast), kind=kOutput, calls=%fused_computation.35 | convolution fusion | flops 38076416 | bytes 4811820 | tf_op jit(solution)/shard_map/dot_general | solution.py:76
  152.7 3.2 %multiply_reduce_fusion.3 = (f32[8]{0:T(128)S(1)}, f32[8,1152]{1,0:T(8,128)S(1)}) fusion(f32[8]{0:T(128)S(1)} %sqrt.16, bf16[8,1152]{1,0:T(8,128)(2,1)S(1)} %copy-done.1, bf16[2048,2304]{1,0:T(8,128)(2,1)} %all-gather.2.cloned.1.call-done, f32[8,2048]{1,0:T(8,128)S(1)} %get-tuple-element.35, f32[]{:T(128)} %bitcast.10, s32[2048]{0:T(1024)S(1)} %all-reduce, ...), kind=kOutput, calls=%fused_computation.49 | convolution fusion | flops 37958648 | bytes 4848736 | tf_op jit(solution)/shard_map/dot_general | solution.py:81
  155.9 0.7 subtract_divide_fusion.1
  156.6 2.0 pad_maximum_fusion.2
  158.6 8.9 %all-reduce.3 = (f32[1152]{0:T(1024)S(1)}, f32[3]{0:T(128)S(1)}) all-reduce(f32[1152]{0:T(1024)S(1)} %get-tuple-element.29, f32[3]{0:T(128)S(1)} %pad_maximum_fusion.2), channel_id=1, replica_groups=mesh['dp_0'=4,'dp_1'=4,'dp_2'=8,'dp_3'=2] {'dp_0'}, use_global_device_ids=true, to_apply=%region_5.6 | all-reduce | flops 1155 | bytes 9240 | tf_op jit(solution)/shard_map/psum | solution.py:27
  167.5 10.4 %all-reduce.2 = (f32[1152]{0:T(1024)S(1)}, f32[3]{0:T(128)S(1)}) all-reduce(f32[1152]{0:T(1024)S(1)} %get-tuple-element.23, f32[3]{0:T(128)S(1)} %get-tuple-element.24), channel_id=1, replica_groups=mesh['dp_0'=4,'dp_1'=4,'dp_2'=8,'dp_3'=2] {'dp_1'}, use_global_device_ids=true, to_apply=%region_6.7 | all-reduce | flops 1155 | bytes 9240 | tf_op jit(solution)/shard_map/psum | solution.py:27
  177.9 16.2 %all-reduce.1 = (f32[1152]{0:T(1024)S(1)}, f32[3]{0:T(128)S(1)}) all-reduce(f32[1152]{0:T(1024)S(1)} %get-tuple-element.21, f32[3]{0:T(128)S(1)} %get-tuple-element.22), channel_id=1, replica_groups=mesh['dp_0'=4,'dp_1'=4,'dp_2'=8,'dp_3'=2] {'dp_2'}, use_global_device_ids=true, to_apply=%region_7.8 | all-reduce | flops 1155 | bytes 9240 | tf_op jit(solution)/shard_map/psum | solution.py:27
  194.1 3.1 %all-reduce.4 = (f32[1152]{0:T(1024)}, f32[3]{0:T(128)S(1)}) all-reduce(f32[1152]{0:T(1024)S(1)} %get-tuple-element.19, f32[3]{0:T(128)S(1)} %get-tuple-element.20), channel_id=1, replica_groups=mesh['dp_0'=4,'dp_1'=4,'dp_2'=8,'dp_3'=2] {'dp_3'}, use_global_device_ids=true, to_apply=%region_8.9 | all-reduce | flops 1155 | bytes 9240 | tf_op jit(solution)/shard_map/psum | solution.py:27
  197.2 0.5 broadcast_multiply_fusion.1
  197.7 0.0 collective-permute-done.1
  197.8 1.2 gather_fusion
  199.0 1.2 broadcast_select_fusion
  (16 shorter events, 0.1 us)
Async XLA Ops:
  7.2 1.1 copy-start
  7.2 132.1 %all-gather.2.cloned.1.call-start = ((), (), s32[]{:S(2)}) async-start(), calls=%async_computation | async-start | bytes 9474048 | tf_op jit(solution)/shard_map/all_gather | solution.py:22
  8.4 10.6 %collective-permute-start = (f32[1,1152]{1,0:T(1,128)S(1)}, f32[1,1152]{1,0:T(1,128)S(1)}, u32[]{:S(2)}, u32[]{:S(2)}) collective-permute-start(f32[1,1152]{1,0:T(1,128)S(1)} %fusion.67), channel_id=1, source_target_pairs={{1,0},{2,1},{3,2},{4,3},{5,4},{6,5},{7,6},{8,7},{9,8},{10,9},{11,1... | collective-permute-start | bytes 13832 | tf_op jit(solution)/shard_map/ppermute | solution.py:13
  139.3 6.7 %copy-start.2 = (f32[1152]{0:T(1024)S(1)}, f32[1152]{0:T(1024)}, u32[]{:S(2)}) copy-start(f32[1152]{0:T(1024)} %param.13) | copy-start | bytes 13828
  139.3 9.0 %copy-start.3 = (s32[8]{0:T(128)S(1)}, s32[8]{0:T(128)}, u32[]{:S(2)}) copy-start(s32[8]{0:T(128)} %param.12) | copy-start | bytes 100
  146.0 6.7 %copy-start.1 = (bf16[8,1152]{1,0:T(8,128)(2,1)S(1)}, bf16[8,1152]{1,0:T(8,128)(2,1)}, u32[]{:S(2)}) copy-start(bf16[8,1152]{1,0:T(8,128)(2,1)} %param.9) | copy-start | bytes 55300
  146.1 51.6 %collective-permute-start.1 = (f32[1,1152]{1,0:T(1,128)S(1)}, f32[1,1152]{1,0:T(1,128)S(1)}, u32[]{:S(2)}, u32[]{:S(2)}) collective-permute-start(f32[1,1152]{1,0:T(1,128)S(1)} %slice.25), channel_id=1, source_target_pairs={{0,1},{1,2},{2,3},{3,4},{4,5},{5,6},{6,7},{7,8},{8,9},{9,10},{10,1... | collective-permute-start | bytes 13832 | tf_op jit(solution)/shard_map/ppermute | solution.py:13
Sparse Core Ops, SparseCore 0:
  21.6 117.6 all-gather.1
where the time goes:
time: 209 us; the launch traced here: 207 us
  blocking collectives  116 us (56%)
  waiting for transfers between devices  38.4 us (18%)
  between operations  15.5 us (7%)
  matrix products  14.8 us (7%)
  starting transfers between devices  11.5 us (6%)
  other arithmetic  8.39 us (4%)
  local copies, waits for them, and re-layouts  2.51 us (1%)
    unnamed x1, blocking collectives  77.3 us
    psum x4, blocking collectives, over_axes(): value = lax.psum(value, axis)  38.6 us
    all_gather x1, waiting for transfers between devices, side_by_side(): lax.all_gather(both, axis, axis=dim, tiled=True)  38.2 us
    ppermute x2, starting transfers between devices, from_behind(): return lax.ppermute(value, axis, pairs)  11.4 us
    dot_general x1, matrix products, per_device(): lax.dot_general(back_low, block_images, (((0,), (0,)), ((), ())), preferr...  6.7 us
    dot_general x1, matrix products, per_device(): lax.dot_general(image_low, block_rows, (((1,), (1,)), ((), ())), preferre...  4.38 us
  transfers between devices with their start and end apart: 3, of which 2 were waited for; matrix products, arithmetic and copies ran while one was open for 6% of the time, Pallas kernels for 0%

commit v1 on v0

v1 whole, which is shorter than its diff:
```python
import jax
import jax.numpy as jnp
from jax import lax
from jax.sharding import Mesh
from jax.sharding import PartitionSpec as P

Y, X, Z, C = ("dp_0", "dp_1", "dp_2", "dp_3")
DP = (Y, X, Z, C)
PLANE = (Y, X)
LANES = 128


def from_behind(value, by):
    count = lax.axis_size(DP)
    pairs = [(i, i + by) for i in range(count) if 0 <= i + by < count]
    return lax.ppermute(value, DP, pairs)


def exchange(value, axis, bit):
    return lax.ppermute(value, axis, [(i, i ^ bit) for i in range(lax.axis_size(axis))])


STEPS = ((Z, 4), (Z, 2), (Z, 1), (C, 1))


def unit_rows(values):
    length = jnp.sqrt(jnp.sum(values * values, axis=1, keepdims=True))
    return (values / length, length)


def to_plane(blocks):
    return lax.all_to_all(blocks, PLANE, 0, 0, tiled=True)


def per_device(image_emb, text_tokens, caption_ids, groups, text_gain, log_scale, logit_bias):
    f32, bf16 = jnp.float32, jnp.bfloat16
    pairs_here, width = image_emb.shape
    total_pairs = pairs_here * lax.axis_size(DP)
    plane = lax.axis_size(PLANE)
    first_pair = lax.axis_index(DP) * pairs_here
    scale_value = jnp.exp(log_scale[0])
    bias_value = logit_bias[0]

    lane = lax.broadcasted_iota(jnp.int32, (pairs_here, LANES), 1)
    id_lanes = jnp.where(
        lane == 0, (groups >> 8)[:, None], jnp.where(lane == 1, (groups & 255)[:, None], 0)
    ).astype(bf16)

    unit_image, image_norm = unit_rows(image_emb.astype(f32))
    images = jnp.concatenate([unit_image.astype(bf16), id_lanes], axis=1)
    for axis, bit in STEPS:
        images = jnp.concatenate([images, exchange(images, axis, bit)], axis=0)

    local_ids = caption_ids - first_pair
    slot = lax.broadcasted_iota(jnp.int32, (2 * pairs_here, 1), 0)
    wanted = jnp.where(slot < pairs_here, slot, jnp.where(slot == pairs_here, -1, -2))
    member = (local_ids[None, :] == wanted).astype(bf16)
    sums = jnp.dot(member, text_tokens, preferred_element_type=f32)
    arrived = from_behind(sums[pairs_here : pairs_here + 1], -1)
    last = lax.broadcasted_iota(jnp.int32, (pairs_here, 1), 0) == pairs_here - 1
    pooled = sums[:pairs_here] + jnp.where(last, arrived, 0.0)
    unit_text, text_norm = unit_rows(pooled * text_gain[None, :])
    text_rows = jnp.concatenate([unit_text.astype(bf16), id_lanes], axis=1)
    texts = to_plane(jnp.broadcast_to(text_rows[None], (plane,) + text_rows.shape))
    texts = texts.reshape(plane * pairs_here, width + LANES)

    image_low, text_low = images[:, :width], texts[:, :width]
    image_ids = images[:, width].astype(f32) * 256.0 + images[:, width + 1].astype(f32)
    text_ids = texts[:, width].astype(f32) * 256.0 + texts[:, width + 1].astype(f32)

    scaled = scale_value * lax.dot_general(
        image_low, text_low, (((1,), (1,)), ((), ())), preferred_element_type=f32
    )
    labels = jnp.where(image_ids[:, None] == text_ids[None, :], 1.0, -1.0).astype(f32)
    margin = -labels * (scaled + bias_value)
    coeffs = -labels * jax.nn.sigmoid(margin)
    sum_terms = jnp.stack(
        [jnp.sum(jax.nn.softplus(margin)), jnp.sum(coeffs * scaled), jnp.sum(coeffs)]
    )
    coeff_low = coeffs.astype(bf16)
    image_part = scale_value * jnp.dot(coeff_low, text_low, preferred_element_type=f32)
    text_part = scale_value * lax.dot_general(
        coeff_low, image_low, (((0,), (0,)), ((), ())), preferred_element_type=f32
    )

    text_back = to_plane(text_part.astype(bf16).reshape(plane, pairs_here, width))
    text_unit_grad = jnp.sum(text_back.astype(f32), axis=0)

    unit = text_low.astype(f32)
    along = jnp.sum(unit * text_part, axis=1, keepdims=True)
    gain_terms = jnp.sum((text_part - unit * along) * unit, axis=0) / text_gain
    totals = jnp.concatenate([gain_terms, sum_terms, jnp.zeros((LANES - 3,), f32)])[None]
    for axis, bit in reversed(STEPS):
        half = image_part.shape[0] // 2
        image_part = image_part[:half] + exchange(
            image_part[half:].astype(bf16), axis, bit
        ).astype(f32)
        totals = totals + exchange(totals, axis, bit)
    totals = jnp.sum(to_plane(jnp.broadcast_to(totals[None], (plane,) + totals.shape)), axis=0)[0]

    image_grad = (
        image_part - unit_image * jnp.sum(unit_image * image_part, axis=1, keepdims=True)
    ) / image_norm
    embed_grad = (
        text_unit_grad - unit_text * jnp.sum(unit_text * text_unit_grad, axis=1, keepdims=True)
    ) / text_norm
    pooled_grad = embed_grad * text_gain[None, :]
    behind = from_behind(pooled_grad[pairs_here - 1 :], 1)
    table = jnp.concatenate(
        [pooled_grad, behind, jnp.zeros((pairs_here - 1, width), f32)], axis=0
    )
    high = lax.reduce_precision(table, 8, 7)
    low = table - high
    parts = jnp.concatenate([high.astype(bf16), low.astype(bf16)], axis=0)
    token_grad = lax.dot_general(
        jnp.concatenate([member, member], axis=0),
        parts,
        (((0,), (0,)), ((), ())),
        preferred_element_type=f32,
    )
    gain_grad = totals[:width]
    scalars = totals[width : width + 3] / float(total_pairs * total_pairs)
    return (image_grad, token_grad, gain_grad, scalars)


def solution(mesh):
    finer = Mesh(mesh.devices.reshape(4, 4, 8, 2), DP)
    placed = (P(DP, None), P(DP, None), P(DP), P(DP), P(), P(), P())
    return jax.shard_map(
        per_device,
        mesh=finer,
        in_specs=placed,
        out_specs=(P(DP, None), P(DP, None), P(), P()),
        check_vma=False,
    )
```

time: 209 us -> 101 us (0.48)
  blocking collectives: 116 us -> 0 us
  starting transfers between devices: 11.5 us -> 49.9 us
  between operations: 15.5 us -> 2.21 us
  matrix products: 14.8 us -> 3.34 us
  waiting for transfers between devices: 38.4 us -> 33.3 us
    unnamed x1 -> x0, blocking collectives: 77.3 us -> none
    psum x4 -> x0, blocking collectives: 38.6 us -> none  [over_axes(): value = lax.psum(value, axis)]
    all_gather x1 -> x0, waiting for transfers between devices: 38.2 us -> none  [side_by_side(): lax.all_gather(both, axis, axis=dim, tiled=True)]
    ppermute x2 -> x14, waiting for transfers between devices: 0.15 us -> 27.2 us  [the longest x12 22.7 us: exchange(): lax.ppermute(value, axis, [(i, i ^ bit) for i in range(lax.axis_size(axis...]
    all_to_all x0 -> x3, starting transfers between devices: none -> 19.5 us  [to_plane(): return lax.all_to_all(blocks, PLANE, 0, 0, tiled=True)]
    ppermute x2 -> x14, starting transfers between devices: 11.4 us -> 30.4 us  [the longest x12 19.2 us: exchange(): lax.ppermute(value, axis, [(i, i ^ bit) for i in range(lax.axis_size(axis...]
    dot_general x5, matrix products: 14.8 us -> 3.34 us  [the longest x1 1.38 us: per_device(): lax.dot_general(jnp.concatenate([member, member], axis=0), parts, (((0,),...]
    all_to_all x0 -> x3, waiting for transfers between devices: none -> 6.12 us  [to_plane(): return lax.all_to_all(blocks, PLANE, 0, 0, tiled=True)]
  transfers between devices with their start and end apart: 3 -> 17, of which waited for: 2 -> 12; matrix products, arithmetic and copies ran while one was open for 6% -> 6% of each run, Pallas kernels for 0% -> 0%
where the time goes in v1:
time: 101 us
  starting transfers between devices  49.9 us (49%)
  waiting for transfers between devices  33.3 us (33%)
  other arithmetic  7.39 us (7%)
  local copies, waits for them, and re-layouts  4.5 us (4%)
  matrix products  3.34 us (3%)
  between operations  2.21 us (2%)
    ppermute x12, waiting for transfers between devices, exchange(): lax.ppermute(value, axis, [(i, i ^ bit) for i in range(lax.axis_size(axis...  22.7 us
    all_to_all x3, starting transfers between devices, to_plane(): return lax.all_to_all(blocks, PLANE, 0, 0, tiled=True)  19.5 us
    ppermute x12, starting transfers between devices, exchange(): lax.ppermute(value, axis, [(i, i ^ bit) for i in range(lax.axis_size(axis...  19.2 us
    ppermute x2, starting transfers between devices, from_behind(): return lax.ppermute(value, DP, pairs)  11.2 us
    all_to_all x3, waiting for transfers between devices, to_plane(): return lax.all_to_all(blocks, PLANE, 0, 0, tiled=True)  6.12 us
    ppermute x2, waiting for transfers between devices, from_behind(): return lax.ppermute(value, DP, pairs)  4.5 us
  transfers between devices with their start and end apart: 17, of which 12 were waited for; matrix products, arithmetic and copies ran while one was open for 6% of the time, Pallas kernels for 0%

profile of v1, /device:TPU:8, one launch (start us, length us, event | category | flops | bytes accessed | tf_op | source)
XLA Modules:
  0.0 100.7 jit_solution(8809873525512956713)
XLA Ops:
  1.9 9.3 %collective-permute-start.4 = (f32[1,1152]{1,0:T(1,128)S(1)}, f32[1,1152]{1,0:T(1,128)S(1)}, u32[]{:S(2)}, u32[]{:S(2)}) collective-permute-start(f32[1,1152]{1,0:T(1,128)S(1)} %slice.88), channel_id=1, source_target_pairs={{1,0},{2,1},{3,2},{4,3},{5,4},{6,5},{7,6},{8,7},{9,8},{10,9},{11,1... | collective-permute-start | bytes 13832 | tf_op jit(solution)/shard_map/ppermute | solution.py:16
  11.3 0.8 fusion.13
  12.9 0.9 multiply_reduce_fusion.3
  13.8 0.8 fusion.27
  16.8 7.2 %all-to-all-start = ((bf16[16,8,1280]{2,1,0:T(8,128)(2,1)}), bf16[16,8,1280]{2,1,0:T(8,128)(2,1)S(1)}, u32[]{:S(2)}, u32[]{:S(2)}) async-start(bf16[16,8,1280]{2,1,0:T(8,128)(2,1)} %broadcast_in_dim.99), calls=%async_computation | async-start | bytes 655360 | tf_op jit(solution)/shard_map/all_to_all | solution.py:32
  24.0 2.0 %collective-permute-start.1 = (bf16[16,1280]{1,0:T(8,128)(2,1)S(1)}, bf16[16,1280]{1,0:T(8,128)(2,1)S(1)}, u32[]{:S(2)}, u32[]{:S(2)}) collective-permute-start(bf16[16,1280]{1,0:T(8,128)(2,1)S(1)} %pad_maximum_fusion.2), channel_id=1, source_target_pairs={{0,4},{2,6},{4,0},{6,2},{8,12},{10,14},{12,8},{14,10},{1,5},{3,7},... | collective-permute-start | bytes 122888 | tf_op jit(solution)/shard_map/ppermute | solution.py:20
  26.0 3.0 %collective-permute-done.1 = bf16[16,1280]{1,0:T(8,128)(2,1)S(1)} collective-permute-done((bf16[16,1280]{1,0:T(8,128)(2,1)S(1)}, bf16[16,1280]{1,0:T(8,128)(2,1)S(1)}, u32[]{:S(2)}, u32[]{:S(2)}) %collective-permute-start.1) | collective-permute-done | bytes 40992 | tf_op jit(solution)/shard_map/ppermute | solution.py:20
  29.0 1.5 %collective-permute-start.2 = (bf16[32,1280]{1,0:T(8,128)(2,1)S(1)}, bf16[32,1280]{1,0:T(8,128)(2,1)S(1)}, u32[]{:S(2)}, u32[]{:S(2)}) collective-permute-start(bf16[32,1280]{1,0:T(8,128)(2,1)S(1)} %pad_maximum_fusion.1), channel_id=1, source_target_pairs={{0,2},{2,0},{4,6},{6,4},{8,10},{10,8},{12,14},{14,12},{1,3},{3,1},... | collective-permute-start | bytes 245768 | tf_op jit(solution)/shard_map/ppermute | solution.py:20
  30.6 3.2 %collective-permute-done.2 = bf16[32,1280]{1,0:T(8,128)(2,1)S(1)} collective-permute-done((bf16[32,1280]{1,0:T(8,128)(2,1)S(1)}, bf16[32,1280]{1,0:T(8,128)(2,1)S(1)}, u32[]{:S(2)}, u32[]{:S(2)}) %collective-permute-start.2) | collective-permute-done | bytes 81952 | tf_op jit(solution)/shard_map/ppermute | solution.py:20
  34.6 0.8 collective-permute-done.3
  35.6 1.0 fusion.26
  37.0 0.9 fusion.2
  38.0 2.0 %concatenate.46 = f32[1280]{0:T(1024)S(1)} concatenate(f32[1152]{0:T(1024)S(1)} %div.46, f32[1]{0:T(128)} %bitcast.4, f32[1]{0:T(128)} %bitcast.5, f32[1]{0:T(128)} %bitcast.6, f32[125]{0:T(128)S(1)} %broadcast_in_dim.103), dimensions={0} | concatenate | bytes 10240 | tf_op jit(solution)/shard_map/concatenate | solution.py:92
  40.4 0.8 collective-permute-done.10
  41.2 1.6 %collective-permute-start.11 = (f32[1,1280]{1,0:T(1,128)S(1)}, f32[1,1280]{1,0:T(1,128)S(1)}, u32[]{:S(2)}, u32[]{:S(2)}) collective-permute-start(f32[1,1280]{1,0:T(1,128)S(1)} %reshape_add_fusion), channel_id=1, source_target_pairs={{0,2},{2,0},{4,6},{6,4},{8,10},{10,8},{12,14},{14,12},{1,3},{3,1},... | collective-permute-start | bytes 15368 | tf_op jit(solution)/shard_map/ppermute | solution.py:20
  42.8 2.1 %collective-permute-done.11 = f32[1,1280]{1,0:T(1,128)S(1)} collective-permute-done((f32[1,1280]{1,0:T(1,128)S(1)}, f32[1,1280]{1,0:T(1,128)S(1)}, u32[]{:S(2)}, u32[]{:S(2)}) %collective-permute-start.11) | collective-permute-done | bytes 5152 | tf_op jit(solution)/shard_map/ppermute | solution.py:20
  44.9 2.2 %collective-permute-start.12 = (f32[1,1280]{1,0:T(1,128)S(1)}, f32[1,1280]{1,0:T(1,128)S(1)}, u32[]{:S(2)}, u32[]{:S(2)}) collective-permute-start(f32[1,1280]{1,0:T(1,128)S(1)} %add.79), channel_id=1, source_target_pairs={{0,4},{2,6},{4,0},{6,2},{8,12},{10,14},{12,8},{14,10},{1,5},{3,7},... | collective-permute-start | bytes 15368 | tf_op jit(solution)/shard_map/ppermute | solution.py:20
  47.1 2.4 %collective-permute-done.12 = f32[1,1280]{1,0:T(1,128)S(1)} collective-permute-done((f32[1,1280]{1,0:T(1,128)S(1)}, f32[1,1280]{1,0:T(1,128)S(1)}, u32[]{:S(2)}, u32[]{:S(2)}) %collective-permute-start.12) | collective-permute-done | bytes 5152 | tf_op jit(solution)/shard_map/ppermute | solution.py:20
  49.5 3.8 %collective-permute-start.13 = (f32[1,1280]{1,0:T(1,128)S(1)}, f32[1,1280]{1,0:T(1,128)S(1)}, u32[]{:S(2)}, u32[]{:S(2)}) collective-permute-start(f32[1,1280]{1,0:T(1,128)S(1)} %add.80), channel_id=1, source_target_pairs={{0,8},{2,10},{4,12},{6,14},{8,0},{10,2},{12,4},{14,6},{1,9},{3,11}... | collective-permute-start | bytes 15368 | tf_op jit(solution)/shard_map/ppermute | solution.py:20
  53.7 3.4 %collective-permute-done.13 = f32[1,1280]{1,0:T(1,128)S(1)} collective-permute-done((f32[1,1280]{1,0:T(1,128)S(1)}, f32[1,1280]{1,0:T(1,128)S(1)}, u32[]{:S(2)}, u32[]{:S(2)}) %collective-permute-start.13) | collective-permute-done | bytes 5152 | tf_op jit(solution)/shard_map/ppermute | solution.py:20
  57.8 7.4 %all-to-all-start.2 = ((f32[16,1,1280]{2,1,0:T(1,128)}), f32[16,1,1280]{2,1,0:T(1,128)S(1)}, u32[]{:S(2)}, u32[]{:S(2)}) async-start(f32[16,1,1280]{2,1,0:T(1,128)} %broadcast_in_dim.106), calls=%async_computation.2 | async-start | bytes 163840 | tf_op jit(solution)/shard_map/all_to_all | solution.py:32
  65.4 6.1 %all-to-all-done.2 = f32[16,1,1280]{2,1,0:T(1,128)S(1)} async-done(((f32[16,1,1280]{2,1,0:T(1,128)}), f32[16,1,1280]{2,1,0:T(1,128)S(1)}, u32[]{:S(2)}, u32[]{:S(2)}) %all-to-all-start.2) | async-done | bytes 81952 | tf_op jit(solution)/shard_map/all_to_all | solution.py:32
  71.5 4.9 %all-to-all-start.1 = ((bf16[16,8,1152]{2,1,0:T(8,128)(2,1)}), bf16[16,8,1152]{2,1,0:T(8,128)(2,1)S(1)}, u32[]{:S(2)}, u32[]{:S(2)}) async-start(bf16[16,8,1152]{2,1,0:T(8,128)(2,1)} %get-tuple-element.10), calls=%async_computation.1 | async-start | bytes 589824 | tf_op jit(solution)/shard_map/all_to_all | solution.py:32
  76.6 1.3 %collective-permute-start.6 = (bf16[32,1152]{1,0:T(8,128)(2,1)S(1)}, bf16[32,1152]{1,0:T(8,128)(2,1)S(1)}, u32[]{:S(2)}, u32[]{:S(2)}) collective-permute-start(bf16[32,1152]{1,0:T(8,128)(2,1)S(1)} %slice.142), channel_id=1, source_target_pairs={{0,2},{2,0},{4,6},{6,4},{8,10},{10,8},{12,14},{14,12},{1,3},{3,1},... | collective-permute-start | bytes 221192 | tf_op jit(solution)/shard_map/ppermute | solution.py:20
  78.4 2.6 %collective-permute-done.6 = bf16[32,1152]{1,0:T(8,128)(2,1)S(1)} collective-permute-done((bf16[32,1152]{1,0:T(8,128)(2,1)S(1)}, bf16[32,1152]{1,0:T(8,128)(2,1)S(1)}, u32[]{:S(2)}, u32[]{:S(2)}) %collective-permute-start.6) | collective-permute-done | bytes 73760 | tf_op jit(solution)/shard_map/ppermute | solution.py:20
  81.1 2.0 %collective-permute-start.7 = (bf16[16,1152]{1,0:T(8,128)(2,1)S(1)}, bf16[16,1152]{1,0:T(8,128)(2,1)S(1)}, u32[]{:S(2)}, u32[]{:S(2)}) collective-permute-start(bf16[16,1152]{1,0:T(8,128)(2,1)S(1)} %slice.143), channel_id=1, source_target_pairs={{0,4},{2,6},{4,0},{6,2},{8,12},{10,14},{12,8},{14,10},{1,5},{3,7},... | collective-permute-start | bytes 110600 | tf_op jit(solution)/shard_map/ppermute | solution.py:20
  83.7 2.4 %collective-permute-done.7 = bf16[16,1152]{1,0:T(8,128)(2,1)S(1)} collective-permute-done((bf16[16,1152]{1,0:T(8,128)(2,1)S(1)}, bf16[16,1152]{1,0:T(8,128)(2,1)S(1)}, u32[]{:S(2)}, u32[]{:S(2)}) %collective-permute-start.7) | collective-permute-done | bytes 36896 | tf_op jit(solution)/shard_map/ppermute | solution.py:20
  86.1 3.7 %collective-permute-start.8 = (bf16[8,1152]{1,0:T(8,128)(2,1)S(1)}, bf16[8,1152]{1,0:T(8,128)(2,1)S(1)}, u32[]{:S(2)}, u32[]{:S(2)}) collective-permute-start(bf16[8,1152]{1,0:T(8,128)(2,1)S(1)} %slice.144), channel_id=1, source_target_pairs={{0,8},{2,10},{4,12},{6,14},{8,0},{10,2},{12,4},{14,6},{1,9},{3,11}... | collective-permute-start | bytes 55304 | tf_op jit(solution)/shard_map/ppermute | solution.py:20
  90.1 1.9 %collective-permute-start.9 = (f32[1,1152]{1,0:T(1,128)S(1)}, f32[1,1152]{1,0:T(1,128)S(1)}, u32[]{:S(2)}, u32[]{:S(2)}) collective-permute-start(f32[1,1152]{1,0:T(1,128)S(1)} %slice.101), channel_id=1, source_target_pairs={{0,1},{1,2},{2,3},{3,4},{4,5},{5,6},{6,7},{7,8},{8,9},{9,10},{10,1... | collective-permute-start | bytes 13832 | tf_op jit(solution)/shard_map/ppermute | solution.py:16
  92.0 1.8 %collective-permute-done.8 = bf16[8,1152]{1,0:T(8,128)(2,1)S(1)} collective-permute-done((bf16[8,1152]{1,0:T(8,128)(2,1)S(1)}, bf16[8,1152]{1,0:T(8,128)(2,1)S(1)}, u32[]{:S(2)}, u32[]{:S(2)}) %collective-permute-start.8) | collective-permute-done | bytes 18464 | tf_op jit(solution)/shard_map/ppermute | solution.py:20
  94.8 4.5 %collective-permute-done.9 = f32[1,1152]{1,0:T(1,128)S(1)} collective-permute-done((f32[1,1152]{1,0:T(1,128)S(1)}, f32[1,1152]{1,0:T(1,128)S(1)}, u32[]{:S(2)}, u32[]{:S(2)}) %collective-permute-start.9) | collective-permute-done | bytes 4640 | tf_op jit(solution)/shard_map/ppermute | solution.py:16
  99.3 1.4 %fusion.8 = f32[256,1152]{1,0:T(8,128)} fusion(bf16[16,1152]{1,0:T(8,128)(2,1)S(1)} %get-tuple-element.12, bf16[16,1152]{1,0:T(8,128)(2,1)S(1)} %get-tuple-element.11, pred[16,256]{1,0:T(8,128)(4,1)S(1)} %broadcast_compare_fusion), kind=kOutput, calls=%fused_computation.28 | convolution fusion | flops 19030016 | bytes 1257472 | tf_op jit(solution)/shard_map/dot_general | solution.py:115
  (68 shorter events, 8.5 us)
Async XLA Ops:
  0.6 1.1 %copy-start = (bf16[256,1152]{1,0:T(8,128)(2,1)S(1)}, bf16[256,1152]{1,0:T(8,128)(2,1)}, u32[]{:S(2)}) copy-start(bf16[256,1152]{1,0:T(8,128)(2,1)} %param.8) | copy-start | bytes 1769476
  1.9 10.9 %collective-permute-start.4 = (f32[1,1152]{1,0:T(1,128)S(1)}, f32[1,1152]{1,0:T(1,128)S(1)}, u32[]{:S(2)}, u32[]{:S(2)}) collective-permute-start(f32[1,1152]{1,0:T(1,128)S(1)} %slice.88), channel_id=1, source_target_pairs={{1,0},{2,1},{3,2},{4,3},{5,4},{6,5},{7,6},{8,7},{9,8},{10,9},{11,1... | collective-permute-start | bytes 13832 | tf_op jit(solution)/shard_map/ppermute | solution.py:16
  14.6 9.4 %collective-permute-start = (bf16[8,1280]{1,0:T(8,128)(2,1)S(1)}, bf16[8,1280]{1,0:T(8,128)(2,1)S(1)}, u32[]{:S(2)}, u32[]{:S(2)}) collective-permute-start(bf16[8,1280]{1,0:T(8,128)(2,1)S(1)} %get-tuple-element.13), channel_id=1, source_target_pairs={{0,8},{2,10},{4,12},{6,14},{8,0},{10,2},{12,4},{14,6},{1,9},{3,11}... | collective-permute-start | bytes 61448 | tf_op jit(solution)/shard_map/ppermute | solution.py:20
  16.8 17.6 %all-to-all-start = ((bf16[16,8,1280]{2,1,0:T(8,128)(2,1)}), bf16[16,8,1280]{2,1,0:T(8,128)(2,1)S(1)}, u32[]{:S(2)}, u32[]{:S(2)}) async-start(bf16[16,8,1280]{2,1,0:T(8,128)(2,1)} %broadcast_in_dim.99), calls=%async_computation | async-start | bytes 655360 | tf_op jit(solution)/shard_map/all_to_all | solution.py:32
  24.0 5.0 %collective-permute-start.1 = (bf16[16,1280]{1,0:T(8,128)(2,1)S(1)}, bf16[16,1280]{1,0:T(8,128)(2,1)S(1)}, u32[]{:S(2)}, u32[]{:S(2)}) collective-permute-start(bf16[16,1280]{1,0:T(8,128)(2,1)S(1)} %pad_maximum_fusion.2), channel_id=1, source_target_pairs={{0,4},{2,6},{4,0},{6,2},{8,12},{10,14},{12,8},{14,10},{1,5},{3,7},... | collective-permute-start | bytes 122888 | tf_op jit(solution)/shard_map/ppermute | solution.py:20
  29.0 4.8 %collective-permute-start.2 = (bf16[32,1280]{1,0:T(8,128)(2,1)S(1)}, bf16[32,1280]{1,0:T(8,128)(2,1)S(1)}, u32[]{:S(2)}, u32[]{:S(2)}) collective-permute-start(bf16[32,1280]{1,0:T(8,128)(2,1)S(1)} %pad_maximum_fusion.1), channel_id=1, source_target_pairs={{0,2},{2,0},{4,6},{6,4},{8,10},{10,8},{12,14},{14,12},{1,3},{3,1},... | collective-permute-start | bytes 245768 | tf_op jit(solution)/shard_map/ppermute | solution.py:20
  33.8 1.6 %collective-permute-start.3 = (bf16[64,1280]{1,0:T(8,128)(2,1)S(1)}, bf16[64,1280]{1,0:T(8,128)(2,1)S(1)}, u32[]{:S(2)}, u32[]{:S(2)}) collective-permute-start(bf16[64,1280]{1,0:T(8,128)(2,1)S(1)} %pad_maximum_fusion), channel_id=1, source_target_pairs={{0,1},{1,0},{2,3},{3,2},{4,5},{5,4},{6,7},{7,6},{8,9},{9,8},{10,11... | collective-permute-start | bytes 491528 | tf_op jit(solution)/shard_map/ppermute | solution.py:20
  36.6 1.4 %copy-start.2 = (f32[1152]{0:T(1024)S(1)}, f32[1152]{0:T(1024)}, u32[]{:S(2)}) copy-start(f32[1152]{0:T(1024)} %param.11) | copy-start | bytes 13828
  40.0 1.3 %collective-permute-start.10 = (f32[1,1280]{1,0:T(1,128)S(1)}, f32[1,1280]{1,0:T(1,128)S(1)}, u32[]{:S(2)}, u32[]{:S(2)}) collective-permute-start(f32[1,1280]{1,0:T(1,128)S(1)} %broadcast_in_dim.104), channel_id=1, source_target_pairs={{0,1},{1,0},{2,3},{3,2},{4,5},{5,4},{6,7},{7,6},{8,9},{9,8},{10,11... | collective-permute-start | bytes 15368 | tf_op jit(solution)/shard_map/ppermute | solution.py:20
  41.2 3.7 %collective-permute-start.11 = (f32[1,1280]{1,0:T(1,128)S(1)}, f32[1,1280]{1,0:T(1,128)S(1)}, u32[]{:S(2)}, u32[]{:S(2)}) collective-permute-start(f32[1,1280]{1,0:T(1,128)S(1)} %reshape_add_fusion), channel_id=1, source_target_pairs={{0,2},{2,0},{4,6},{6,4},{8,10},{10,8},{12,14},{14,12},{1,3},{3,1},... | collective-permute-start | bytes 15368 | tf_op jit(solution)/shard_map/ppermute | solution.py:20
  44.9 4.6 %collective-permute-start.12 = (f32[1,1280]{1,0:T(1,128)S(1)}, f32[1,1280]{1,0:T(1,128)S(1)}, u32[]{:S(2)}, u32[]{:S(2)}) collective-permute-start(f32[1,1280]{1,0:T(1,128)S(1)} %add.79), channel_id=1, source_target_pairs={{0,4},{2,6},{4,0},{6,2},{8,12},{10,14},{12,8},{14,10},{1,5},{3,7},... | collective-permute-start | bytes 15368 | tf_op jit(solution)/shard_map/ppermute | solution.py:20
  49.5 7.6 %collective-permute-start.13 = (f32[1,1280]{1,0:T(1,128)S(1)}, f32[1,1280]{1,0:T(1,128)S(1)}, u32[]{:S(2)}, u32[]{:S(2)}) collective-permute-start(f32[1,1280]{1,0:T(1,128)S(1)} %add.80), channel_id=1, source_target_pairs={{0,8},{2,10},{4,12},{6,14},{8,0},{10,2},{12,4},{14,6},{1,9},{3,11}... | collective-permute-start | bytes 15368 | tf_op jit(solution)/shard_map/ppermute | solution.py:20
  53.6 22.9 %collective-permute-start.5 = (bf16[64,1152]{1,0:T(8,128)(2,1)S(1)}, bf16[64,1152]{1,0:T(8,128)(2,1)S(1)}, u32[]{:S(2)}, u32[]{:S(2)}) collective-permute-start(bf16[64,1152]{1,0:T(8,128)(2,1)S(1)} %slice.141), channel_id=1, source_target_pairs={{0,1},{1,0},{2,3},{3,2},{4,5},{5,4},{6,7},{7,6},{8,9},{9,8},{10,11... | collective-permute-start | bytes 442376 | tf_op jit(solution)/shard_map/ppermute | solution.py:20
  57.8 13.7 %all-to-all-start.2 = ((f32[16,1,1280]{2,1,0:T(1,128)}), f32[16,1,1280]{2,1,0:T(1,128)S(1)}, u32[]{:S(2)}, u32[]{:S(2)}) async-start(f32[16,1,1280]{2,1,0:T(1,128)} %broadcast_in_dim.106), calls=%async_computation.2 | async-start | bytes 163840 | tf_op jit(solution)/shard_map/all_to_all | solution.py:32
  71.5 18.3 %all-to-all-start.1 = ((bf16[16,8,1152]{2,1,0:T(8,128)(2,1)}), bf16[16,8,1152]{2,1,0:T(8,128)(2,1)S(1)}, u32[]{:S(2)}, u32[]{:S(2)}) async-start(bf16[16,8,1152]{2,1,0:T(8,128)(2,1)} %get-tuple-element.10), calls=%async_computation.1 | async-start | bytes 589824 | tf_op jit(solution)/shard_map/all_to_all | solution.py:32
  76.4 17.4 %copy-start.1 = (bf16[8,1152]{1,0:T(8,128)(2,1)S(1)}, bf16[8,1152]{1,0:T(8,128)(2,1)}, u32[]{:S(2)}) copy-start(bf16[8,1152]{1,0:T(8,128)(2,1)} %param.7) | copy-start | bytes 55300
  76.6 4.4 %collective-permute-start.6 = (bf16[32,1152]{1,0:T(8,128)(2,1)S(1)}, bf16[32,1152]{1,0:T(8,128)(2,1)S(1)}, u32[]{:S(2)}, u32[]{:S(2)}) collective-permute-start(bf16[32,1152]{1,0:T(8,128)(2,1)S(1)} %slice.142), channel_id=1, source_target_pairs={{0,2},{2,0},{4,6},{6,4},{8,10},{10,8},{12,14},{14,12},{1,3},{3,1},... | collective-permute-start | bytes 221192 | tf_op jit(solution)/shard_map/ppermute | solution.py:20
  81.1 5.0 %collective-permute-start.7 = (bf16[16,1152]{1,0:T(8,128)(2,1)S(1)}, bf16[16,1152]{1,0:T(8,128)(2,1)S(1)}, u32[]{:S(2)}, u32[]{:S(2)}) collective-permute-start(bf16[16,1152]{1,0:T(8,128)(2,1)S(1)} %slice.143), channel_id=1, source_target_pairs={{0,4},{2,6},{4,0},{6,2},{8,12},{10,14},{12,8},{14,10},{1,5},{3,7},... | collective-permute-start | bytes 110600 | tf_op jit(solution)/shard_map/ppermute | solution.py:20
  86.1 7.8 %collective-permute-start.8 = (bf16[8,1152]{1,0:T(8,128)(2,1)S(1)}, bf16[8,1152]{1,0:T(8,128)(2,1)S(1)}, u32[]{:S(2)}, u32[]{:S(2)}) collective-permute-start(bf16[8,1152]{1,0:T(8,128)(2,1)S(1)} %slice.144), channel_id=1, source_target_pairs={{0,8},{2,10},{4,12},{6,14},{8,0},{10,2},{12,4},{14,6},{1,9},{3,11}... | collective-permute-start | bytes 55304 | tf_op jit(solution)/shard_map/ppermute | solution.py:20
  90.1 9.2 %collective-permute-start.9 = (f32[1,1152]{1,0:T(1,128)S(1)}, f32[1,1152]{1,0:T(1,128)S(1)}, u32[]{:S(2)}, u32[]{:S(2)}) collective-permute-start(f32[1,1152]{1,0:T(1,128)S(1)} %slice.101), channel_id=1, source_target_pairs={{0,1},{1,2},{2,3},{3,4},{4,5},{5,6},{6,7},{7,8},{8,9},{9,10},{10,1... | collective-permute-start | bytes 13832 | tf_op jit(solution)/shard_map/ppermute | solution.py:16

commit v2 on v1

v2 whole, which is shorter than its diff:
```python
import jax
import jax.numpy as jnp
from jax import lax
from jax.experimental import pallas as pl
from jax.experimental.pallas import tpu as pltpu
from jax.sharding import Mesh
from jax.sharding import PartitionSpec as P

Y, X, Z, C = ("dp_0", "dp_1", "dp_2", "dp_3")
DP = (Y, X, Z, C)
PLANE = (Y, X)
LANES = 128
F32, BF16 = jnp.float32, jnp.bfloat16
SMEM = pl.BlockSpec(memory_space=pltpu.SMEM)
VMEM = pl.BlockSpec(memory_space=pltpu.VMEM)

STEPS = ((Z, 4), (Z, 2), (Z, 1), (C, 1))


def from_behind(value, by):
    count = lax.axis_size(DP)
    pairs = [(i, i + by) for i in range(count) if 0 <= i + by < count]
    return lax.ppermute(value, DP, pairs)


def exchange(value, axis, bit):
    return lax.ppermute(value, axis, [(i, i ^ bit) for i in range(lax.axis_size(axis))])


def to_plane(blocks):
    return lax.all_to_all(blocks, PLANE, 0, 0, tiled=True)


def members(ids, pairs, copies):
    slot = lax.broadcasted_iota(jnp.int32, (2 * pairs * copies, 1), 0) % (2 * pairs)
    last = ids[:, ids.shape[1] - 1 :]
    wanted = jnp.where(slot < pairs, slot - (pairs - 1), jnp.where(slot == pairs, -pairs, 1))
    return (ids - last == wanted).astype(F32).astype(BF16)


def id_tile(groups_ref, pairs, for_text):
    row = lax.broadcasted_iota(jnp.int32, (pairs, LANES), 0)
    lane = lax.broadcasted_iota(jnp.int32, (pairs, LANES), 1)
    ids = jnp.zeros((pairs, LANES), jnp.int32)
    for r in range(pairs):
        ids = jnp.where(row == r, groups_ref[r], ids)
    high, low = (ids >> 8) << 8, ids & 255
    if for_text:
        cells = jnp.where(lane < 2, 1, jnp.where(lane == 2, -high, jnp.where(lane == 3, -low, 0)))
    else:
        cells = jnp.where(lane == 0, high, jnp.where(lane == 1, low, jnp.where(lane < 4, 1, 0)))
    return cells.astype(F32).astype(BF16)


def prepare(groups_ref, ids_ref, image_ref, tokens_ref, row_ref, unit_ref, norm_ref, pooled_ref, spill_ref):
    pairs, width = image_ref.shape
    image = image_ref[...].astype(F32)
    norm = jnp.sqrt(jnp.sum(image * image, axis=1, keepdims=True))
    unit = image / norm
    unit_ref[...] = unit
    norm_ref[...] = norm
    row_ref[:, :width] = unit.astype(BF16)
    row_ref[:, width:] = id_tile(groups_ref, pairs, False)
    sums = jnp.dot(members(ids_ref[...], pairs, 1), tokens_ref[...], preferred_element_type=F32)
    pooled_ref[...] = sums[:pairs]
    spill_ref[...] = sums[pairs : pairs + 1]


def text_rows(groups_ref, pooled_ref, arrived_ref, gain_ref, rows_ref, unit_ref, norm_ref):
    pairs, width = pooled_ref.shape
    last = lax.broadcasted_iota(jnp.int32, (pairs, 1), 0) == pairs - 1
    pooled = pooled_ref[...] + jnp.where(last, arrived_ref[...], 0.0)
    embedded = pooled * gain_ref[...]
    norm = jnp.sqrt(jnp.sum(embedded * embedded, axis=1, keepdims=True))
    unit = embedded / norm
    unit_ref[...] = unit
    norm_ref[...] = norm
    low, ids = unit.astype(BF16), id_tile(groups_ref, pairs, True)
    for k in range(rows_ref.shape[0]):
        rows_ref[k, :, :width] = low
        rows_ref[k, :, width:] = ids


def pair_math(scalars_ref, image_ref, text_ref, gain_ref, text_out, keep_out, send_out):
    width = gain_ref.shape[1]
    scale = jnp.exp(jnp.full((1, LANES), scalars_ref[0], F32))[:, :1]
    image, text = image_ref[:, :width], text_ref[:, :width]
    contract = (((1,), (1,)), ((), ()))
    scaled = scale * lax.dot_general(image, text, contract, preferred_element_type=F32)
    apart = lax.dot_general(
        image_ref[:, width:], text_ref[:, width:], contract, preferred_element_type=F32
    )
    match = apart == 0.0
    logits = scaled + scalars_ref[1]
    margin = jnp.where(match, -logits, logits)
    tail = jnp.exp(-jnp.abs(margin))
    losses = jnp.maximum(margin, 0.0) + jnp.log1p(tail)
    sigmoid = jnp.where(margin >= 0.0, 1.0, tail) / (1.0 + tail)
    coeffs = jnp.where(match, -sigmoid, sigmoid)
    image_part = scale * jnp.dot(coeffs.astype(BF16), text, preferred_element_type=F32)
    text_part = scale * jnp.dot(coeffs.T.astype(BF16), image, preferred_element_type=F32)
    half = keep_out.shape[0]
    keep_out[...] = image_part[:half]
    send_out[...] = image_part[half:].astype(BF16)
    text_out[:, :width] = text_part.astype(BF16)

    unit = text.astype(F32)
    along = jnp.sum(unit * text_part, axis=1, keepdims=True)
    gain_terms = jnp.sum((text_part - unit * along) * unit, axis=0, keepdims=True) / gain_ref[...]
    row = lax.broadcasted_iota(jnp.int32, (8, LANES), 0)
    lane = lax.broadcasted_iota(jnp.int32, (8, LANES), 1)
    first = jnp.zeros((8, LANES), F32)
    for r in range(8):
        first = jnp.where(row == r, gain_terms[:, LANES * r : LANES * (r + 1)], first)
    second = jnp.where(row == 0, gain_terms[:, 8 * LANES : 9 * LANES], 0.0)
    for i, terms in enumerate((losses, coeffs * scaled, coeffs)):
        total = jnp.sum(jnp.sum(terms, axis=0, keepdims=True), axis=1, keepdims=True)
        high = total.astype(BF16).astype(F32)
        second = jnp.where((row == 1) & (lane == i), high, second)
        second = jnp.where((row == 2) & (lane == i), total - high, second)
    packed = jnp.concatenate([first, second], axis=1).astype(BF16)
    for k in range(text_out.shape[0] // 8):
        text_out[8 * k : 8 * (k + 1), width:] = packed


def text_gradient(back_ref, unit_ref, norm_ref, gain_ref, grad_out, last_out, totals_out):
    pairs, width = unit_ref.shape
    total = jnp.sum(back_ref[...].astype(F32), axis=0)
    totals_out[...] = total[:, width:]
    grad, unit = total[:, :width], unit_ref[...]
    grad = grad - unit * jnp.sum(unit * grad, axis=1, keepdims=True)
    grad = grad / norm_ref[...] * gain_ref[...]
    grad_out[...] = grad
    last_out[...] = grad[pairs - 1 :]


def finish(ids_ref, grad_ref, behind_ref, keep_ref, came_ref, unit_ref, norm_ref, token_out, image_out):
    pairs, width = grad_ref.shape
    table = jnp.concatenate(
        [grad_ref[...], jnp.broadcast_to(behind_ref[...], (pairs, width))], axis=0
    )
    high = table.astype(BF16)
    low = (table - high.astype(F32)).astype(BF16)
    token_out[...] = lax.dot_general(
        members(ids_ref[...], pairs, 2),
        jnp.concatenate([high, low], axis=0),
        (((0,), (0,)), ((), ())),
        preferred_element_type=F32,
    )
    grad, unit = keep_ref[...] + came_ref[...].astype(F32), unit_ref[...]
    grad = grad - unit * jnp.sum(unit * grad, axis=1, keepdims=True)
    image_out[...] = grad / norm_ref[...]


def local(kernel, specs, *outs):
    return pl.pallas_call(
        kernel,
        in_specs=specs,
        out_specs=[VMEM] * len(outs),
        out_shape=[jax.ShapeDtypeStruct(*o) for o in outs],
        compiler_params=pltpu.CompilerParams(vmem_limit_bytes=16 << 20),
    )


def per_device(image_emb, text_tokens, caption_ids, groups, text_gain, log_scale, logit_bias):
    pairs, width = image_emb.shape
    total_pairs = pairs * lax.axis_size(DP)
    plane = lax.axis_size(PLANE)
    wide = width + LANES
    ids = caption_ids[None, :]
    gain = text_gain[None, :]
    row, unit_image, image_norm, pooled, spill = local(
        prepare, [SMEM, VMEM, VMEM, VMEM],
        ((pairs, wide), BF16), ((pairs, width), F32), ((pairs, 1), F32), ((pairs, width), F32), ((1, width), F32),
    )(groups, ids, image_emb, text_tokens)

    arrived = from_behind(spill, -1)
    images = row
    for axis, bit in STEPS:
        images = jnp.concatenate([images, exchange(images, axis, bit)], axis=0)

    rows, unit_text, text_norm = local(
        text_rows, [SMEM, VMEM, VMEM, VMEM],
        ((plane, pairs, wide), BF16), ((pairs, width), F32), ((pairs, 1), F32),
    )(groups, pooled, arrived, gain)
    texts = to_plane(rows).reshape(plane * pairs, wide)

    line = images.shape[0]
    text_part, keep, send = local(
        pair_math, [SMEM, VMEM, VMEM, VMEM],
        ((plane * pairs, wide + LANES), BF16), ((line // 2, width), F32), ((line // 2, width), BF16),
    )(jnp.concatenate([log_scale, logit_bias]), images, texts, gain)

    back = to_plane(text_part.reshape(plane, pairs, wide + LANES))
    for n, (axis, bit) in enumerate(reversed(STEPS)):
        came = exchange(send, axis, bit)
        if n + 1 < len(STEPS):
            whole = keep + came.astype(F32)
            half = whole.shape[0] // 2
            keep, send = whole[:half], whole[half:].astype(BF16)

    pooled_grad, last, totals = local(
        text_gradient, [VMEM, VMEM, VMEM, VMEM],
        ((pairs, width), F32), ((1, width), F32), ((pairs, 2 * LANES), F32),
    )(back, unit_text, text_norm, gain)
    behind = from_behind(last, 1)
    for axis, bit in reversed(STEPS):
        totals = totals + exchange(totals, axis, bit)

    token_grad, image_grad = local(
        finish, [VMEM] * 7, ((text_tokens.shape[0], width), F32), ((pairs, width), F32)
    )(ids, pooled_grad, behind, keep, came, unit_image, image_norm)
    gain_grad = jnp.concatenate([totals[:, :LANES].reshape(-1), totals[0, LANES:]])
    scalars = (totals[1, LANES : LANES + 3] + totals[2, LANES : LANES + 3]) / float(
        total_pairs * total_pairs
    )
    return (image_grad, token_grad, gain_grad, scalars)


def solution(mesh):
    finer = Mesh(mesh.devices.reshape(4, 4, 8, 2), DP)
    placed = (P(DP, None), P(DP, None), P(DP), P(DP), P(), P(), P())
    return jax.shard_map(
        per_device,
        mesh=finer,
        in_specs=placed,
        out_specs=(P(DP, None), P(DP, None), P(), P()),
        check_vma=False,
    )
```

time: 101 us -> 80.4 us (0.80)
  starting transfers between devices: 49.9 us -> 39.5 us
  waiting for transfers between devices: 33.3 us -> 27.2 us
  other arithmetic: 7.39 us -> 1.3 us
  Pallas kernels: 0 us -> 5.81 us
  matrix products: 3.34 us -> 0 us
    ppermute x12, waiting for transfers between devices: 22.7 us -> 13.9 us  [exchange(): lax.ppermute(value, axis, [(i, i ^ bit) for i in range(lax.axis_size(axis...]
    pallas_call x0 -> x5, Pallas kernels: none -> 5.81 us  [the longest x1 2.08 us: per_device(): local(pair_math, [SMEM, VMEM, VMEM, VMEM], ((plane * pairs, wide + LANES)...]
    ppermute x12, starting transfers between devices: 19.2 us -> 13.9 us  [exchange(): lax.ppermute(value, axis, [(i, i ^ bit) for i in range(lax.axis_size(axis...]
    all_to_all x3 -> x2, starting transfers between devices: 19.5 us -> 14.4 us  [to_plane(): return lax.all_to_all(blocks, PLANE, 0, 0, tiled=True)]
    dot_general x5 -> x0, matrix products: 3.34 us -> none  [the longest x1 1.38 us: per_device(): lax.dot_general(jnp.concatenate([member, member], axis=0), parts, (((0,),...]
    reduce_sum x7 -> x0, other arithmetic: 3.1 us -> none  [the longest x2 1.74 us: unit_rows(): length = jnp.sqrt(jnp.sum(values * values, axis=1, keepdims=True))]
    unnamed x9 -> x14, local copies, waits for them, and re-layouts: 0.33 us -> 3.14 us
    ppermute x2, waiting for transfers between devices: 4.5 us -> 7.2 us  [from_behind(): return lax.ppermute(value, DP, pairs)]
  transfers between devices with their start and end apart: 17 -> 16, of which waited for: 12 -> 8; matrix products, arithmetic and copies ran while one was open for 6% -> 1% of each run, Pallas kernels for 0% -> 4%
where the time goes in v2:
time: 80.4 us; the launch traced here: 79.8 us
  starting transfers between devices  39.5 us (49%)
  waiting for transfers between devices  27.2 us (34%)
  Pallas kernels  5.81 us (7%)
  local copies, waits for them, and re-layouts  3.88 us (5%)
  between operations  2.1 us (3%)
  other arithmetic  1.3 us (2%)
    all_to_all x2, starting transfers between devices, to_plane(): return lax.all_to_all(blocks, PLANE, 0, 0, tiled=True)  14.4 us
    ppermute x12, waiting for transfers between devices, exchange(): lax.ppermute(value, axis, [(i, i ^ bit) for i in range(lax.axis_size(axis...  13.9 us
    ppermute x12, starting transfers between devices, exchange(): lax.ppermute(value, axis, [(i, i ^ bit) for i in range(lax.axis_size(axis...  13.9 us
    ppermute x2, starting transfers between devices, from_behind(): return lax.ppermute(value, DP, pairs)  11.2 us
    ppermute x2, waiting for transfers between devices, from_behind(): return lax.ppermute(value, DP, pairs)  7.2 us
    all_to_all x2, waiting for transfers between devices, to_plane(): return lax.all_to_all(blocks, PLANE, 0, 0, tiled=True)  6.08 us
    unnamed x14, local copies, waits for them, and re-layouts  3.14 us
    pallas_call x1, Pallas kernels, per_device(): local(pair_math, [SMEM, VMEM, VMEM, VMEM], ((plane * pairs, wide + LANES)...  2.08 us
  transfers between devices with their start and end apart: 16, of which 8 were waited for; matrix products, arithmetic and copies ran while one was open for 1% of the time, Pallas kernels for 4%

profile of v2, /device:TPU:8, one launch (start us, length us, event | category | flops | bytes accessed | tf_op | source)
XLA Modules:
  0.0 79.8 jit_solution(17408359612273984095)
XLA Ops:
  0.6 1.1 %copy-done = bf16[256,1152]{1,0:T(8,128)(2,1)S(1)} copy-done((bf16[256,1152]{1,0:T(8,128)(2,1)S(1)}, bf16[256,1152]{1,0:T(8,128)(2,1)}, u32[]{:S(2)}) %copy-start) | copy-done | bytes 589848
  1.7 0.7 copy-done.1
  2.4 0.7 copy-done.2
  3.1 0.7 copy-done.4
  3.8 0.8 shard_map.102
  4.5 9.3 %collective-permute-start.4 = (f32[1,1152]{1,0:T(1,128)S(1)}, f32[1,1152]{1,0:T(1,128)S(1)}, u32[]{:S(2)}, u32[]{:S(2)}) collective-permute-start(f32[1,1152]{1,0:T(1,128)S(1)} %get-tuple-element.22), channel_id=1, source_target_pairs={{1,0},{2,1},{3,2},{4,3},{5,4},{6,5},{7,6},{8,7},{9,8},{10,9},{11,1... | collective-permute-start | bytes 13832 | tf_op jit(solution)/shard_map/ppermute | solution.py:23
  15.3 0.7 broadcast_in_dim.7.gain_ref
  16.0 1.4 %shard_map.103 = (bf16[16,8,1280]{2,1,0:T(8,128)(2,1)}, f32[8,1152]{1,0:T(8,128)S(1)}, f32[8,1]{1,0:T(8,128)S(1)}) custom-call(s32[8]{0:T(128)S(1)} %copy-done.4, f32[8,1152]{1,0:T(8,128)S(1)} %get-tuple-element.21.pooled_ref, f32[1,1152]{1,0:T(1,128)S(1)} %collective-permute-done.4.arrived_ref, f32[1,1152]{1,0:T(1,128)S(1)} %broadcast_in_dim.7.gain_ref), custom_call_target="tpu_custom_call" | custom-call | tf_op jit(solution)/shard_map/pallas_call | solution.py:182
  17.4 7.2 %all-to-all-start = ((bf16[16,8,1280]{2,1,0:T(8,128)(2,1)}), bf16[16,8,1280]{2,1,0:T(8,128)(2,1)S(1)}, u32[]{:S(2)}, u32[]{:S(2)}) async-start(bf16[16,8,1280]{2,1,0:T(8,128)(2,1)} %get-tuple-element.23), calls=%async_computation | async-start | bytes 655360 | tf_op jit(solution)/shard_map/all_to_all | solution.py:31
  24.6 2.0 %collective-permute-start.1 = (bf16[16,1280]{1,0:T(8,128)(2,1)S(1)}, bf16[16,1280]{1,0:T(8,128)(2,1)S(1)}, u32[]{:S(2)}, u32[]{:S(2)}) collective-permute-start(bf16[16,1280]{1,0:T(8,128)(2,1)S(1)} %pad_maximum_fusion.2), channel_id=1, source_target_pairs={{0,4},{2,6},{4,0},{6,2},{8,12},{10,14},{12,8},{14,10},{1,5},{3,7},... | collective-permute-start | bytes 122888 | tf_op jit(solution)/shard_map/ppermute | solution.py:27
  26.6 3.0 %collective-permute-done.1 = bf16[16,1280]{1,0:T(8,128)(2,1)S(1)} collective-permute-done((bf16[16,1280]{1,0:T(8,128)(2,1)S(1)}, bf16[16,1280]{1,0:T(8,128)(2,1)S(1)}, u32[]{:S(2)}, u32[]{:S(2)}) %collective-permute-start.1) | collective-permute-done | bytes 40992 | tf_op jit(solution)/shard_map/ppermute | solution.py:27
  29.6 1.5 %collective-permute-start.2 = (bf16[32,1280]{1,0:T(8,128)(2,1)S(1)}, bf16[32,1280]{1,0:T(8,128)(2,1)S(1)}, u32[]{:S(2)}, u32[]{:S(2)}) collective-permute-start(bf16[32,1280]{1,0:T(8,128)(2,1)S(1)} %pad_maximum_fusion.1), channel_id=1, source_target_pairs={{0,2},{2,0},{4,6},{6,4},{8,10},{10,8},{12,14},{14,12},{1,3},{3,1},... | collective-permute-start | bytes 245768 | tf_op jit(solution)/shard_map/ppermute | solution.py:27
  31.1 3.0 %collective-permute-done.2 = bf16[32,1280]{1,0:T(8,128)(2,1)S(1)} collective-permute-done((bf16[32,1280]{1,0:T(8,128)(2,1)S(1)}, bf16[32,1280]{1,0:T(8,128)(2,1)S(1)}, u32[]{:S(2)}, u32[]{:S(2)}) %collective-permute-start.2) | collective-permute-done | bytes 81952 | tf_op jit(solution)/shard_map/ppermute | solution.py:27
  34.2 1.4 %collective-permute-done.3 = bf16[64,1280]{1,0:T(8,128)(2,1)S(1)} collective-permute-done((bf16[64,1280]{1,0:T(8,128)(2,1)S(1)}, bf16[64,1280]{1,0:T(8,128)(2,1)S(1)}, u32[]{:S(2)}, u32[]{:S(2)}) %collective-permute-start.3) | collective-permute-done | bytes 163872 | tf_op jit(solution)/shard_map/ppermute | solution.py:27
  35.6 2.1 %shard_map.104 = (bf16[128,1408]{1,0:T(8,128)(2,1)}, f32[64,1152]{1,0:T(8,128)S(1)}, bf16[64,1152]{1,0:T(8,128)(2,1)S(1)}) custom-call(f32[2]{0:T(128)S(1)} %pad_maximum_fusion.4.scalars_ref, bf16[128,1280]{1,0:T(8,128)(2,1)S(1)} %constant_dynamic-update-slice_fusion.image_ref, bf16[128,1280]{1,0:T(8,128)(2,1)S(1)} %bitcast.9, ...), custom_call_target="tpu_custom_call" | custom-call | tf_op jit(solution)/shard_map/pallas_call | solution.py:189
  37.7 0.1 collective-permute-start.6
  37.8 1.2 %collective-permute-done.6 = bf16[64,1152]{1,0:T(8,128)(2,1)S(1)} collective-permute-done((bf16[64,1152]{1,0:T(8,128)(2,1)S(1)}, bf16[64,1152]{1,0:T(8,128)(2,1)S(1)}, u32[]{:S(2)}, u32[]{:S(2)}) %collective-permute-start.6) | collective-permute-done | bytes 147488 | tf_op jit(solution)/shard_map/ppermute | solution.py:27
  39.1 1.5 %collective-permute-start.7 = (bf16[32,1152]{1,0:T(8,128)(2,1)S(1)}, bf16[32,1152]{1,0:T(8,128)(2,1)S(1)}, u32[]{:S(2)}, u32[]{:S(2)}) collective-permute-start(bf16[32,1152]{1,0:T(8,128)(2,1)S(1)} %slice.68), channel_id=1, source_target_pairs={{0,2},{2,0},{4,6},{6,4},{8,10},{10,8},{12,14},{14,12},{1,3},{3,1},... | collective-permute-start | bytes 221192 | tf_op jit(solution)/shard_map/ppermute | solution.py:27
  40.6 7.2 %all-to-all-start.1 = ((bf16[16,8,1408]{2,1,0:T(8,128)(2,1)}), bf16[16,8,1408]{2,1,0:T(8,128)(2,1)S(1)}, u32[]{:S(2)}, u32[]{:S(2)}) async-start(bf16[16,8,1408]{2,1,0:T(8,128)(2,1)} %bitcast.2), calls=%async_computation.1 | async-start | bytes 720896 | tf_op jit(solution)/shard_map/all_to_all | solution.py:31
  47.9 1.6 %collective-permute-start.8 = (bf16[16,1152]{1,0:T(8,128)(2,1)S(1)}, bf16[16,1152]{1,0:T(8,128)(2,1)S(1)}, u32[]{:S(2)}, u32[]{:S(2)}) collective-permute-start(bf16[16,1152]{1,0:T(8,128)(2,1)S(1)} %slice.69), channel_id=1, source_target_pairs={{0,4},{2,6},{4,0},{6,2},{8,12},{10,14},{12,8},{14,10},{1,5},{3,7},... | collective-permute-start | bytes 110600 | tf_op jit(solution)/shard_map/ppermute | solution.py:27
  49.5 6.1 %all-to-all-done.1.back_ref = bf16[16,8,1408]{2,1,0:T(8,128)(2,1)S(1)} async-done(((bf16[16,8,1408]{2,1,0:T(8,128)(2,1)}), bf16[16,8,1408]{2,1,0:T(8,128)(2,1)S(1)}, u32[]{:S(2)}, u32[]{:S(2)}) %all-to-all-start.1) | async-done | bytes 360480 | tf_op jit(solution)/shard_map/all_to_all | solution.py:31
  55.8 1.2 %collective-permute-done.10 = f32[8,256]{1,0:T(8,128)S(1)} collective-permute-done((f32[8,256]{1,0:T(8,128)S(1)}, f32[8,256]{1,0:T(8,128)S(1)}, u32[]{:S(2)}, u32[]{:S(2)}) %collective-permute-start.10) | collective-permute-done | bytes 8224 | tf_op jit(solution)/shard_map/ppermute | solution.py:27
  57.0 0.6 collective-permute-start.11
  57.6 4.2 %collective-permute-start.9 = (bf16[8,1152]{1,0:T(8,128)(2,1)S(1)}, bf16[8,1152]{1,0:T(8,128)(2,1)S(1)}, u32[]{:S(2)}, u32[]{:S(2)}) collective-permute-start(bf16[8,1152]{1,0:T(8,128)(2,1)S(1)} %slice.70), channel_id=1, source_target_pairs={{0,8},{2,10},{4,12},{6,14},{8,0},{10,2},{12,4},{14,6},{1,9},{3,11}... | collective-permute-start | bytes 55304 | tf_op jit(solution)/shard_map/ppermute | solution.py:27
  61.7 0.4 collective-permute-start.12
  62.1 4.2 %collective-permute-done.12 = f32[8,256]{1,0:T(8,128)S(1)} collective-permute-done((f32[8,256]{1,0:T(8,128)S(1)}, f32[8,256]{1,0:T(8,128)S(1)}, u32[]{:S(2)}, u32[]{:S(2)}) %collective-permute-start.12) | collective-permute-done | bytes 8224 | tf_op jit(solution)/shard_map/ppermute | solution.py:27
  66.3 1.9 %collective-permute-start.13 = (f32[8,256]{1,0:T(8,128)S(1)}, f32[8,256]{1,0:T(8,128)S(1)}, u32[]{:S(2)}, u32[]{:S(2)}) collective-permute-start(f32[8,256]{1,0:T(8,128)S(1)} %add.30), channel_id=1, source_target_pairs={{0,8},{2,10},{4,12},{6,14},{8,0},{10,2},{12,4},{14,6},{1,9},{3,11}... | collective-permute-start | bytes 24584 | tf_op jit(solution)/shard_map/ppermute | solution.py:27
  68.1 1.9 %collective-permute-start.5 = (f32[1,1152]{1,0:T(1,128)S(1)}, f32[1,1152]{1,0:T(1,128)S(1)}, u32[]{:S(2)}, u32[]{:S(2)}) collective-permute-start(f32[1,1152]{1,0:T(1,128)S(1)} %get-tuple-element.28), channel_id=1, source_target_pairs={{0,1},{1,2},{2,3},{3,4},{4,5},{5,6},{6,7},{7,8},{8,9},{9,10},{10,1... | collective-permute-start | bytes 13832 | tf_op jit(solution)/shard_map/ppermute | solution.py:23
  70.1 7.2 %collective-permute-done.5.behind_ref = f32[1,1152]{1,0:T(1,128)S(1)} collective-permute-done((f32[1,1152]{1,0:T(1,128)S(1)}, f32[1,1152]{1,0:T(1,128)S(1)}, u32[]{:S(2)}, u32[]{:S(2)}) %collective-permute-start.5) | collective-permute-done | bytes 4640 | tf_op jit(solution)/shard_map/ppermute | solution.py:23
  77.3 1.4 %shard_map.106 = (f32[256,1152]{1,0:T(8,128)}, f32[8,1152]{1,0:T(8,128)}) custom-call(s32[1,256]{1,0:T(1,128)S(1)} %bitcast.11, f32[8,1152]{1,0:T(8,128)S(1)} %get-tuple-element.27.grad_ref, f32[1,1152]{1,0:T(1,128)S(1)} %collective-permute-done.5.behind_ref, f32[8,1152]{1,0:T(8,128)S(1)} %slice.47.keep_ref, ...), custom_call_target="tpu_custom_call" | custom-call | tf_op jit(solution)/shard_map/pallas_call | solution.py:210
  78.7 0.5 fusion.1
  79.2 0.6 pad_maximum_fusion.3
  (40 shorter events, 0.7 us)
Async XLA Ops:
  0.6 1.1 %copy-start = (bf16[256,1152]{1,0:T(8,128)(2,1)S(1)}, bf16[256,1152]{1,0:T(8,128)(2,1)}, u32[]{:S(2)}) copy-start(bf16[256,1152]{1,0:T(8,128)(2,1)} %tokens_ref.1) | copy-start | bytes 1769476
  1.7 0.7 copy-start.1
  2.4 0.7 copy-start.2
  3.1 0.7 copy-start.4
  4.5 11.5 %collective-permute-start.4 = (f32[1,1152]{1,0:T(1,128)S(1)}, f32[1,1152]{1,0:T(1,128)S(1)}, u32[]{:S(2)}, u32[]{:S(2)}) collective-permute-start(f32[1,1152]{1,0:T(1,128)S(1)} %get-tuple-element.22), channel_id=1, source_target_pairs={{1,0},{2,1},{3,2},{4,3},{5,4},{6,5},{7,6},{8,7},{9,8},{10,9},{11,1... | collective-permute-start | bytes 13832 | tf_op jit(solution)/shard_map/ppermute | solution.py:23
  13.8 10.8 %collective-permute-start = (bf16[8,1280]{1,0:T(8,128)(2,1)S(1)}, bf16[8,1280]{1,0:T(8,128)(2,1)S(1)}, u32[]{:S(2)}, u32[]{:S(2)}) collective-permute-start(bf16[8,1280]{1,0:T(8,128)(2,1)S(1)} %get-tuple-element.20), channel_id=1, source_target_pairs={{0,8},{2,10},{4,12},{6,14},{8,0},{10,2},{12,4},{14,6},{1,9},{3,11}... | collective-permute-start | bytes 61448 | tf_op jit(solution)/shard_map/ppermute | solution.py:27
  17.4 18.2 %all-to-all-start = ((bf16[16,8,1280]{2,1,0:T(8,128)(2,1)}), bf16[16,8,1280]{2,1,0:T(8,128)(2,1)S(1)}, u32[]{:S(2)}, u32[]{:S(2)}) async-start(bf16[16,8,1280]{2,1,0:T(8,128)(2,1)} %get-tuple-element.23), calls=%async_computation | async-start | bytes 655360 | tf_op jit(solution)/shard_map/all_to_all | solution.py:31
  24.6 5.0 %collective-permute-start.1 = (bf16[16,1280]{1,0:T(8,128)(2,1)S(1)}, bf16[16,1280]{1,0:T(8,128)(2,1)S(1)}, u32[]{:S(2)}, u32[]{:S(2)}) collective-permute-start(bf16[16,1280]{1,0:T(8,128)(2,1)S(1)} %pad_maximum_fusion.2), channel_id=1, source_target_pairs={{0,4},{2,6},{4,0},{6,2},{8,12},{10,14},{12,8},{14,10},{1,5},{3,7},... | collective-permute-start | bytes 122888 | tf_op jit(solution)/shard_map/ppermute | solution.py:27
  29.6 4.4 %collective-permute-start.2 = (bf16[32,1280]{1,0:T(8,128)(2,1)S(1)}, bf16[32,1280]{1,0:T(8,128)(2,1)S(1)}, u32[]{:S(2)}, u32[]{:S(2)}) collective-permute-start(bf16[32,1280]{1,0:T(8,128)(2,1)S(1)} %pad_maximum_fusion.1), channel_id=1, source_target_pairs={{0,2},{2,0},{4,6},{6,4},{8,10},{10,8},{12,14},{14,12},{1,3},{3,1},... | collective-permute-start | bytes 245768 | tf_op jit(solution)/shard_map/ppermute | solution.py:27
  34.1 1.5 %collective-permute-start.3 = (bf16[64,1280]{1,0:T(8,128)(2,1)S(1)}, bf16[64,1280]{1,0:T(8,128)(2,1)S(1)}, u32[]{:S(2)}, u32[]{:S(2)}) collective-permute-start(bf16[64,1280]{1,0:T(8,128)(2,1)S(1)} %pad_maximum_fusion), channel_id=1, source_target_pairs={{0,1},{1,0},{2,3},{3,2},{4,5},{5,4},{6,7},{7,6},{8,9},{9,8},{10,11... | collective-permute-start | bytes 491528 | tf_op jit(solution)/shard_map/ppermute | solution.py:27
  37.7 1.4 %collective-permute-start.6 = (bf16[64,1152]{1,0:T(8,128)(2,1)S(1)}, bf16[64,1152]{1,0:T(8,128)(2,1)S(1)}, u32[]{:S(2)}, u32[]{:S(2)}) collective-permute-start(bf16[64,1152]{1,0:T(8,128)(2,1)S(1)} %get-tuple-element.30), channel_id=1, source_target_pairs={{0,1},{1,0},{2,3},{3,2},{4,5},{5,4},{6,7},{7,6},{8,9},{9,8},{10,11... | collective-permute-start | bytes 442376 | tf_op jit(solution)/shard_map/ppermute | solution.py:27
  39.1 38.2 %copy-start.3 = (s32[256]{0:T(256)S(1)}, s32[256]{0:T(256)}, u32[]{:S(2)}) copy-start(s32[256]{0:T(256)} %param.9) | copy-start | bytes 3076
  39.1 8.8 %collective-permute-start.7 = (bf16[32,1152]{1,0:T(8,128)(2,1)S(1)}, bf16[32,1152]{1,0:T(8,128)(2,1)S(1)}, u32[]{:S(2)}, u32[]{:S(2)}) collective-permute-start(bf16[32,1152]{1,0:T(8,128)(2,1)S(1)} %slice.68), channel_id=1, source_target_pairs={{0,2},{2,0},{4,6},{6,4},{8,10},{10,8},{12,14},{14,12},{1,3},{3,1},... | collective-permute-start | bytes 221192 | tf_op jit(solution)/shard_map/ppermute | solution.py:27
  40.6 14.9 %all-to-all-start.1 = ((bf16[16,8,1408]{2,1,0:T(8,128)(2,1)}), bf16[16,8,1408]{2,1,0:T(8,128)(2,1)S(1)}, u32[]{:S(2)}, u32[]{:S(2)}) async-start(bf16[16,8,1408]{2,1,0:T(8,128)(2,1)} %bitcast.2), calls=%async_computation.1 | async-start | bytes 720896 | tf_op jit(solution)/shard_map/all_to_all | solution.py:31
  47.9 9.6 %collective-permute-start.8 = (bf16[16,1152]{1,0:T(8,128)(2,1)S(1)}, bf16[16,1152]{1,0:T(8,128)(2,1)S(1)}, u32[]{:S(2)}, u32[]{:S(2)}) collective-permute-start(bf16[16,1152]{1,0:T(8,128)(2,1)S(1)} %slice.69), channel_id=1, source_target_pairs={{0,4},{2,6},{4,0},{6,2},{8,12},{10,14},{12,8},{14,10},{1,5},{3,7},... | collective-permute-start | bytes 110600 | tf_op jit(solution)/shard_map/ppermute | solution.py:27
  55.7 1.3 %collective-permute-start.10 = (f32[8,256]{1,0:T(8,128)S(1)}, f32[8,256]{1,0:T(8,128)S(1)}, u32[]{:S(2)}, u32[]{:S(2)}) collective-permute-start(f32[8,256]{1,0:T(8,128)S(1)} %get-tuple-element.35), channel_id=1, source_target_pairs={{0,1},{1,0},{2,3},{3,2},{4,5},{5,4},{6,7},{7,6},{8,9},{9,8},{10,11... | collective-permute-start | bytes 24584 | tf_op jit(solution)/shard_map/ppermute | solution.py:27
  57.0 4.8 %collective-permute-start.11 = (f32[8,256]{1,0:T(8,128)S(1)}, f32[8,256]{1,0:T(8,128)S(1)}, u32[]{:S(2)}, u32[]{:S(2)}) collective-permute-start(f32[8,256]{1,0:T(8,128)S(1)} %add.28), channel_id=1, source_target_pairs={{0,2},{2,0},{4,6},{6,4},{8,10},{10,8},{12,14},{14,12},{1,3},{3,1},... | collective-permute-start | bytes 24584 | tf_op jit(solution)/shard_map/ppermute | solution.py:27
  57.6 12.5 %collective-permute-start.9 = (bf16[8,1152]{1,0:T(8,128)(2,1)S(1)}, bf16[8,1152]{1,0:T(8,128)(2,1)S(1)}, u32[]{:S(2)}, u32[]{:S(2)}) collective-permute-start(bf16[8,1152]{1,0:T(8,128)(2,1)S(1)} %slice.70), channel_id=1, source_target_pairs={{0,8},{2,10},{4,12},{6,14},{8,0},{10,2},{12,4},{14,6},{1,9},{3,11}... | collective-permute-start | bytes 55304 | tf_op jit(solution)/shard_map/ppermute | solution.py:27
  61.7 4.6 %collective-permute-start.12 = (f32[8,256]{1,0:T(8,128)S(1)}, f32[8,256]{1,0:T(8,128)S(1)}, u32[]{:S(2)}, u32[]{:S(2)}) collective-permute-start(f32[8,256]{1,0:T(8,128)S(1)} %add.29), channel_id=1, source_target_pairs={{0,4},{2,6},{4,0},{6,2},{8,12},{10,14},{12,8},{14,10},{1,5},{3,7},... | collective-permute-start | bytes 24584 | tf_op jit(solution)/shard_map/ppermute | solution.py:27
  66.3 12.4 %collective-permute-start.13 = (f32[8,256]{1,0:T(8,128)S(1)}, f32[8,256]{1,0:T(8,128)S(1)}, u32[]{:S(2)}, u32[]{:S(2)}) collective-permute-start(f32[8,256]{1,0:T(8,128)S(1)} %add.30), channel_id=1, source_target_pairs={{0,8},{2,10},{4,12},{6,14},{8,0},{10,2},{12,4},{14,6},{1,9},{3,11}... | collective-permute-start | bytes 24584 | tf_op jit(solution)/shard_map/ppermute | solution.py:27
  68.1 9.1 %collective-permute-start.5 = (f32[1,1152]{1,0:T(1,128)S(1)}, f32[1,1152]{1,0:T(1,128)S(1)}, u32[]{:S(2)}, u32[]{:S(2)}) collective-permute-start(f32[1,1152]{1,0:T(1,128)S(1)} %get-tuple-element.28), channel_id=1, source_target_pairs={{0,1},{1,2},{2,3},{3,4},{4,5},{5,6},{6,7},{7,8},{8,9},{9,10},{10,1... | collective-permute-start | bytes 13832 | tf_op jit(solution)/shard_map/ppermute | solution.py:23

commit v3 on v2

--- a/solution.py
+++ b/solution.py
@@ -1,3 +1,5 @@
+import functools
+
 import jax
 import jax.numpy as jnp
 from jax import lax
@@ -13,8 +15,10 @@
 F32, BF16 = jnp.float32, jnp.bfloat16
 SMEM = pl.BlockSpec(memory_space=pltpu.SMEM)
 VMEM = pl.BlockSpec(memory_space=pltpu.VMEM)
+HBM = pl.BlockSpec(memory_space=pltpu.HBM)
 
 STEPS = ((Z, 4), (Z, 2), (Z, 1), (C, 1))
+FROM = (0, 4, 2, 6, 1, 5, 3, 7)
 
 
 def from_behind(value, by):
@@ -27,8 +31,8 @@
     return lax.ppermute(value, axis, [(i, i ^ bit) for i in range(lax.axis_size(axis))])
 
 
-def to_plane(blocks):
-    return lax.all_to_all(blocks, PLANE, 0, 0, tiled=True)
+def to_all(blocks, axes):
+    return lax.all_to_all(blocks, axes, 0, 0, tiled=True)
 
 
 def members(ids, pairs, copies):
@@ -52,8 +56,25 @@
     return cells.astype(F32).astype(BF16)
 
 
-def prepare(groups_ref, ids_ref, image_ref, tokens_ref, row_ref, unit_ref, norm_ref, pooled_ref, spill_ref):
-    pairs, width = image_ref.shape
+def prepare(
+    groups_hbm, ids_hbm, image_hbm, tokens_hbm, gain_hbm,
+    row_ref, unit_ref, norm_ref, pooled_ref, spill_ref, tile_ref, gain_out,
+    groups_ref, ids_ref, image_ref, tokens_ref, gain_ref, sems,
+):
+    pairs, width = image_hbm.shape
+    moves = [
+        pltpu.make_async_copy(source, target, sems.at[i])
+        for i, (source, target) in enumerate(
+            (
+                (image_hbm, image_ref), (groups_hbm, groups_ref), (ids_hbm, ids_ref),
+                (tokens_hbm, tokens_ref), (gain_hbm, gain_ref),
+            )
+        )
+    ]
+    for move in moves:
+        move.start()
+    moves[0].wait()
+    moves[1].wait()
     image = image_ref[...].astype(F32)
     norm = jnp.sqrt(jnp.sum(image * image, axis=1, keepdims=True))
     unit = image / norm
@@ -61,12 +82,17 @@
     norm_ref[...] = norm
     row_ref[:, :width] = unit.astype(BF16)
     row_ref[:, width:] = id_tile(groups_ref, pairs, False)
+    tile_ref[...] = id_tile(groups_ref, pairs, True)
+    moves[4].wait()
+    gain_out[...] = gain_ref[...][None, :]
+    moves[2].wait()
+    moves[3].wait()
     sums = jnp.dot(members(ids_ref[...], pairs, 1), tokens_ref[...], preferred_element_type=F32)
     pooled_ref[...] = sums[:pairs]
     spill_ref[...] = sums[pairs : pairs + 1]
 
 
-def text_rows(groups_ref, pooled_ref, arrived_ref, gain_ref, rows_ref, unit_ref, norm_ref):
+def text_rows(tile_ref, pooled_ref, arrived_ref, gain_ref, rows_ref, unit_ref, norm_ref):
     pairs, width = pooled_ref.shape
     last = lax.broadcasted_iota(jnp.int32, (pairs, 1), 0) == pairs - 1
     pooled = pooled_ref[...] + jnp.where(last, arrived_ref[...], 0.0)
@@ -75,15 +101,15 @@
     unit = embedded / norm
     unit_ref[...] = unit
     norm_ref[...] = norm
-    low, ids = unit.astype(BF16), id_tile(groups_ref, pairs, True)
+    low, ids = unit.astype(BF16), tile_ref[...]
     for k in range(rows_ref.shape[0]):
         rows_ref[k, :, :width] = low
         rows_ref[k, :, width:] = ids
 
 
-def pair_math(scalars_ref, image_ref, text_ref, gain_ref, text_out, keep_out, send_out):
+def pair_math(log_scale_ref, bias_ref, image_ref, text_ref, gain_ref, text_out, keep_out, send_out):
     width = gain_ref.shape[1]
-    scale = jnp.exp(jnp.full((1, LANES), scalars_ref[0], F32))[:, :1]
+    scale = jnp.exp(jnp.full((1, LANES), log_scale_ref[0], F32))[:, :1]
     image, text = image_ref[:, :width], text_ref[:, :width]
     contract = (((1,), (1,)), ((), ()))
     scaled = scale * lax.dot_general(image, text, contract, preferred_element_type=F32)
@@ -91,7 +117,7 @@
         image_ref[:, width:], text_ref[:, width:], contract, preferred_element_type=F32
     )
     match = apart == 0.0
-    logits = scaled + scalars_ref[1]
+    logits = scaled + bias_ref[0]
     margin = jnp.where(match, -logits, logits)
     tail = jnp.exp(-jnp.abs(margin))
     losses = jnp.maximum(margin, 0.0) + jnp.log1p(tail)
@@ -134,7 +160,22 @@
     last_out[...] = grad[pairs - 1 :]
 
 
-def finish(ids_ref, grad_ref, behind_ref, keep_ref, came_ref, unit_ref, norm_ref, token_out, image_out):
+def pack(place_ref, keep_ref, came_ref, totals_ref, other_ref, out_ref):
+    places, pairs, _ = out_ref.shape
+    width = keep_ref.shape[1]
+    total = totals_ref[...] + other_ref[...]
+    high = total.astype(BF16)
+    low = (total - high.astype(F32)).astype(BF16)
+    for k in range(places):
+        rows = slice(pairs * k, pairs * (k + 1))
+        block = keep_ref[rows] + came_ref[rows].astype(F32)
+        place = place_ref[0] ^ FROM[k]
+        out_ref[place, :, :width] = block.astype(BF16)
+        out_ref[place, :, width : width + 2 * LANES] = high
+        out_ref[place, :, width + 2 * LANES :] = low
+
+
+def token_rows(ids_ref, grad_ref, behind_ref, token_out):
     pairs, width = grad_ref.shape
     table = jnp.concatenate(
         [grad_ref[...], jnp.broadcast_to(behind_ref[...], (pairs, width))], axis=0
@@ -147,32 +188,48 @@
         (((0,), (0,)), ((), ())),
         preferred_element_type=F32,
     )
-    grad, unit = keep_ref[...] + came_ref[...].astype(F32), unit_ref[...]
+
+
+def finish(back_ref, unit_ref, norm_ref, image_out, gain_out, scalars_out, *, count):
+    width = unit_ref.shape[1]
+    total = jnp.sum(back_ref[...].astype(F32), axis=0)
+    first = total[:, width : width + LANES] + total[:, width + 2 * LANES : width + 3 * LANES]
+    second = total[:, width + LANES : width + 2 * LANES] + total[:, width + 3 * LANES :]
+    gain_out[...] = jnp.concatenate([first[r] for r in range(8)] + [second[0]])
+    scalars_out[...] = ((second[1] + second[2]) / count)[:3]
+    grad, unit = total[:, :width], unit_ref[...]
     grad = grad - unit * jnp.sum(unit * grad, axis=1, keepdims=True)
     image_out[...] = grad / norm_ref[...]
 
 
-def local(kernel, specs, *outs):
+def local(kernel, specs, *outs, scratch=()):
     return pl.pallas_call(
         kernel,
         in_specs=specs,
         out_specs=[VMEM] * len(outs),
         out_shape=[jax.ShapeDtypeStruct(*o) for o in outs],
+        scratch_shapes=scratch,
         compiler_params=pltpu.CompilerParams(vmem_limit_bytes=16 << 20),
     )
 
 
 def per_device(image_emb, text_tokens, caption_ids, groups, text_gain, log_scale, logit_bias):
     pairs, width = image_emb.shape
+    tokens = text_tokens.shape[0]
     total_pairs = pairs * lax.axis_size(DP)
     plane = lax.axis_size(PLANE)
     wide = width + LANES
     ids = caption_ids[None, :]
-    gain = text_gain[None, :]
-    row, unit_image, image_norm, pooled, spill = local(
-        prepare, [SMEM, VMEM, VMEM, VMEM],
+    row, unit_image, image_norm, pooled, spill, tile, gain = local(
+        prepare, [HBM] * 5,
         ((pairs, wide), BF16), ((pairs, width), F32), ((pairs, 1), F32), ((pairs, width), F32), ((1, width), F32),
-    )(groups, ids, image_emb, text_tokens)
+        ((pairs, LANES), BF16), ((1, width), F32),
+        scratch=(
+            pltpu.SMEM((pairs,), jnp.int32), pltpu.VMEM((1, tokens), jnp.int32),
+            pltpu.VMEM((pairs, width), BF16), pltpu.VMEM((tokens, width), BF16),
+            pltpu.VMEM((width,), F32), pltpu.SemaphoreType.DMA((5,)),
+        ),
+    )(*(pltpu.with_memory_space_constraint(a, pltpu.HBM) for a in (groups, ids, image_emb, text_tokens, text_gain)))
 
     arrived = from_behind(spill, -1)
     images = row
@@ -180,40 +237,35 @@
         images = jnp.concatenate([images, exchange(images, axis, bit)], axis=0)
 
     rows, unit_text, text_norm = local(
-        text_rows, [SMEM, VMEM, VMEM, VMEM],
+        text_rows, [VMEM] * 4,
         ((plane, pairs, wide), BF16), ((pairs, width), F32), ((pairs, 1), F32),
-    )(groups, pooled, arrived, gain)
-    texts = to_plane(rows).reshape(plane * pairs, wide)
+    )(tile, pooled, arrived, gain)
+    texts = to_all(rows, PLANE).reshape(plane * pairs, wide)
 
     line = images.shape[0]
     text_part, keep, send = local(
-        pair_math, [SMEM, VMEM, VMEM, VMEM],
+        pair_math, [SMEM, SMEM, VMEM, VMEM, VMEM],
         ((plane * pairs, wide + LANES), BF16), ((line // 2, width), F32), ((line // 2, width), BF16),
-    )(jnp.concatenate([log_scale, logit_bias]), images, texts, gain)
-
-    back = to_plane(text_part.reshape(plane, pairs, wide + LANES))
-    for n, (axis, bit) in enumerate(reversed(STEPS)):
-        came = exchange(send, axis, bit)
-        if n + 1 < len(STEPS):
-            whole = keep + came.astype(F32)
-            half = whole.shape[0] // 2
-            keep, send = whole[:half], whole[half:].astype(BF16)
-
+    )(log_scale, logit_bias, images, texts, gain)
+
+    back = to_all(text_part.reshape(plane, pairs, wide + LANES), PLANE)
+    came = exchange(send, C, 1)
     pooled_grad, last, totals = local(
         text_gradient, [VMEM, VMEM, VMEM, VMEM],
         ((pairs, width), F32), ((1, width), F32), ((pairs, 2 * LANES), F32),
     )(back, unit_text, text_norm, gain)
+    other = exchange(totals, C, 1)
+    depth = lax.axis_size(Z)
+    (blocks,) = local(
+        pack, [SMEM, VMEM, VMEM, VMEM, VMEM], ((depth, pairs, width + 4 * LANES), BF16)
+    )(lax.axis_index(Z)[None], keep, came, totals, other)
+    line_back = to_all(blocks, Z)
     behind = from_behind(last, 1)
-    for axis, bit in reversed(STEPS):
-        totals = totals + exchange(totals, axis, bit)
-
-    token_grad, image_grad = local(
-        finish, [VMEM] * 7, ((text_tokens.shape[0], width), F32), ((pairs, width), F32)
-    )(ids, pooled_grad, behind, keep, came, unit_image, image_norm)
-    gain_grad = jnp.concatenate([totals[:, :LANES].reshape(-1), totals[0, LANES:]])
-    scalars = (totals[1, LANES : LANES + 3] + totals[2, LANES : LANES + 3]) / float(
-        total_pairs * total_pairs
-    )
+    (token_grad,) = local(token_rows, [VMEM] * 3, ((tokens, width), F32))(ids, pooled_grad, behind)
+    image_grad, gain_grad, scalars = local(
+        functools.partial(finish, count=float(total_pairs * total_pairs)), [VMEM] * 3,
+        ((pairs, width), F32), ((width,), F32), ((3,), F32),
+    )(line_back, unit_image, image_norm)
     return (image_grad, token_grad, gain_grad, scalars)
 
 

time: 80.4 us -> 69.7 us (0.87)
  the two profiles are of different devices: /device:TPU:8 before, /device:TPU:1 now
where the time goes in v3:
time: 69.7 us; the launch traced here: 69.2 us
  starting transfers between devices  40.4 us (58%)
  waiting for transfers between devices  20 us (29%)
  Pallas kernels  6.78 us (10%)
  between operations  2.02 us (3%)
    all_to_all x3, starting transfers between devices, to_all(): return lax.all_to_all(blocks, axes, 0, 0, tiled=True)  18.8 us
    ppermute x6, starting transfers between devices, exchange(): lax.ppermute(value, axis, [(i, i ^ bit) for i in range(lax.axis_size(axis...  12.3 us
    all_to_all x3, waiting for transfers between devices, to_all(): return lax.all_to_all(blocks, axes, 0, 0, tiled=True)  12 us
    ppermute x2, starting transfers between devices, from_behind(): return lax.ppermute(value, DP, pairs)  9.26 us
    ppermute x6, waiting for transfers between devices, exchange(): lax.ppermute(value, axis, [(i, i ^ bit) for i in range(lax.axis_size(axis...  7.25 us
    pallas_call x1, Pallas kernels, per_device(): local(pair_math, [SMEM, SMEM, VMEM, VMEM, VMEM], ((plane * pairs, wide +...  1.54 us
    pallas_call x1, Pallas kernels, per_device(): local(token_rows, [VMEM] * 3, ((tokens, width), F32))  1.42 us
  transfers between devices with their start and end apart: 11, of which 7 were waited for; matrix products, arithmetic and copies ran while one was open for 0% of the time, Pallas kernels for 3%

profile of v3, /device:TPU:1, one launch (start us, length us, event | category | flops | bytes accessed | tf_op | source)
XLA Modules:
  0.0 69.2 jit_solution(6347969830177030116)
XLA Ops:
  0.6 1.4 %shard_map.102 = (bf16[8,1280]{1,0:T(8,128)(2,1)S(1)}, f32[8,1152]{1,0:T(8,128)S(1)}, f32[8,1]{1,0:T(8,128)S(1)}, f32[8,1152]{1,0:T(8,128)S(1)}, f32[1,1152]{1,0...) custom-call(s32[8]{0:T(128)} %groups_hbm.1, s32[1,256]{1,0:T(1,128)} %bitcast.5, ...), custom_call_target="tpu_custom_call" | custom-call | tf_op jit(solution)/shard_map/pallas_call | solution.py:223
  2.0 5.1 %collective-permute-start.4 = (f32[1,1152]{1,0:T(1,128)S(1)}, f32[1,1152]{1,0:T(1,128)S(1)}, u32[]{:S(2)}, u32[]{:S(2)}) collective-permute-start(f32[1,1152]{1,0:T(1,128)S(1)} %get-tuple-element.26), channel_id=1, source_target_pairs={{1,0},{2,1},{3,2},{4,3},{5,4},{6,5},{7,6},{8,7},{9,8},{10,9},{11,1... | collective-permute-start | bytes 13832 | tf_op jit(solution)/shard_map/ppermute | solution.py:27
  7.1 5.3 %collective-permute-start = (bf16[8,1280]{1,0:T(8,128)(2,1)S(1)}, bf16[8,1280]{1,0:T(8,128)(2,1)S(1)}, u32[]{:S(2)}, u32[]{:S(2)}) collective-permute-start(bf16[8,1280]{1,0:T(8,128)(2,1)S(1)} %get-tuple-element.23), channel_id=1, source_target_pairs={{0,8},{2,10},{4,12},{6,14},{8,0},{10,2},{12,4},{14,6},{1,9},{3,11}... | collective-permute-start | bytes 61448 | tf_op jit(solution)/shard_map/ppermute | solution.py:31
  13.7 0.0 collective-permute-done.4.arrived_ref
  13.7 0.9 %shard_map.103 = (bf16[16,8,1280]{2,1,0:T(8,128)(2,1)}, f32[8,1152]{1,0:T(8,128)S(1)}, f32[8,1]{1,0:T(8,128)S(1)}) custom-call(bf16[8,128]{1,0:T(8,128)(2,1)S(1)} %get-tuple-element.24.tile_ref, f32[8,1152]{1,0:T(8,128)S(1)} %get-tuple-element.25.pooled_ref, f32[1,1152]{1,0:T(1,128)S(1)} %collective-permute-done.4.arrived_ref, ...), custom_call_target="tpu_custom_call" | custom-call | tf_op jit(solution)/shard_map/pallas_call | solution.py:239
  14.6 6.8 %all-to-all-start = ((bf16[16,8,1280]{2,1,0:T(8,128)(2,1)}), bf16[16,8,1280]{2,1,0:T(8,128)(2,1)S(1)}, u32[]{:S(2)}, u32[]{:S(2)}) async-start(bf16[16,8,1280]{2,1,0:T(8,128)(2,1)} %get-tuple-element.28), calls=%async_computation | async-start | bytes 655360 | tf_op jit(solution)/shard_map/all_to_all | solution.py:35
  21.4 0.0 collective-permute-done
  21.4 1.3 %collective-permute-start.1 = (bf16[16,1280]{1,0:T(8,128)(2,1)S(1)}, bf16[16,1280]{1,0:T(8,128)(2,1)S(1)}, u32[]{:S(2)}, u32[]{:S(2)}) collective-permute-start(bf16[16,1280]{1,0:T(8,128)(2,1)S(1)} %pad_maximum_fusion.2), channel_id=1, source_target_pairs={{0,4},{2,6},{4,0},{6,2},{8,12},{10,14},{12,8},{14,10},{1,5},{3,7},... | collective-permute-start | bytes 122888 | tf_op jit(solution)/shard_map/ppermute | solution.py:31
  22.7 2.6 %collective-permute-done.1 = bf16[16,1280]{1,0:T(8,128)(2,1)S(1)} collective-permute-done((bf16[16,1280]{1,0:T(8,128)(2,1)S(1)}, bf16[16,1280]{1,0:T(8,128)(2,1)S(1)}, u32[]{:S(2)}, u32[]{:S(2)}) %collective-permute-start.1) | collective-permute-done | bytes 40992 | tf_op jit(solution)/shard_map/ppermute | solution.py:31
  25.2 0.7 %collective-permute-start.2 = (bf16[32,1280]{1,0:T(8,128)(2,1)S(1)}, bf16[32,1280]{1,0:T(8,128)(2,1)S(1)}, u32[]{:S(2)}, u32[]{:S(2)}) collective-permute-start(bf16[32,1280]{1,0:T(8,128)(2,1)S(1)} %pad_maximum_fusion.1), channel_id=1, source_target_pairs={{0,2},{2,0},{4,6},{6,4},{8,10},{10,8},{12,14},{14,12},{1,3},{3,1},... | collective-permute-start | bytes 245768 | tf_op jit(solution)/shard_map/ppermute | solution.py:31
  26.0 2.8 %collective-permute-done.2 = bf16[32,1280]{1,0:T(8,128)(2,1)S(1)} collective-permute-done((bf16[32,1280]{1,0:T(8,128)(2,1)S(1)}, bf16[32,1280]{1,0:T(8,128)(2,1)S(1)}, u32[]{:S(2)}, u32[]{:S(2)}) %collective-permute-start.2) | collective-permute-done | bytes 81952 | tf_op jit(solution)/shard_map/ppermute | solution.py:31
  28.8 2.7 %collective-permute-start.3 = (bf16[64,1280]{1,0:T(8,128)(2,1)S(1)}, bf16[64,1280]{1,0:T(8,128)(2,1)S(1)}, u32[]{:S(2)}, u32[]{:S(2)}) collective-permute-start(bf16[64,1280]{1,0:T(8,128)(2,1)S(1)} %pad_maximum_fusion), channel_id=1, source_target_pairs={{0,1},{1,0},{2,3},{3,2},{4,5},{5,4},{6,7},{7,6},{8,9},{9,8},{10,11... | collective-permute-start | bytes 491528 | tf_op jit(solution)/shard_map/ppermute | solution.py:31
  31.5 1.0 %collective-permute-done.3 = bf16[64,1280]{1,0:T(8,128)(2,1)S(1)} collective-permute-done((bf16[64,1280]{1,0:T(8,128)(2,1)S(1)}, bf16[64,1280]{1,0:T(8,128)(2,1)S(1)}, u32[]{:S(2)}, u32[]{:S(2)}) %collective-permute-start.3) | collective-permute-done | bytes 163872 | tf_op jit(solution)/shard_map/ppermute | solution.py:31
  32.5 0.0 all-to-all-done
  32.6 1.5 %shard_map.104 = (bf16[128,1408]{1,0:T(8,128)(2,1)}, f32[64,1152]{1,0:T(8,128)S(1)}, bf16[64,1152]{1,0:T(8,128)(2,1)S(1)}) custom-call(f32[1]{0:T(128)S(6)} %copy.15.log_scale_ref, f32[1]{0:T(128)S(6)} %copy.16.bias_ref, bf16[128,1280]{1,0:T(8,128)(2,1)S(1)} %constant_dynamic-update-slice_fusion.image_ref, bf16[128,1280]{1,0:T(8,128)(2,1)S(1)} %bitcast.4, ...), custom_call_target="tpu_custom_call" | custom-call | tf_op jit(solution)/shard_map/pallas_call | solution.py:246
  34.1 0.0 copy-start
  34.1 7.1 %all-to-all-start.1 = ((bf16[16,8,1408]{2,1,0:T(8,128)(2,1)}), bf16[16,8,1408]{2,1,0:T(8,128)(2,1)S(1)}, u32[]{:S(2)}, u32[]{:S(2)}) async-start(bf16[16,8,1408]{2,1,0:T(8,128)(2,1)} %bitcast.3), calls=%async_computation.1 | async-start | bytes 720896 | tf_op jit(solution)/shard_map/all_to_all | solution.py:35
  41.2 0.7 %collective-permute-start.5 = (bf16[64,1152]{1,0:T(8,128)(2,1)S(1)}, bf16[64,1152]{1,0:T(8,128)(2,1)S(1)}, u32[]{:S(2)}, u32[]{:S(2)}) collective-permute-start(bf16[64,1152]{1,0:T(8,128)(2,1)S(1)} %get-tuple-element.30), channel_id=1, source_target_pairs={{0,1},{1,0},{2,3},{3,2},{4,5},{5,4},{6,7},{7,6},{8,9},{9,8},{10,11... | collective-permute-start | bytes 442376 | tf_op jit(solution)/shard_map/ppermute | solution.py:31
  41.9 8.5 %all-to-all-done.1.back_ref = bf16[16,8,1408]{2,1,0:T(8,128)(2,1)S(1)} async-done(((bf16[16,8,1408]{2,1,0:T(8,128)(2,1)}), bf16[16,8,1408]{2,1,0:T(8,128)(2,1)S(1)}, u32[]{:S(2)}, u32[]{:S(2)}) %all-to-all-start.1) | async-done | bytes 360480 | tf_op jit(solution)/shard_map/all_to_all | solution.py:35
  50.4 0.1 shard_map.105
  50.5 1.6 %collective-permute-start.6 = (f32[8,256]{1,0:T(8,128)S(1)}, f32[8,256]{1,0:T(8,128)S(1)}, u32[]{:S(2)}, u32[]{:S(2)}) collective-permute-start(f32[8,256]{1,0:T(8,128)S(1)} %get-tuple-element.34.totals_ref), channel_id=1, source_target_pairs={{0,1},{1,0},{2,3},{3,2},{4,5},{5,4},{6,7},{7,6},{8,9},{9,8},{10,11... | collective-permute-start | bytes 24584 | tf_op jit(solution)/shard_map/ppermute | solution.py:31
  52.1 0.0 collective-permute-done.5.came_ref
  52.1 0.8 %collective-permute-done.6.other_ref = f32[8,256]{1,0:T(8,128)S(1)} collective-permute-done((f32[8,256]{1,0:T(8,128)S(1)}, f32[8,256]{1,0:T(8,128)S(1)}, u32[]{:S(2)}, u32[]{:S(2)}) %collective-permute-start.6) | collective-permute-done | bytes 8224 | tf_op jit(solution)/shard_map/ppermute | solution.py:31
  52.9 0.7 %shard_map.106 = bf16[8,8,1664]{2,1,0:T(8,128)(2,1)} custom-call(s32[1]{0:T(128)} %bitcast.place_ref, f32[64,1152]{1,0:T(8,128)S(1)} %get-tuple-element.29.keep_ref, bf16[64,1152]{1,0:T(8,128)(2,1)S(1)} %collective-permute-done.5.came_ref, f32[8,256]{1,0:T(8,128)S(1)} %get-tuple-element.34.totals_ref, f32[8,256]{1,0:T(8,128)S(1)} %collective-permute-done.6.other_ref), custom_call_target="tpu_custom_call" | custom-call | tf_op jit(solution)/shard_map/pallas_call | solution.py:259
  53.6 5.0 %all-to-all-start.2 = ((bf16[8,8,1664]{2,1,0:T(8,128)(2,1)}), bf16[8,8,1664]{2,1,0:T(8,128)(2,1)S(1)}, u32[]{:S(2)}, u32[]{:S(2)}) async-start(bf16[8,8,1664]{2,1,0:T(8,128)(2,1)} %shard_map.106), calls=%async_computation.2 | async-start | bytes 425984 | tf_op jit(solution)/shard_map/all_to_all | solution.py:35
  58.6 4.1 %collective-permute-start.7 = (f32[1,1152]{1,0:T(1,128)S(1)}, f32[1,1152]{1,0:T(1,128)S(1)}, u32[]{:S(2)}, u32[]{:S(2)}) collective-permute-start(f32[1,1152]{1,0:T(1,128)S(1)} %get-tuple-element.39), channel_id=1, source_target_pairs={{0,1},{1,2},{2,3},{3,4},{4,5},{5,6},{6,7},{7,8},{8,9},{9,10},{10,1... | collective-permute-start | bytes 13832 | tf_op jit(solution)/shard_map/ppermute | solution.py:27
  62.8 0.7 %collective-permute-done.7.behind_ref = f32[1,1152]{1,0:T(1,128)S(1)} collective-permute-done((f32[1,1152]{1,0:T(1,128)S(1)}, f32[1,1152]{1,0:T(1,128)S(1)}, u32[]{:S(2)}, u32[]{:S(2)}) %collective-permute-start.7) | collective-permute-done | bytes 4640 | tf_op jit(solution)/shard_map/ppermute | solution.py:27
  63.5 0.0 copy-done
  63.5 1.4 %shard_map.108 = f32[256,1152]{1,0:T(8,128)} custom-call(s32[1,256]{1,0:T(1,128)S(1)} %bitcast.6, f32[8,1152]{1,0:T(8,128)S(1)} %get-tuple-element.38.grad_ref, f32[1,1152]{1,0:T(1,128)S(1)} %collective-permute-done.7.behind_ref), custom_call_target="tpu_custom_call" | custom-call | tf_op jit(solution)/shard_map/pallas_call | solution.py:264
  65.0 3.5 %all-to-all-done.2.back_ref = bf16[8,8,1664]{2,1,0:T(8,128)(2,1)S(1)} async-done(((bf16[8,8,1664]{2,1,0:T(8,128)(2,1)}), bf16[8,8,1664]{2,1,0:T(8,128)(2,1)S(1)}, u32[]{:S(2)}, u32[]{:S(2)}) %all-to-all-start.2) | async-done | bytes 213024 | tf_op jit(solution)/shard_map/all_to_all | solution.py:35
  68.5 0.7 %shard_map.107 = (f32[8,1152]{1,0:T(8,128)}, f32[1152]{0:T(1024)}, f32[3]{0:T(128)}) custom-call(bf16[8,8,1664]{2,1,0:T(8,128)(2,1)S(1)} %all-to-all-done.2.back_ref, f32[8,1152]{1,0:T(8,128)S(1)} %get-tuple-element.35.unit_ref, f32[8,1]{1,0:T(8,128)S(1)} %get-tuple-element.36.norm_ref), custom_call_target="tpu_custom_call" | custom-call | tf_op jit(solution)/shard_map/pallas_call | solution.py:265
  (8 shorter events, 0.1 us)
Async XLA Ops:
  2.0 11.7 %collective-permute-start.4 = (f32[1,1152]{1,0:T(1,128)S(1)}, f32[1,1152]{1,0:T(1,128)S(1)}, u32[]{:S(2)}, u32[]{:S(2)}) collective-permute-start(f32[1,1152]{1,0:T(1,128)S(1)} %get-tuple-element.26), channel_id=1, source_target_pairs={{1,0},{2,1},{3,2},{4,3},{5,4},{6,5},{7,6},{8,7},{9,8},{10,9},{11,1... | collective-permute-start | bytes 13832 | tf_op jit(solution)/shard_map/ppermute | solution.py:27
  7.1 14.2 %collective-permute-start = (bf16[8,1280]{1,0:T(8,128)(2,1)S(1)}, bf16[8,1280]{1,0:T(8,128)(2,1)S(1)}, u32[]{:S(2)}, u32[]{:S(2)}) collective-permute-start(bf16[8,1280]{1,0:T(8,128)(2,1)S(1)} %get-tuple-element.23), channel_id=1, source_target_pairs={{0,8},{2,10},{4,12},{6,14},{8,0},{10,2},{12,4},{14,6},{1,9},{3,11}... | collective-permute-start | bytes 61448 | tf_op jit(solution)/shard_map/ppermute | solution.py:31
  14.6 17.9 %all-to-all-start = ((bf16[16,8,1280]{2,1,0:T(8,128)(2,1)}), bf16[16,8,1280]{2,1,0:T(8,128)(2,1)S(1)}, u32[]{:S(2)}, u32[]{:S(2)}) async-start(bf16[16,8,1280]{2,1,0:T(8,128)(2,1)} %get-tuple-element.28), calls=%async_computation | async-start | bytes 655360 | tf_op jit(solution)/shard_map/all_to_all | solution.py:35
  21.4 3.8 %collective-permute-start.1 = (bf16[16,1280]{1,0:T(8,128)(2,1)S(1)}, bf16[16,1280]{1,0:T(8,128)(2,1)S(1)}, u32[]{:S(2)}, u32[]{:S(2)}) collective-permute-start(bf16[16,1280]{1,0:T(8,128)(2,1)S(1)} %pad_maximum_fusion.2), channel_id=1, source_target_pairs={{0,4},{2,6},{4,0},{6,2},{8,12},{10,14},{12,8},{14,10},{1,5},{3,7},... | collective-permute-start | bytes 122888 | tf_op jit(solution)/shard_map/ppermute | solution.py:31
  25.2 3.6 %collective-permute-start.2 = (bf16[32,1280]{1,0:T(8,128)(2,1)S(1)}, bf16[32,1280]{1,0:T(8,128)(2,1)S(1)}, u32[]{:S(2)}, u32[]{:S(2)}) collective-permute-start(bf16[32,1280]{1,0:T(8,128)(2,1)S(1)} %pad_maximum_fusion.1), channel_id=1, source_target_pairs={{0,2},{2,0},{4,6},{6,4},{8,10},{10,8},{12,14},{14,12},{1,3},{3,1},... | collective-permute-start | bytes 245768 | tf_op jit(solution)/shard_map/ppermute | solution.py:31
  28.8 3.7 %collective-permute-start.3 = (bf16[64,1280]{1,0:T(8,128)(2,1)S(1)}, bf16[64,1280]{1,0:T(8,128)(2,1)S(1)}, u32[]{:S(2)}, u32[]{:S(2)}) collective-permute-start(bf16[64,1280]{1,0:T(8,128)(2,1)S(1)} %pad_maximum_fusion), channel_id=1, source_target_pairs={{0,1},{1,0},{2,3},{3,2},{4,5},{5,4},{6,7},{7,6},{8,9},{9,8},{10,11... | collective-permute-start | bytes 491528 | tf_op jit(solution)/shard_map/ppermute | solution.py:31
  34.1 29.4 %copy-start = (s32[256]{0:T(256)S(1)}, s32[256]{0:T(256)}, u32[]{:S(2)}) copy-start(s32[256]{0:T(256)} %param.9) | copy-start | bytes 3076
  34.1 16.3 %all-to-all-start.1 = ((bf16[16,8,1408]{2,1,0:T(8,128)(2,1)}), bf16[16,8,1408]{2,1,0:T(8,128)(2,1)S(1)}, u32[]{:S(2)}, u32[]{:S(2)}) async-start(bf16[16,8,1408]{2,1,0:T(8,128)(2,1)} %bitcast.3), calls=%async_computation.1 | async-start | bytes 720896 | tf_op jit(solution)/shard_map/all_to_all | solution.py:35
  41.2 10.9 %collective-permute-start.5 = (bf16[64,1152]{1,0:T(8,128)(2,1)S(1)}, bf16[64,1152]{1,0:T(8,128)(2,1)S(1)}, u32[]{:S(2)}, u32[]{:S(2)}) collective-permute-start(bf16[64,1152]{1,0:T(8,128)(2,1)S(1)} %get-tuple-element.30), channel_id=1, source_target_pairs={{0,1},{1,0},{2,3},{3,2},{4,5},{5,4},{6,7},{7,6},{8,9},{9,8},{10,11... | collective-permute-start | bytes 442376 | tf_op jit(solution)/shard_map/ppermute | solution.py:31
  50.5 2.4 %collective-permute-start.6 = (f32[8,256]{1,0:T(8,128)S(1)}, f32[8,256]{1,0:T(8,128)S(1)}, u32[]{:S(2)}, u32[]{:S(2)}) collective-permute-start(f32[8,256]{1,0:T(8,128)S(1)} %get-tuple-element.34.totals_ref), channel_id=1, source_target_pairs={{0,1},{1,0},{2,3},{3,2},{4,5},{5,4},{6,7},{7,6},{8,9},{9,8},{10,11... | collective-permute-start | bytes 24584 | tf_op jit(solution)/shard_map/ppermute | solution.py:31
  53.6 14.9 %all-to-all-start.2 = ((bf16[8,8,1664]{2,1,0:T(8,128)(2,1)}), bf16[8,8,1664]{2,1,0:T(8,128)(2,1)S(1)}, u32[]{:S(2)}, u32[]{:S(2)}) async-start(bf16[8,8,1664]{2,1,0:T(8,128)(2,1)} %shard_map.106), calls=%async_computation.2 | async-start | bytes 425984 | tf_op jit(solution)/shard_map/all_to_all | solution.py:35
  58.6 4.9 %collective-permute-start.7 = (f32[1,1152]{1,0:T(1,128)S(1)}, f32[1,1152]{1,0:T(1,128)S(1)}, u32[]{:S(2)}, u32[]{:S(2)}) collective-permute-start(f32[1,1152]{1,0:T(1,128)S(1)} %get-tuple-element.39), channel_id=1, source_target_pairs={{0,1},{1,2},{2,3},{3,4},{4,5},{5,6},{6,7},{7,8},{8,9},{9,10},{10,1... | collective-permute-start | bytes 13832 | tf_op jit(solution)/shard_map/ppermute | solution.py:27

commit v4 on v3

--- a/solution.py
+++ b/solution.py
@@ -13,12 +13,8 @@
 PLANE = (Y, X)
 LANES = 128
 F32, BF16 = jnp.float32, jnp.bfloat16
-SMEM = pl.BlockSpec(memory_space=pltpu.SMEM)
 VMEM = pl.BlockSpec(memory_space=pltpu.VMEM)
 HBM = pl.BlockSpec(memory_space=pltpu.HBM)
-
-STEPS = ((Z, 4), (Z, 2), (Z, 1), (C, 1))
-FROM = (0, 4, 2, 6, 1, 5, 3, 7)
 
 
 def from_behind(value, by):
@@ -56,12 +52,19 @@
     return cells.astype(F32).astype(BF16)
 
 
+def repeat(rows_ref, features, ids):
+    width = features.shape[1]
+    for k in range(rows_ref.shape[0]):
+        rows_ref[k, :, :width] = features
+        rows_ref[k, :, width:] = ids
+
+
 def prepare(
     groups_hbm, ids_hbm, image_hbm, tokens_hbm, gain_hbm,
-    row_ref, unit_ref, norm_ref, pooled_ref, spill_ref, tile_ref, gain_out,
+    rows_ref, unit_ref, norm_ref, pooled_ref, spill_ref, tile_ref, gain_out,
     groups_ref, ids_ref, image_ref, tokens_ref, gain_ref, sems,
 ):
-    pairs, width = image_hbm.shape
+    pairs, _ = image_hbm.shape
     moves = [
         pltpu.make_async_copy(source, target, sems.at[i])
         for i, (source, target) in enumerate(
@@ -80,8 +83,7 @@
     unit = image / norm
     unit_ref[...] = unit
     norm_ref[...] = norm
-    row_ref[:, :width] = unit.astype(BF16)
-    row_ref[:, width:] = id_tile(groups_ref, pairs, False)
+    repeat(rows_ref, unit.astype(BF16), id_tile(groups_ref, pairs, False))
     tile_ref[...] = id_tile(groups_ref, pairs, True)
     moves[4].wait()
     gain_out[...] = gain_ref[...][None, :]
@@ -93,7 +95,7 @@
 
 
 def text_rows(tile_ref, pooled_ref, arrived_ref, gain_ref, rows_ref, unit_ref, norm_ref):
-    pairs, width = pooled_ref.shape
+    pairs, _ = pooled_ref.shape
     last = lax.broadcasted_iota(jnp.int32, (pairs, 1), 0) == pairs - 1
     pooled = pooled_ref[...] + jnp.where(last, arrived_ref[...], 0.0)
     embedded = pooled * gain_ref[...]
@@ -101,23 +103,21 @@
     unit = embedded / norm
     unit_ref[...] = unit
     norm_ref[...] = norm
-    low, ids = unit.astype(BF16), tile_ref[...]
-    for k in range(rows_ref.shape[0]):
-        rows_ref[k, :, :width] = low
-        rows_ref[k, :, width:] = ids
-
-
-def pair_math(log_scale_ref, bias_ref, image_ref, text_ref, gain_ref, text_out, keep_out, send_out):
+    repeat(rows_ref, unit.astype(BF16), tile_ref[...])
+
+
+def pair_math(knobs_ref, near_ref, far_ref, text_ref, gain_ref, text_out, keep_out, send_out):
     width = gain_ref.shape[1]
-    scale = jnp.exp(jnp.full((1, LANES), log_scale_ref[0], F32))[:, :1]
-    image, text = image_ref[:, :width], text_ref[:, :width]
+    scale = jnp.exp(knobs_ref[:, :1])
+    rows = jnp.concatenate([near_ref[...], far_ref[...]], axis=0)
+    image, text = rows[:, :width], text_ref[:, :width]
     contract = (((1,), (1,)), ((), ()))
     scaled = scale * lax.dot_general(image, text, contract, preferred_element_type=F32)
     apart = lax.dot_general(
-        image_ref[:, width:], text_ref[:, width:], contract, preferred_element_type=F32
+        rows[:, width:], text_ref[:, width:], contract, preferred_element_type=F32
     )
     match = apart == 0.0
-    logits = scaled + bias_ref[0]
+    logits = scaled + knobs_ref[:, 1:2]
     margin = jnp.where(match, -logits, logits)
     tail = jnp.exp(-jnp.abs(margin))
     losses = jnp.maximum(margin, 0.0) + jnp.log1p(tail)
@@ -160,7 +160,7 @@
     last_out[...] = grad[pairs - 1 :]
 
 
-def pack(place_ref, keep_ref, came_ref, totals_ref, other_ref, out_ref):
+def pack(keep_ref, came_ref, totals_ref, other_ref, out_ref):
     places, pairs, _ = out_ref.shape
     width = keep_ref.shape[1]
     total = totals_ref[...] + other_ref[...]
@@ -169,10 +169,9 @@
     for k in range(places):
         rows = slice(pairs * k, pairs * (k + 1))
         block = keep_ref[rows] + came_ref[rows].astype(F32)
-        place = place_ref[0] ^ FROM[k]
-        out_ref[place, :, :width] = block.astype(BF16)
-        out_ref[place, :, width : width + 2 * LANES] = high
-        out_ref[place, :, width + 2 * LANES :] = low
+        out_ref[k, :, :width] = block.astype(BF16)
+        out_ref[k, :, width : width + 2 * LANES] = high
+        out_ref[k, :, width + 2 * LANES :] = low
 
 
 def token_rows(ids_ref, grad_ref, behind_ref, token_out):
@@ -217,36 +216,41 @@
     pairs, width = image_emb.shape
     tokens = text_tokens.shape[0]
     total_pairs = pairs * lax.axis_size(DP)
-    plane = lax.axis_size(PLANE)
+    plane, depth = lax.axis_size(PLANE), lax.axis_size(Z)
     wide = width + LANES
     ids = caption_ids[None, :]
-    row, unit_image, image_norm, pooled, spill, tile, gain = local(
+    near, unit_image, image_norm, pooled, spill, tile, gain = local(
         prepare, [HBM] * 5,
-        ((pairs, wide), BF16), ((pairs, width), F32), ((pairs, 1), F32), ((pairs, width), F32), ((1, width), F32),
-        ((pairs, LANES), BF16), ((1, width), F32),
+        ((depth, pairs, wide), BF16), ((pairs, width), F32), ((pairs, 1), F32), ((pairs, width), F32),
+        ((1, width), F32), ((pairs, LANES), BF16), ((1, width), F32),
         scratch=(
             pltpu.SMEM((pairs,), jnp.int32), pltpu.VMEM((1, tokens), jnp.int32),
-            pltpu.VMEM((pairs, width), BF16), pltpu.VMEM((tokens, width), BF16),
-            pltpu.VMEM((width,), F32), pltpu.SemaphoreType.DMA((5,)),
+            pltpu.VMEM((pairs, width), BF16), pltpu.VMEM((tokens, width), BF16), pltpu.VMEM((width,), F32),
+            pltpu.SemaphoreType.DMA((5,)),
         ),
-    )(*(pltpu.with_memory_space_constraint(a, pltpu.HBM) for a in (groups, ids, image_emb, text_tokens, text_gain)))
-
+    )(
+        *(
+            pltpu.with_memory_space_constraint(a, pltpu.HBM)
+            for a in (groups, ids, image_emb, text_tokens, text_gain)
+        )
+    )
+
+    near = to_all(near, Z).reshape(depth * pairs, wide)
     arrived = from_behind(spill, -1)
-    images = row
-    for axis, bit in STEPS:
-        images = jnp.concatenate([images, exchange(images, axis, bit)], axis=0)
-
     rows, unit_text, text_norm = local(
         text_rows, [VMEM] * 4,
         ((plane, pairs, wide), BF16), ((pairs, width), F32), ((pairs, 1), F32),
     )(tile, pooled, arrived, gain)
     texts = to_all(rows, PLANE).reshape(plane * pairs, wide)
 
-    line = images.shape[0]
+    far = exchange(near, C, 1)
+    far, log_scale, logit_bias = lax.optimization_barrier((far, log_scale, logit_bias))
+    lane = lax.broadcasted_iota(jnp.int32, (1, LANES), 1)
+    knobs = jnp.where(lane == 0, log_scale[0], logit_bias[0])
     text_part, keep, send = local(
-        pair_math, [SMEM, SMEM, VMEM, VMEM, VMEM],
-        ((plane * pairs, wide + LANES), BF16), ((line // 2, width), F32), ((line // 2, width), BF16),
-    )(log_scale, logit_bias, images, texts, gain)
+        pair_math, [VMEM] * 5,
+        ((plane * pairs, wide + LANES), BF16), ((depth * pairs, width), F32), ((depth * pairs, width), BF16),
+    )(knobs, near, far, texts, gain)
 
     back = to_all(text_part.reshape(plane, pairs, wide + LANES), PLANE)
     came = exchange(send, C, 1)
@@ -255,10 +259,9 @@
         ((pairs, width), F32), ((1, width), F32), ((pairs, 2 * LANES), F32),
     )(back, unit_text, text_norm, gain)
     other = exchange(totals, C, 1)
-    depth = lax.axis_size(Z)
-    (blocks,) = local(
-        pack, [SMEM, VMEM, VMEM, VMEM, VMEM], ((depth, pairs, width + 4 * LANES), BF16)
-    )(lax.axis_index(Z)[None], keep, came, totals, other)
+    (blocks,) = local(pack, [VMEM] * 4, ((depth, pairs, width + 4 * LANES), BF16))(
+        keep, came, totals, other
+    )
     line_back = to_all(blocks, Z)
     behind = from_behind(last, 1)
     (token_grad,) = local(token_rows, [VMEM] * 3, ((tokens, width), F32))(ids, pooled_grad, behind)

time: 69.7 us -> 69.2 us (level)
  waiting for transfers between devices: 20 us -> 17.4 us
  starting transfers between devices: 40.4 us -> 42 us
    ppermute x6 -> x3, waiting for transfers between devices: 7.25 us -> 0.83 us  [exchange(): lax.ppermute(value, axis, [(i, i ^ bit) for i in range(lax.axis_size(axis...]
    all_to_all x3 -> x4, starting transfers between devices: 18.8 us -> 23 us  [to_all(): return lax.all_to_all(blocks, axes, 0, 0, tiled=True)]
    ppermute x2, waiting for transfers between devices: 0.74 us -> 4.17 us  [from_behind(): return lax.ppermute(value, DP, pairs)]
    ppermute x2, starting transfers between devices: 9.26 us -> 7 us  [from_behind(): return lax.ppermute(value, DP, pairs)]
    all_to_all x3 -> x4, waiting for transfers between devices: 12 us -> 12.4 us  [to_all(): return lax.all_to_all(blocks, axes, 0, 0, tiled=True)]
    ppermute x6 -> x3, starting transfers between devices: 12.3 us -> 12 us  [exchange(): lax.ppermute(value, axis, [(i, i ^ bit) for i in range(lax.axis_size(axis...]
  transfers between devices with their start and end apart: 11 -> 9, of which waited for: 7 -> 7; matrix products, arithmetic and copies ran while one was open for 0% -> 0% of each run, Pallas kernels for 3% -> 4%
where the time goes in v4:
time: 69.2 us; the launch traced here: 68.6 us
  starting transfers between devices  42 us (61%)
  waiting for transfers between devices  17.4 us (25%)
  Pallas kernels  7.23 us (10%)
  between operations  2 us (3%)
    all_to_all x4, starting transfers between devices, to_all(): return lax.all_to_all(blocks, axes, 0, 0, tiled=True)  23 us
    all_to_all x4, waiting for transfers between devices, to_all(): return lax.all_to_all(blocks, axes, 0, 0, tiled=True)  12.4 us
    ppermute x3, starting transfers between devices, exchange(): lax.ppermute(value, axis, [(i, i ^ bit) for i in range(lax.axis_size(axis...  12 us
    ppermute x2, starting transfers between devices, from_behind(): return lax.ppermute(value, DP, pairs)  7 us
    ppermute x2, waiting for transfers between devices, from_behind(): return lax.ppermute(value, DP, pairs)  4.17 us
    pallas_call x1, Pallas kernels, per_device(): local(prepare, [HBM] * 5, ((depth, pairs, wide), BF16), ((pairs, width),...  1.83 us
    pallas_call x1, Pallas kernels, per_device(): local(pair_math, [VMEM] * 5, ((plane * pairs, wide + LANES), BF16), ((dep...  1.53 us
    pallas_call x1, Pallas kernels, per_device(): local(token_rows, [VMEM] * 3, ((tokens, width), F32))  1.43 us
  transfers between devices with their start and end apart: 9, of which 7 were waited for; matrix products, arithmetic and copies ran while one was open for 0% of the time, Pallas kernels for 4%

profile of v4, /device:TPU:1, one launch (start us, length us, event | category | flops | bytes accessed | tf_op | source)
XLA Modules:
  0.0 68.6 jit_solution(9733879995333907132)
XLA Ops:
  0.6 1.8 %shard_map.102 = (bf16[8,8,1280]{2,1,0:T(8,128)(2,1)}, f32[8,1152]{1,0:T(8,128)S(1)}, f32[8,1]{1,0:T(8,128)S(1)}, f32[8,1152]{1,0:T(8,128)S(1)}, f32[1,1152]{1,0...) custom-call(s32[8]{0:T(128)} %groups_hbm.1, s32[1,256]{1,0:T(1,128)} %bitcast.11, ...), custom_call_target="tpu_custom_call" | custom-call | tf_op jit(solution)/shard_map/pallas_call | solution.py:222
  2.5 9.0 %all-to-all-start = ((bf16[8,8,1280]{2,1,0:T(8,128)(2,1)}), bf16[8,8,1280]{2,1,0:T(8,128)(2,1)S(1)}, u32[]{:S(2)}, u32[]{:S(2)}) async-start(bf16[8,8,1280]{2,1,0:T(8,128)(2,1)} %get-tuple-element.26), calls=%async_computation | async-start | bytes 327680 | tf_op jit(solution)/shard_map/all_to_all | solution.py:31
  11.5 2.9 %collective-permute-start.1 = (f32[1,1152]{1,0:T(1,128)S(1)}, f32[1,1152]{1,0:T(1,128)S(1)}, u32[]{:S(2)}, u32[]{:S(2)}) collective-permute-start(f32[1,1152]{1,0:T(1,128)S(1)} %get-tuple-element.32), channel_id=1, source_target_pairs={{1,0},{2,1},{3,2},{4,3},{5,4},{6,5},{7,6},{8,7},{9,8},{10,9},{11,1... | collective-permute-start | bytes 13832 | tf_op jit(solution)/shard_map/ppermute | solution.py:23
  14.3 3.4 %collective-permute-done.1.arrived_ref = f32[1,1152]{1,0:T(1,128)S(1)} collective-permute-done((f32[1,1152]{1,0:T(1,128)S(1)}, f32[1,1152]{1,0:T(1,128)S(1)}, u32[]{:S(2)}, u32[]{:S(2)}) %collective-permute-start.1) | collective-permute-done | bytes 4640 | tf_op jit(solution)/shard_map/ppermute | solution.py:23
  17.8 0.9 %shard_map.103 = (bf16[16,8,1280]{2,1,0:T(8,128)(2,1)}, f32[8,1152]{1,0:T(8,128)S(1)}, f32[8,1]{1,0:T(8,128)S(1)}) custom-call(bf16[8,128]{1,0:T(8,128)(2,1)S(1)} %get-tuple-element.30.tile_ref, f32[8,1152]{1,0:T(8,128)S(1)} %get-tuple-element.31.pooled_ref, f32[1,1152]{1,0:T(1,128)S(1)} %collective-permute-done.1.arrived_ref, ...), custom_call_target="tpu_custom_call" | custom-call | tf_op jit(solution)/shard_map/pallas_call | solution.py:240
  18.6 1.1 %all-to-all-done = bf16[8,8,1280]{2,1,0:T(8,128)(2,1)S(1)} async-done(((bf16[8,8,1280]{2,1,0:T(8,128)(2,1)}), bf16[8,8,1280]{2,1,0:T(8,128)(2,1)S(1)}, u32[]{:S(2)}, u32[]{:S(2)}) %all-to-all-start) | async-done | bytes 163872 | tf_op jit(solution)/shard_map/all_to_all | solution.py:31
  19.7 6.8 %all-to-all-start.1 = ((bf16[16,8,1280]{2,1,0:T(8,128)(2,1)}), bf16[16,8,1280]{2,1,0:T(8,128)(2,1)S(1)}, u32[]{:S(2)}, u32[]{:S(2)}) async-start(bf16[16,8,1280]{2,1,0:T(8,128)(2,1)} %get-tuple-element.34), calls=%async_computation.1 | async-start | bytes 655360 | tf_op jit(solution)/shard_map/all_to_all | solution.py:31
  26.5 2.9 %collective-permute-start = (bf16[64,1280]{1,0:T(8,128)(2,1)S(1)}, bf16[64,1280]{1,0:T(8,128)(2,1)S(1)}, u32[]{:S(2)}, u32[]{:S(2)}) collective-permute-start(bf16[64,1280]{1,0:T(8,128)(2,1)S(1)} %bitcast.9), channel_id=1, source_target_pairs={{0,1},{1,0},{2,3},{3,2},{4,5},{5,4},{6,7},{7,6},{8,9},{9,8},{10,11... | collective-permute-start | bytes 491528 | tf_op jit(solution)/shard_map/ppermute | solution.py:27
  30.6 0.0 collective-permute-done.far_ref
  30.7 3.7 %all-to-all-done.1 = bf16[16,8,1280]{2,1,0:T(8,128)(2,1)S(1)} async-done(((bf16[16,8,1280]{2,1,0:T(8,128)(2,1)}), bf16[16,8,1280]{2,1,0:T(8,128)(2,1)S(1)}, u32[]{:S(2)}, u32[]{:S(2)}) %all-to-all-start.1) | async-done | bytes 327712 | tf_op jit(solution)/shard_map/all_to_all | solution.py:31
  34.4 1.5 %shard_map.104 = (bf16[128,1408]{1,0:T(8,128)(2,1)}, f32[64,1152]{1,0:T(8,128)S(1)}, bf16[64,1152]{1,0:T(8,128)(2,1)S(1)}) custom-call(f32[1,128]{1,0:T(1,128)S(1)} %compare_select_fusion.knobs_ref, bf16[64,1280]{1,0:T(8,128)(2,1)S(1)} %bitcast.10, bf16[64,1280]{1,0:T(8,128)(2,1)S(1)} %collective-permute-done.far_ref, bf16[128,1280]{1,0:T(8,128)(2,1)S(1)} %bitcast.8, ...), custom_call_target="tpu_custom_call" | custom-call | tf_op jit(solution)/shard_map/pallas_call | solution.py:250
  35.9 0.0 copy-start
  35.9 3.7 %all-to-all-start.2 = ((bf16[16,8,1408]{2,1,0:T(8,128)(2,1)}), bf16[16,8,1408]{2,1,0:T(8,128)(2,1)S(1)}, u32[]{:S(2)}, u32[]{:S(2)}) async-start(bf16[16,8,1408]{2,1,0:T(8,128)(2,1)} %bitcast.5), calls=%async_computation.2 | async-start | bytes 720896 | tf_op jit(solution)/shard_map/all_to_all | solution.py:31
  39.6 4.0 %collective-permute-start.2 = (bf16[64,1152]{1,0:T(8,128)(2,1)S(1)}, bf16[64,1152]{1,0:T(8,128)(2,1)S(1)}, u32[]{:S(2)}, u32[]{:S(2)}) collective-permute-start(bf16[64,1152]{1,0:T(8,128)(2,1)S(1)} %get-tuple-element.36), channel_id=1, source_target_pairs={{0,1},{1,0},{2,3},{3,2},{4,5},{5,4},{6,7},{7,6},{8,9},{9,8},{10,11... | collective-permute-start | bytes 442376 | tf_op jit(solution)/shard_map/ppermute | solution.py:27
  43.6 4.0 %all-to-all-done.2.back_ref = bf16[16,8,1408]{2,1,0:T(8,128)(2,1)S(1)} async-done(((bf16[16,8,1408]{2,1,0:T(8,128)(2,1)}), bf16[16,8,1408]{2,1,0:T(8,128)(2,1)S(1)}, u32[]{:S(2)}, u32[]{:S(2)}) %all-to-all-start.2) | async-done | bytes 360480 | tf_op jit(solution)/shard_map/all_to_all | solution.py:31
  47.6 0.1 shard_map.105
  47.8 5.1 %collective-permute-start.3 = (f32[8,256]{1,0:T(8,128)S(1)}, f32[8,256]{1,0:T(8,128)S(1)}, u32[]{:S(2)}, u32[]{:S(2)}) collective-permute-start(f32[8,256]{1,0:T(8,128)S(1)} %get-tuple-element.40.totals_ref), channel_id=1, source_target_pairs={{0,1},{1,0},{2,3},{3,2},{4,5},{5,4},{6,7},{7,6},{8,9},{9,8},{10,11... | collective-permute-start | bytes 24584 | tf_op jit(solution)/shard_map/ppermute | solution.py:27
  52.9 0.0 collective-permute-done.2.came_ref
  52.9 0.8 %collective-permute-done.3.other_ref = f32[8,256]{1,0:T(8,128)S(1)} collective-permute-done((f32[8,256]{1,0:T(8,128)S(1)}, f32[8,256]{1,0:T(8,128)S(1)}, u32[]{:S(2)}, u32[]{:S(2)}) %collective-permute-start.3) | collective-permute-done | bytes 8224 | tf_op jit(solution)/shard_map/ppermute | solution.py:27
  53.8 0.7 %shard_map.106 = bf16[8,8,1664]{2,1,0:T(8,128)(2,1)} custom-call(f32[64,1152]{1,0:T(8,128)S(1)} %get-tuple-element.35.keep_ref, bf16[64,1152]{1,0:T(8,128)(2,1)S(1)} %collective-permute-done.2.came_ref, f32[8,256]{1,0:T(8,128)S(1)} %get-tuple-element.40.totals_ref, f32[8,256]{1,0:T(8,128)S(1)} %collective-permute-done.3.other_ref), custom_call_target="tpu_custom_call" | custom-call | tf_op jit(solution)/shard_map/pallas_call | solution.py:262
  54.5 3.6 %all-to-all-start.3 = ((bf16[8,8,1664]{2,1,0:T(8,128)(2,1)}), bf16[8,8,1664]{2,1,0:T(8,128)(2,1)S(1)}, u32[]{:S(2)}, u32[]{:S(2)}) async-start(bf16[8,8,1664]{2,1,0:T(8,128)(2,1)} %shard_map.106), calls=%async_computation.3 | async-start | bytes 425984 | tf_op jit(solution)/shard_map/all_to_all | solution.py:31
  58.1 4.1 %collective-permute-start.4 = (f32[1,1152]{1,0:T(1,128)S(1)}, f32[1,1152]{1,0:T(1,128)S(1)}, u32[]{:S(2)}, u32[]{:S(2)}) collective-permute-start(f32[1,1152]{1,0:T(1,128)S(1)} %get-tuple-element.45), channel_id=1, source_target_pairs={{0,1},{1,2},{2,3},{3,4},{4,5},{5,6},{6,7},{7,8},{8,9},{9,10},{10,1... | collective-permute-start | bytes 13832 | tf_op jit(solution)/shard_map/ppermute | solution.py:23
  62.2 0.7 %collective-permute-done.4.behind_ref = f32[1,1152]{1,0:T(1,128)S(1)} collective-permute-done((f32[1,1152]{1,0:T(1,128)S(1)}, f32[1,1152]{1,0:T(1,128)S(1)}, u32[]{:S(2)}, u32[]{:S(2)}) %collective-permute-start.4) | collective-permute-done | bytes 4640 | tf_op jit(solution)/shard_map/ppermute | solution.py:23
  63.0 0.0 copy-done
  63.0 1.4 %shard_map.108 = f32[256,1152]{1,0:T(8,128)} custom-call(s32[1,256]{1,0:T(1,128)S(1)} %bitcast.12, f32[8,1152]{1,0:T(8,128)S(1)} %get-tuple-element.44.grad_ref, f32[1,1152]{1,0:T(1,128)S(1)} %collective-permute-done.4.behind_ref), custom_call_target="tpu_custom_call" | custom-call | tf_op jit(solution)/shard_map/pallas_call | solution.py:267
  64.4 3.5 %all-to-all-done.3.back_ref = bf16[8,8,1664]{2,1,0:T(8,128)(2,1)S(1)} async-done(((bf16[8,8,1664]{2,1,0:T(8,128)(2,1)}), bf16[8,8,1664]{2,1,0:T(8,128)(2,1)S(1)}, u32[]{:S(2)}, u32[]{:S(2)}) %all-to-all-start.3) | async-done | bytes 213024 | tf_op jit(solution)/shard_map/all_to_all | solution.py:31
  67.9 0.7 %shard_map.107 = (f32[8,1152]{1,0:T(8,128)}, f32[1152]{0:T(1024)}, f32[3]{0:T(128)}) custom-call(bf16[8,8,1664]{2,1,0:T(8,128)(2,1)S(1)} %all-to-all-done.3.back_ref, f32[8,1152]{1,0:T(8,128)S(1)} %get-tuple-element.41.unit_ref, f32[8,1]{1,0:T(8,128)S(1)} %get-tuple-element.42.norm_ref), custom_call_target="tpu_custom_call" | custom-call | tf_op jit(solution)/shard_map/pallas_call | solution.py:268
  (1 shorter events, 0.0 us)
Async XLA Ops:
  2.5 17.2 %all-to-all-start = ((bf16[8,8,1280]{2,1,0:T(8,128)(2,1)}), bf16[8,8,1280]{2,1,0:T(8,128)(2,1)S(1)}, u32[]{:S(2)}, u32[]{:S(2)}) async-start(bf16[8,8,1280]{2,1,0:T(8,128)(2,1)} %get-tuple-element.26), calls=%async_computation | async-start | bytes 327680 | tf_op jit(solution)/shard_map/all_to_all | solution.py:31
  11.5 6.3 %collective-permute-start.1 = (f32[1,1152]{1,0:T(1,128)S(1)}, f32[1,1152]{1,0:T(1,128)S(1)}, u32[]{:S(2)}, u32[]{:S(2)}) collective-permute-start(f32[1,1152]{1,0:T(1,128)S(1)} %get-tuple-element.32), channel_id=1, source_target_pairs={{1,0},{2,1},{3,2},{4,3},{5,4},{6,5},{7,6},{8,7},{9,8},{10,9},{11,1... | collective-permute-start | bytes 13832 | tf_op jit(solution)/shard_map/ppermute | solution.py:23
  19.7 14.7 %all-to-all-start.1 = ((bf16[16,8,1280]{2,1,0:T(8,128)(2,1)}), bf16[16,8,1280]{2,1,0:T(8,128)(2,1)S(1)}, u32[]{:S(2)}, u32[]{:S(2)}) async-start(bf16[16,8,1280]{2,1,0:T(8,128)(2,1)} %get-tuple-element.34), calls=%async_computation.1 | async-start | bytes 655360 | tf_op jit(solution)/shard_map/all_to_all | solution.py:31
  26.5 4.2 %collective-permute-start = (bf16[64,1280]{1,0:T(8,128)(2,1)S(1)}, bf16[64,1280]{1,0:T(8,128)(2,1)S(1)}, u32[]{:S(2)}, u32[]{:S(2)}) collective-permute-start(bf16[64,1280]{1,0:T(8,128)(2,1)S(1)} %bitcast.9), channel_id=1, source_target_pairs={{0,1},{1,0},{2,3},{3,2},{4,5},{5,4},{6,7},{7,6},{8,9},{9,8},{10,11... | collective-permute-start | bytes 491528 | tf_op jit(solution)/shard_map/ppermute | solution.py:27
  35.9 27.0 %copy-start = (s32[256]{0:T(256)S(1)}, s32[256]{0:T(256)}, u32[]{:S(2)}) copy-start(s32[256]{0:T(256)} %param.9) | copy-start | bytes 3076
  35.9 11.7 %all-to-all-start.2 = ((bf16[16,8,1408]{2,1,0:T(8,128)(2,1)}), bf16[16,8,1408]{2,1,0:T(8,128)(2,1)S(1)}, u32[]{:S(2)}, u32[]{:S(2)}) async-start(bf16[16,8,1408]{2,1,0:T(8,128)(2,1)} %bitcast.5), calls=%async_computation.2 | async-start | bytes 720896 | tf_op jit(solution)/shard_map/all_to_all | solution.py:31
  39.6 13.3 %collective-permute-start.2 = (bf16[64,1152]{1,0:T(8,128)(2,1)S(1)}, bf16[64,1152]{1,0:T(8,128)(2,1)S(1)}, u32[]{:S(2)}, u32[]{:S(2)}) collective-permute-start(bf16[64,1152]{1,0:T(8,128)(2,1)S(1)} %get-tuple-element.36), channel_id=1, source_target_pairs={{0,1},{1,0},{2,3},{3,2},{4,5},{5,4},{6,7},{7,6},{8,9},{9,8},{10,11... | collective-permute-start | bytes 442376 | tf_op jit(solution)/shard_map/ppermute | solution.py:27
  47.8 6.0 %collective-permute-start.3 = (f32[8,256]{1,0:T(8,128)S(1)}, f32[8,256]{1,0:T(8,128)S(1)}, u32[]{:S(2)}, u32[]{:S(2)}) collective-permute-start(f32[8,256]{1,0:T(8,128)S(1)} %get-tuple-element.40.totals_ref), channel_id=1, source_target_pairs={{0,1},{1,0},{2,3},{3,2},{4,5},{5,4},{6,7},{7,6},{8,9},{9,8},{10,11... | collective-permute-start | bytes 24584 | tf_op jit(solution)/shard_map/ppermute | solution.py:27
  54.5 13.4 %all-to-all-start.3 = ((bf16[8,8,1664]{2,1,0:T(8,128)(2,1)}), bf16[8,8,1664]{2,1,0:T(8,128)(2,1)S(1)}, u32[]{:S(2)}, u32[]{:S(2)}) async-start(bf16[8,8,1664]{2,1,0:T(8,128)(2,1)} %shard_map.106), calls=%async_computation.3 | async-start | bytes 425984 | tf_op jit(solution)/shard_map/all_to_all | solution.py:31
  58.1 4.9 %collective-permute-start.4 = (f32[1,1152]{1,0:T(1,128)S(1)}, f32[1,1152]{1,0:T(1,128)S(1)}, u32[]{:S(2)}, u32[]{:S(2)}) collective-permute-start(f32[1,1152]{1,0:T(1,128)S(1)} %get-tuple-element.45), channel_id=1, source_target_pairs={{0,1},{1,2},{2,3},{3,4},{4,5},{5,6},{6,7},{7,8},{8,9},{9,10},{10,1... | collective-permute-start | bytes 13832 | tf_op jit(solution)/shard_map/ppermute | solution.py:23

commit v5 on v4

--- a/solution.py
+++ b/solution.py
@@ -14,7 +14,10 @@
 LANES = 128
 F32, BF16 = jnp.float32, jnp.bfloat16
 VMEM = pl.BlockSpec(memory_space=pltpu.VMEM)
+SMEM = pl.BlockSpec(memory_space=pltpu.SMEM)
 HBM = pl.BlockSpec(memory_space=pltpu.HBM)
+
+FROM = (0, 2, 4, 6, 1, 3, 5, 7)
 
 
 def from_behind(value, by):
@@ -52,19 +55,12 @@
     return cells.astype(F32).astype(BF16)
 
 
-def repeat(rows_ref, features, ids):
-    width = features.shape[1]
-    for k in range(rows_ref.shape[0]):
-        rows_ref[k, :, :width] = features
-        rows_ref[k, :, width:] = ids
-
-
 def prepare(
     groups_hbm, ids_hbm, image_hbm, tokens_hbm, gain_hbm,
-    rows_ref, unit_ref, norm_ref, pooled_ref, spill_ref, tile_ref, gain_out,
+    row_ref, unit_ref, norm_ref, pooled_ref, spill_ref, tile_ref, gain_out,
     groups_ref, ids_ref, image_ref, tokens_ref, gain_ref, sems,
 ):
-    pairs, _ = image_hbm.shape
+    pairs, width = image_hbm.shape
     moves = [
         pltpu.make_async_copy(source, target, sems.at[i])
         for i, (source, target) in enumerate(
@@ -83,7 +79,8 @@
     unit = image / norm
     unit_ref[...] = unit
     norm_ref[...] = norm
-    repeat(rows_ref, unit.astype(BF16), id_tile(groups_ref, pairs, False))
+    row_ref[:, :width] = unit.astype(BF16)
+    row_ref[:, width:] = id_tile(groups_ref, pairs, False)
     tile_ref[...] = id_tile(groups_ref, pairs, True)
     moves[4].wait()
     gain_out[...] = gain_ref[...][None, :]
@@ -95,7 +92,7 @@
 
 
 def text_rows(tile_ref, pooled_ref, arrived_ref, gain_ref, rows_ref, unit_ref, norm_ref):
-    pairs, _ = pooled_ref.shape
+    pairs, width = pooled_ref.shape
     last = lax.broadcasted_iota(jnp.int32, (pairs, 1), 0) == pairs - 1
     pooled = pooled_ref[...] + jnp.where(last, arrived_ref[...], 0.0)
     embedded = pooled * gain_ref[...]
@@ -103,7 +100,10 @@
     unit = embedded / norm
     unit_ref[...] = unit
     norm_ref[...] = norm
-    repeat(rows_ref, unit.astype(BF16), tile_ref[...])
+    low, ids = unit.astype(BF16), tile_ref[...]
+    for k in range(rows_ref.shape[0]):
+        rows_ref[k, :, :width] = low
+        rows_ref[k, :, width:] = ids
 
 
 def pair_math(knobs_ref, near_ref, far_ref, text_ref, gain_ref, text_out, keep_out, send_out):
@@ -160,7 +160,7 @@
     last_out[...] = grad[pairs - 1 :]
 
 
-def pack(keep_ref, came_ref, totals_ref, other_ref, out_ref):
+def pack(place_ref, keep_ref, came_ref, totals_ref, other_ref, out_ref):
     places, pairs, _ = out_ref.shape
     width = keep_ref.shape[1]
     total = totals_ref[...] + other_ref[...]
@@ -169,9 +169,10 @@
     for k in range(places):
         rows = slice(pairs * k, pairs * (k + 1))
         block = keep_ref[rows] + came_ref[rows].astype(F32)
-        out_ref[k, :, :width] = block.astype(BF16)
-        out_ref[k, :, width : width + 2 * LANES] = high
-        out_ref[k, :, width + 2 * LANES :] = low
+        place = place_ref[0] ^ FROM[k]
+        out_ref[place, :, :width] = block.astype(BF16)
+        out_ref[place, :, width : width + 2 * LANES] = high
+        out_ref[place, :, width + 2 * LANES :] = low
 
 
 def token_rows(ids_ref, grad_ref, behind_ref, token_out):
@@ -219,9 +220,9 @@
     plane, depth = lax.axis_size(PLANE), lax.axis_size(Z)
     wide = width + LANES
     ids = caption_ids[None, :]
-    near, unit_image, image_norm, pooled, spill, tile, gain = local(
+    row, unit_image, image_norm, pooled, spill, tile, gain = local(
         prepare, [HBM] * 5,
-        ((depth, pairs, wide), BF16), ((pairs, width), F32), ((pairs, 1), F32), ((pairs, width), F32),
+        ((pairs, wide), BF16), ((pairs, width), F32), ((pairs, 1), F32), ((pairs, width), F32),
         ((1, width), F32), ((pairs, LANES), BF16), ((1, width), F32),
         scratch=(
             pltpu.SMEM((pairs,), jnp.int32), pltpu.VMEM((1, tokens), jnp.int32),
@@ -235,8 +236,12 @@
         )
     )
 
-    near = to_all(near, Z).reshape(depth * pairs, wide)
     arrived = from_behind(spill, -1)
+    near = [row]
+    for step in FROM[1:4]:
+        near.append(exchange(row, Z, step))
+    near = jnp.concatenate(near, axis=0)
+    near = jnp.concatenate([near, exchange(near, Z, 1)], axis=0)
     rows, unit_text, text_norm = local(
         text_rows, [VMEM] * 4,
         ((plane, pairs, wide), BF16), ((pairs, width), F32), ((pairs, 1), F32),
@@ -259,8 +264,8 @@
         ((pairs, width), F32), ((1, width), F32), ((pairs, 2 * LANES), F32),
     )(back, unit_text, text_norm, gain)
     other = exchange(totals, C, 1)
-    (blocks,) = local(pack, [VMEM] * 4, ((depth, pairs, width + 4 * LANES), BF16))(
-        keep, came, totals, other
+    (blocks,) = local(pack, [SMEM] + [VMEM] * 4, ((depth, pairs, width + 4 * LANES), BF16))(
+        lax.axis_index(Z)[None], keep, came, totals, other
     )
     line_back = to_all(blocks, Z)
     behind = from_behind(last, 1)

time: 69.2 us -> 68.6 us (level)
  starting transfers between devices: 42 us -> 40.2 us
  waiting for transfers between devices: 17.4 us -> 19.1 us
    all_to_all x4 -> x3, starting transfers between devices: 23 us -> 18.3 us  [to_all(): return lax.all_to_all(blocks, axes, 0, 0, tiled=True)]
    ppermute x3 -> x7, starting transfers between devices: 12 us -> 14.6 us  [exchange(): lax.ppermute(value, axis, [(i, i ^ bit) for i in range(lax.axis_size(axis...]
    ppermute x3 -> x7, waiting for transfers between devices: 0.83 us -> 3.4 us  [exchange(): lax.ppermute(value, axis, [(i, i ^ bit) for i in range(lax.axis_size(axis...]
    ppermute x2, waiting for transfers between devices: 4.17 us -> 2.93 us  [from_behind(): return lax.ppermute(value, DP, pairs)]
    all_to_all x4 -> x3, waiting for transfers between devices: 12.4 us -> 12.8 us  [to_all(): return lax.all_to_all(blocks, axes, 0, 0, tiled=True)]
  transfers between devices with their start and end apart: 9 -> 12, of which waited for: 7 -> 7; matrix products, arithmetic and copies ran while one was open for 0% -> 0% of each run, Pallas kernels for 4% -> 4%
where the time goes in v5:
time: 68.6 us; the launch traced here: 68.1 us
  starting transfers between devices  40.2 us (59%)
  waiting for transfers between devices  19.1 us (28%)
  Pallas kernels  6.77 us (10%)
  between operations  2.04 us (3%)
    all_to_all x3, starting transfers between devices, to_all(): return lax.all_to_all(blocks, axes, 0, 0, tiled=True)  18.3 us
    ppermute x7, starting transfers between devices, exchange(): lax.ppermute(value, axis, [(i, i ^ bit) for i in range(lax.axis_size(axis...  14.6 us
    all_to_all x3, waiting for transfers between devices, to_all(): return lax.all_to_all(blocks, axes, 0, 0, tiled=True)  12.8 us
    ppermute x2, starting transfers between devices, from_behind(): return lax.ppermute(value, DP, pairs)  7.28 us
    ppermute x7, waiting for transfers between devices, exchange(): lax.ppermute(value, axis, [(i, i ^ bit) for i in range(lax.axis_size(axis...  3.4 us
    ppermute x2, waiting for transfers between devices, from_behind(): return lax.ppermute(value, DP, pairs)  2.93 us
    pallas_call x1, Pallas kernels, per_device(): local(pair_math, [VMEM] * 5, ((plane * pairs, wide + LANES), BF16), ((dep...  1.53 us
    pallas_call x1, Pallas kernels, per_device(): local(token_rows, [VMEM] * 3, ((tokens, width), F32))  1.43 us
  transfers between devices with their start and end apart: 12, of which 7 were waited for; matrix products, arithmetic and copies ran while one was open for 0% of the time, Pallas kernels for 4%

profile of v5, /device:TPU:1, one launch (start us, length us, event | category | flops | bytes accessed | tf_op | source)
XLA Modules:
  0.0 68.1 jit_solution(15014474432873085167)
XLA Ops:
  0.6 1.4 %shard_map.102 = (bf16[8,1280]{1,0:T(8,128)(2,1)S(1)}, f32[8,1152]{1,0:T(8,128)S(1)}, f32[8,1]{1,0:T(8,128)S(1)}, f32[8,1152]{1,0:T(8,128)S(1)}, f32[1,1152]{1,0...) custom-call(s32[8]{0:T(128)} %groups_hbm.1, s32[1,256]{1,0:T(1,128)} %bitcast.9, ...), custom_call_target="tpu_custom_call" | custom-call | tf_op jit(solution)/shard_map/pallas_call | solution.py:223
  2.0 6.9 %collective-permute-start.2 = (bf16[8,1280]{1,0:T(8,128)(2,1)S(1)}, bf16[8,1280]{1,0:T(8,128)(2,1)S(1)}, u32[]{:S(2)}, u32[]{:S(2)}) collective-permute-start(bf16[8,1280]{1,0:T(8,128)(2,1)S(1)} %get-tuple-element.26), channel_id=1, source_target_pairs={{0,12},{2,14},{4,8},{6,10},{8,4},{10,6},{12,0},{14,2},{1,13},{3,15... | collective-permute-start | bytes 61448 | tf_op jit(solution)/shard_map/ppermute | solution.py:30
  8.9 1.0 %collective-permute-start.1 = (bf16[8,1280]{1,0:T(8,128)(2,1)S(1)}, bf16[8,1280]{1,0:T(8,128)(2,1)S(1)}, u32[]{:S(2)}, u32[]{:S(2)}) collective-permute-start(bf16[8,1280]{1,0:T(8,128)(2,1)S(1)} %get-tuple-element.26), channel_id=1, source_target_pairs={{0,8},{2,10},{4,12},{6,14},{8,0},{10,2},{12,4},{14,6},{1,9},{3,11}... | collective-permute-start | bytes 61448 | tf_op jit(solution)/shard_map/ppermute | solution.py:30
  9.9 1.2 %collective-permute-start = (bf16[8,1280]{1,0:T(8,128)(2,1)S(1)}, bf16[8,1280]{1,0:T(8,128)(2,1)S(1)}, u32[]{:S(2)}, u32[]{:S(2)}) collective-permute-start(bf16[8,1280]{1,0:T(8,128)(2,1)S(1)} %get-tuple-element.26), channel_id=1, source_target_pairs={{0,4},{2,6},{4,0},{6,2},{8,12},{10,14},{12,8},{14,10},{1,5},{3,7},... | collective-permute-start | bytes 61448 | tf_op jit(solution)/shard_map/ppermute | solution.py:30
  11.1 3.1 %collective-permute-start.5 = (f32[1,1152]{1,0:T(1,128)S(1)}, f32[1,1152]{1,0:T(1,128)S(1)}, u32[]{:S(2)}, u32[]{:S(2)}) collective-permute-start(f32[1,1152]{1,0:T(1,128)S(1)} %get-tuple-element.32), channel_id=1, source_target_pairs={{1,0},{2,1},{3,2},{4,3},{5,4},{6,5},{7,6},{8,7},{9,8},{10,9},{11,1... | collective-permute-start | bytes 13832 | tf_op jit(solution)/shard_map/ppermute | solution.py:26
  14.3 2.2 %collective-permute-done.5.arrived_ref = f32[1,1152]{1,0:T(1,128)S(1)} collective-permute-done((f32[1,1152]{1,0:T(1,128)S(1)}, f32[1,1152]{1,0:T(1,128)S(1)}, u32[]{:S(2)}, u32[]{:S(2)}) %collective-permute-start.5) | collective-permute-done | bytes 4640 | tf_op jit(solution)/shard_map/ppermute | solution.py:26
  16.5 0.9 %shard_map.103 = (bf16[16,8,1280]{2,1,0:T(8,128)(2,1)}, f32[8,1152]{1,0:T(8,128)S(1)}, f32[8,1]{1,0:T(8,128)S(1)}) custom-call(bf16[8,128]{1,0:T(8,128)(2,1)S(1)} %get-tuple-element.30.tile_ref, f32[8,1152]{1,0:T(8,128)S(1)} %get-tuple-element.31.pooled_ref, f32[1,1152]{1,0:T(1,128)S(1)} %collective-permute-done.5.arrived_ref, ...), custom_call_target="tpu_custom_call" | custom-call | tf_op jit(solution)/shard_map/pallas_call | solution.py:245
  17.3 6.8 %all-to-all-start = ((bf16[16,8,1280]{2,1,0:T(8,128)(2,1)}), bf16[16,8,1280]{2,1,0:T(8,128)(2,1)S(1)}, u32[]{:S(2)}, u32[]{:S(2)}) async-start(bf16[16,8,1280]{2,1,0:T(8,128)(2,1)} %get-tuple-element.34), calls=%async_computation | async-start | bytes 655360 | tf_op jit(solution)/shard_map/all_to_all | solution.py:34
  24.1 0.0 collective-permute-done.2
  24.1 0.0 collective-permute-done.1
  24.1 0.0 collective-permute-done
  24.1 0.8 %collective-permute-start.3 = (bf16[32,1280]{1,0:T(8,128)(2,1)S(1)}, bf16[32,1280]{1,0:T(8,128)(2,1)S(1)}, u32[]{:S(2)}, u32[]{:S(2)}) collective-permute-start(bf16[32,1280]{1,0:T(8,128)(2,1)S(1)} %pad_maximum_fusion), channel_id=1, source_target_pairs={{0,2},{2,0},{4,6},{6,4},{8,10},{10,8},{12,14},{14,12},{1,3},{3,1},... | collective-permute-start | bytes 245768 | tf_op jit(solution)/shard_map/ppermute | solution.py:30
  25.0 2.6 %collective-permute-done.3 = bf16[32,1280]{1,0:T(8,128)(2,1)S(1)} collective-permute-done((bf16[32,1280]{1,0:T(8,128)(2,1)S(1)}, bf16[32,1280]{1,0:T(8,128)(2,1)S(1)}, u32[]{:S(2)}, u32[]{:S(2)}) %collective-permute-start.3) | collective-permute-done | bytes 81952 | tf_op jit(solution)/shard_map/ppermute | solution.py:30
  27.5 2.7 %collective-permute-start.4 = (bf16[64,1280]{1,0:T(8,128)(2,1)S(1)}, bf16[64,1280]{1,0:T(8,128)(2,1)S(1)}, u32[]{:S(2)}, u32[]{:S(2)}) collective-permute-start(bf16[64,1280]{1,0:T(8,128)(2,1)S(1)} %constant_dynamic-update-slice_fusion.near_ref), channel_id=1, source_target_pairs={{0,1},{1,0},{2,3},{3,2},{4,5},{5,4},{6,7},{7,6},{8,9},{9,8},{10,11... | collective-permute-start | bytes 491528 | tf_op jit(solution)/shard_map/ppermute | solution.py:30
  31.6 0.0 collective-permute-done.4.far_ref
  31.6 0.5 all-to-all-done
  32.0 1.5 %shard_map.104 = (bf16[128,1408]{1,0:T(8,128)(2,1)}, f32[64,1152]{1,0:T(8,128)S(1)}, bf16[64,1152]{1,0:T(8,128)(2,1)S(1)}) custom-call(f32[1,128]{1,0:T(1,128)S(1)} %compare_select_fusion.knobs_ref, bf16[64,1280]{1,0:T(8,128)(2,1)S(1)} %constant_dynamic-update-slice_fusion.near_ref, bf16[64,1280]{1,0:T(8,128)(2,1)S(1)} %collective-permute-done.4.far_ref, ...), custom_call_target="tpu_custom_call" | custom-call | tf_op jit(solution)/shard_map/pallas_call | solution.py:255
  33.6 6.6 %all-to-all-start.1 = ((bf16[16,8,1408]{2,1,0:T(8,128)(2,1)}), bf16[16,8,1408]{2,1,0:T(8,128)(2,1)S(1)}, u32[]{:S(2)}, u32[]{:S(2)}) async-start(bf16[16,8,1408]{2,1,0:T(8,128)(2,1)} %bitcast.5), calls=%async_computation.1 | async-start | bytes 720896 | tf_op jit(solution)/shard_map/all_to_all | solution.py:34
  40.2 0.4 collective-permute-start.6
  40.6 8.8 %all-to-all-done.1.back_ref = bf16[16,8,1408]{2,1,0:T(8,128)(2,1)S(1)} async-done(((bf16[16,8,1408]{2,1,0:T(8,128)(2,1)}), bf16[16,8,1408]{2,1,0:T(8,128)(2,1)S(1)}, u32[]{:S(2)}, u32[]{:S(2)}) %all-to-all-start.1) | async-done | bytes 360480 | tf_op jit(solution)/shard_map/all_to_all | solution.py:34
  49.4 0.1 shard_map.105
  49.6 1.5 %collective-permute-start.7 = (f32[8,256]{1,0:T(8,128)S(1)}, f32[8,256]{1,0:T(8,128)S(1)}, u32[]{:S(2)}, u32[]{:S(2)}) collective-permute-start(f32[8,256]{1,0:T(8,128)S(1)} %get-tuple-element.40.totals_ref), channel_id=1, source_target_pairs={{0,1},{1,0},{2,3},{3,2},{4,5},{5,4},{6,7},{7,6},{8,9},{9,8},{10,11... | collective-permute-start | bytes 24584 | tf_op jit(solution)/shard_map/ppermute | solution.py:30
  51.1 0.0 collective-permute-done.6.came_ref
  51.1 0.8 %collective-permute-done.7.other_ref = f32[8,256]{1,0:T(8,128)S(1)} collective-permute-done((f32[8,256]{1,0:T(8,128)S(1)}, f32[8,256]{1,0:T(8,128)S(1)}, u32[]{:S(2)}, u32[]{:S(2)}) %collective-permute-start.7) | collective-permute-done | bytes 8224 | tf_op jit(solution)/shard_map/ppermute | solution.py:30
  51.9 0.7 %shard_map.106 = bf16[8,8,1664]{2,1,0:T(8,128)(2,1)} custom-call(s32[1]{0:T(128)} %bitcast.place_ref, f32[64,1152]{1,0:T(8,128)S(1)} %get-tuple-element.35.keep_ref, bf16[64,1152]{1,0:T(8,128)(2,1)S(1)} %collective-permute-done.6.came_ref, f32[8,256]{1,0:T(8,128)S(1)} %get-tuple-element.40.totals_ref, f32[8,256]{1,0:T(8,128)S(1)} %collective-permute-done.7.other_ref), custom_call_target="tpu_custom_call" | custom-call | tf_op jit(solution)/shard_map/pallas_call | solution.py:267
  52.6 4.9 %all-to-all-start.2 = ((bf16[8,8,1664]{2,1,0:T(8,128)(2,1)}), bf16[8,8,1664]{2,1,0:T(8,128)(2,1)S(1)}, u32[]{:S(2)}, u32[]{:S(2)}) async-start(bf16[8,8,1664]{2,1,0:T(8,128)(2,1)} %shard_map.106), calls=%async_computation.2 | async-start | bytes 425984 | tf_op jit(solution)/shard_map/all_to_all | solution.py:34
  57.5 4.1 %collective-permute-start.8 = (f32[1,1152]{1,0:T(1,128)S(1)}, f32[1,1152]{1,0:T(1,128)S(1)}, u32[]{:S(2)}, u32[]{:S(2)}) collective-permute-start(f32[1,1152]{1,0:T(1,128)S(1)} %get-tuple-element.45), channel_id=1, source_target_pairs={{0,1},{1,2},{2,3},{3,4},{4,5},{5,6},{6,7},{7,8},{8,9},{9,10},{10,1... | collective-permute-start | bytes 13832 | tf_op jit(solution)/shard_map/ppermute | solution.py:26
  61.7 0.7 %collective-permute-done.8.behind_ref = f32[1,1152]{1,0:T(1,128)S(1)} collective-permute-done((f32[1,1152]{1,0:T(1,128)S(1)}, f32[1,1152]{1,0:T(1,128)S(1)}, u32[]{:S(2)}, u32[]{:S(2)}) %collective-permute-start.8) | collective-permute-done | bytes 4640 | tf_op jit(solution)/shard_map/ppermute | solution.py:26
  62.4 0.0 copy-done
  62.4 1.4 %shard_map.108 = f32[256,1152]{1,0:T(8,128)} custom-call(s32[1,256]{1,0:T(1,128)S(1)} %bitcast.10, f32[8,1152]{1,0:T(8,128)S(1)} %get-tuple-element.44.grad_ref, f32[1,1152]{1,0:T(1,128)S(1)} %collective-permute-done.8.behind_ref), custom_call_target="tpu_custom_call" | custom-call | tf_op jit(solution)/shard_map/pallas_call | solution.py:272
  63.9 3.5 %all-to-all-done.2.back_ref = bf16[8,8,1664]{2,1,0:T(8,128)(2,1)S(1)} async-done(((bf16[8,8,1664]{2,1,0:T(8,128)(2,1)}), bf16[8,8,1664]{2,1,0:T(8,128)(2,1)S(1)}, u32[]{:S(2)}, u32[]{:S(2)}) %all-to-all-start.2) | async-done | bytes 213024 | tf_op jit(solution)/shard_map/all_to_all | solution.py:34
  67.4 0.7 %shard_map.107 = (f32[8,1152]{1,0:T(8,128)}, f32[1152]{0:T(1024)}, f32[3]{0:T(128)}) custom-call(bf16[8,8,1664]{2,1,0:T(8,128)(2,1)S(1)} %all-to-all-done.2.back_ref, f32[8,1152]{1,0:T(8,128)S(1)} %get-tuple-element.41.unit_ref, f32[8,1]{1,0:T(8,128)S(1)} %get-tuple-element.42.norm_ref), custom_call_target="tpu_custom_call" | custom-call | tf_op jit(solution)/shard_map/pallas_call | solution.py:273
  (8 shorter events, 0.0 us)
Async XLA Ops:
  2.0 22.1 %collective-permute-start.2 = (bf16[8,1280]{1,0:T(8,128)(2,1)S(1)}, bf16[8,1280]{1,0:T(8,128)(2,1)S(1)}, u32[]{:S(2)}, u32[]{:S(2)}) collective-permute-start(bf16[8,1280]{1,0:T(8,128)(2,1)S(1)} %get-tuple-element.26), channel_id=1, source_target_pairs={{0,12},{2,14},{4,8},{6,10},{8,4},{10,6},{12,0},{14,2},{1,13},{3,15... | collective-permute-start | bytes 61448 | tf_op jit(solution)/shard_map/ppermute | solution.py:30
  8.9 15.2 %collective-permute-start.1 = (bf16[8,1280]{1,0:T(8,128)(2,1)S(1)}, bf16[8,1280]{1,0:T(8,128)(2,1)S(1)}, u32[]{:S(2)}, u32[]{:S(2)}) collective-permute-start(bf16[8,1280]{1,0:T(8,128)(2,1)S(1)} %get-tuple-element.26), channel_id=1, source_target_pairs={{0,8},{2,10},{4,12},{6,14},{8,0},{10,2},{12,4},{14,6},{1,9},{3,11}... | collective-permute-start | bytes 61448 | tf_op jit(solution)/shard_map/ppermute | solution.py:30
  9.9 14.2 %collective-permute-start = (bf16[8,1280]{1,0:T(8,128)(2,1)S(1)}, bf16[8,1280]{1,0:T(8,128)(2,1)S(1)}, u32[]{:S(2)}, u32[]{:S(2)}) collective-permute-start(bf16[8,1280]{1,0:T(8,128)(2,1)S(1)} %get-tuple-element.26), channel_id=1, source_target_pairs={{0,4},{2,6},{4,0},{6,2},{8,12},{10,14},{12,8},{14,10},{1,5},{3,7},... | collective-permute-start | bytes 61448 | tf_op jit(solution)/shard_map/ppermute | solution.py:30
  11.1 5.3 %collective-permute-start.5 = (f32[1,1152]{1,0:T(1,128)S(1)}, f32[1,1152]{1,0:T(1,128)S(1)}, u32[]{:S(2)}, u32[]{:S(2)}) collective-permute-start(f32[1,1152]{1,0:T(1,128)S(1)} %get-tuple-element.32), channel_id=1, source_target_pairs={{1,0},{2,1},{3,2},{4,3},{5,4},{6,5},{7,6},{8,7},{9,8},{10,9},{11,1... | collective-permute-start | bytes 13832 | tf_op jit(solution)/shard_map/ppermute | solution.py:26
  17.3 14.7 %all-to-all-start = ((bf16[16,8,1280]{2,1,0:T(8,128)(2,1)}), bf16[16,8,1280]{2,1,0:T(8,128)(2,1)S(1)}, u32[]{:S(2)}, u32[]{:S(2)}) async-start(bf16[16,8,1280]{2,1,0:T(8,128)(2,1)} %get-tuple-element.34), calls=%async_computation | async-start | bytes 655360 | tf_op jit(solution)/shard_map/all_to_all | solution.py:34
  24.1 3.4 %collective-permute-start.3 = (bf16[32,1280]{1,0:T(8,128)(2,1)S(1)}, bf16[32,1280]{1,0:T(8,128)(2,1)S(1)}, u32[]{:S(2)}, u32[]{:S(2)}) collective-permute-start(bf16[32,1280]{1,0:T(8,128)(2,1)S(1)} %pad_maximum_fusion), channel_id=1, source_target_pairs={{0,2},{2,0},{4,6},{6,4},{8,10},{10,8},{12,14},{14,12},{1,3},{3,1},... | collective-permute-start | bytes 245768 | tf_op jit(solution)/shard_map/ppermute | solution.py:30
  27.5 4.0 %collective-permute-start.4 = (bf16[64,1280]{1,0:T(8,128)(2,1)S(1)}, bf16[64,1280]{1,0:T(8,128)(2,1)S(1)}, u32[]{:S(2)}, u32[]{:S(2)}) collective-permute-start(bf16[64,1280]{1,0:T(8,128)(2,1)S(1)} %constant_dynamic-update-slice_fusion.near_ref), channel_id=1, source_target_pairs={{0,1},{1,0},{2,3},{3,2},{4,5},{5,4},{6,7},{7,6},{8,9},{9,8},{10,11... | collective-permute-start | bytes 491528 | tf_op jit(solution)/shard_map/ppermute | solution.py:30
  33.6 28.9 %copy-start = (s32[256]{0:T(256)S(1)}, s32[256]{0:T(256)}, u32[]{:S(2)}) copy-start(s32[256]{0:T(256)} %param.9) | copy-start | bytes 3076
  33.6 15.9 %all-to-all-start.1 = ((bf16[16,8,1408]{2,1,0:T(8,128)(2,1)}), bf16[16,8,1408]{2,1,0:T(8,128)(2,1)S(1)}, u32[]{:S(2)}, u32[]{:S(2)}) async-start(bf16[16,8,1408]{2,1,0:T(8,128)(2,1)} %bitcast.5), calls=%async_computation.1 | async-start | bytes 720896 | tf_op jit(solution)/shard_map/all_to_all | solution.py:34
  40.2 10.9 %collective-permute-start.6 = (bf16[64,1152]{1,0:T(8,128)(2,1)S(1)}, bf16[64,1152]{1,0:T(8,128)(2,1)S(1)}, u32[]{:S(2)}, u32[]{:S(2)}) collective-permute-start(bf16[64,1152]{1,0:T(8,128)(2,1)S(1)} %get-tuple-element.36), channel_id=1, source_target_pairs={{0,1},{1,0},{2,3},{3,2},{4,5},{5,4},{6,7},{7,6},{8,9},{9,8},{10,11... | collective-permute-start | bytes 442376 | tf_op jit(solution)/shard_map/ppermute | solution.py:30
  49.6 2.4 %collective-permute-start.7 = (f32[8,256]{1,0:T(8,128)S(1)}, f32[8,256]{1,0:T(8,128)S(1)}, u32[]{:S(2)}, u32[]{:S(2)}) collective-permute-start(f32[8,256]{1,0:T(8,128)S(1)} %get-tuple-element.40.totals_ref), channel_id=1, source_target_pairs={{0,1},{1,0},{2,3},{3,2},{4,5},{5,4},{6,7},{7,6},{8,9},{9,8},{10,11... | collective-permute-start | bytes 24584 | tf_op jit(solution)/shard_map/ppermute | solution.py:30
  52.6 14.7 %all-to-all-start.2 = ((bf16[8,8,1664]{2,1,0:T(8,128)(2,1)}), bf16[8,8,1664]{2,1,0:T(8,128)(2,1)S(1)}, u32[]{:S(2)}, u32[]{:S(2)}) async-start(bf16[8,8,1664]{2,1,0:T(8,128)(2,1)} %shard_map.106), calls=%async_computation.2 | async-start | bytes 425984 | tf_op jit(solution)/shard_map/all_to_all | solution.py:34
  57.5 4.9 %collective-permute-start.8 = (f32[1,1152]{1,0:T(1,128)S(1)}, f32[1,1152]{1,0:T(1,128)S(1)}, u32[]{:S(2)}, u32[]{:S(2)}) collective-permute-start(f32[1,1152]{1,0:T(1,128)S(1)} %get-tuple-element.45), channel_id=1, source_target_pairs={{0,1},{1,2},{2,3},{3,4},{4,5},{5,6},{6,7},{7,8},{8,9},{9,10},{10,1... | collective-permute-start | bytes 13832 | tf_op jit(solution)/shard_map/ppermute | solution.py:26

commit v6 on v5

--- a/solution.py
+++ b/solution.py
@@ -31,7 +31,9 @@
 
 
 def to_all(blocks, axes):
-    return lax.all_to_all(blocks, axes, 0, 0, tiled=True)
+    count = lax.axis_size(axes)
+    backward = [list(range(count))[::-1]]
+    return lax.all_to_all(blocks, axes, 0, 0, tiled=True, axis_index_groups=backward)
 
 
 def members(ids, pairs, copies):
@@ -169,7 +171,7 @@
     for k in range(places):
         rows = slice(pairs * k, pairs * (k + 1))
         block = keep_ref[rows] + came_ref[rows].astype(F32)
-        place = place_ref[0] ^ FROM[k]
+        place = places - 1 - (place_ref[0] ^ FROM[k])
         out_ref[place, :, :width] = block.astype(BF16)
         out_ref[place, :, width : width + 2 * LANES] = high
         out_ref[place, :, width + 2 * LANES :] = low

time: 68.6 us -> 67 us (0.977)
  the two profiles are of different devices: /device:TPU:1 before, /device:TPU:8 now
where the time goes in v6:
time: 67 us; the launch traced here: 66.5 us
  starting transfers between devices  36.9 us (55%)
  waiting for transfers between devices  20.7 us (31%)
  Pallas kernels  6.77 us (10%)
  between operations  2.07 us (3%)
    all_to_all x3, starting transfers between devices, to_all(): lax.all_to_all(blocks, axes, 0, 0, tiled=True, axis_index_groups=backward)  19.8 us
    ppermute x7, starting transfers between devices, exchange(): lax.ppermute(value, axis, [(i, i ^ bit) for i in range(lax.axis_size(axis...  9.04 us
    ppermute x2, waiting for transfers between devices, from_behind(): return lax.ppermute(value, DP, pairs)  8.81 us
    ppermute x2, starting transfers between devices, from_behind(): return lax.ppermute(value, DP, pairs)  8.08 us
    all_to_all x3, waiting for transfers between devices, to_all(): lax.all_to_all(blocks, axes, 0, 0, tiled=True, axis_index_groups=backward)  6.26 us
    ppermute x7, waiting for transfers between devices, exchange(): lax.ppermute(value, axis, [(i, i ^ bit) for i in range(lax.axis_size(axis...  5.63 us
    pallas_call x1, Pallas kernels, per_device(): local(pair_math, [VMEM] * 5, ((plane * pairs, wide + LANES), BF16), ((dep...  1.54 us
    pallas_call x1, Pallas kernels, per_device(): local(token_rows, [VMEM] * 3, ((tokens, width), F32))  1.43 us
  transfers between devices with their start and end apart: 12, of which 6 were waited for; matrix products, arithmetic and copies ran while one was open for 0% of the time, Pallas kernels for 4%

profile of v6, /device:TPU:8, one launch (start us, length us, event | category | flops | bytes accessed | tf_op | source)
XLA Modules:
  0.0 66.5 jit_solution(2333613400987830215)
XLA Ops:
  0.6 1.4 %shard_map.102 = (bf16[8,1280]{1,0:T(8,128)(2,1)S(1)}, f32[8,1152]{1,0:T(8,128)S(1)}, f32[8,1]{1,0:T(8,128)S(1)}, f32[8,1152]{1,0:T(8,128)S(1)}, f32[1,1152]{1,0...) custom-call(s32[8]{0:T(128)} %groups_hbm.1, s32[1,256]{1,0:T(1,128)} %bitcast.9, ...), custom_call_target="tpu_custom_call" | custom-call | tf_op jit(solution)/shard_map/pallas_call | solution.py:225
  2.0 6.4 %collective-permute-start.2 = (bf16[8,1280]{1,0:T(8,128)(2,1)S(1)}, bf16[8,1280]{1,0:T(8,128)(2,1)S(1)}, u32[]{:S(2)}, u32[]{:S(2)}) collective-permute-start(bf16[8,1280]{1,0:T(8,128)(2,1)S(1)} %get-tuple-element.26), channel_id=1, source_target_pairs={{0,12},{2,14},{4,8},{6,10},{8,4},{10,6},{12,0},{14,2},{1,13},{3,15... | collective-permute-start | bytes 61448 | tf_op jit(solution)/shard_map/ppermute | solution.py:30
  8.4 1.0 %collective-permute-start.1 = (bf16[8,1280]{1,0:T(8,128)(2,1)S(1)}, bf16[8,1280]{1,0:T(8,128)(2,1)S(1)}, u32[]{:S(2)}, u32[]{:S(2)}) collective-permute-start(bf16[8,1280]{1,0:T(8,128)(2,1)S(1)} %get-tuple-element.26), channel_id=1, source_target_pairs={{0,8},{2,10},{4,12},{6,14},{8,0},{10,2},{12,4},{14,6},{1,9},{3,11}... | collective-permute-start | bytes 61448 | tf_op jit(solution)/shard_map/ppermute | solution.py:30
  9.4 1.5 %collective-permute-start = (bf16[8,1280]{1,0:T(8,128)(2,1)S(1)}, bf16[8,1280]{1,0:T(8,128)(2,1)S(1)}, u32[]{:S(2)}, u32[]{:S(2)}) collective-permute-start(bf16[8,1280]{1,0:T(8,128)(2,1)S(1)} %get-tuple-element.26), channel_id=1, source_target_pairs={{0,4},{2,6},{4,0},{6,2},{8,12},{10,14},{12,8},{14,10},{1,5},{3,7},... | collective-permute-start | bytes 61448 | tf_op jit(solution)/shard_map/ppermute | solution.py:30
  10.9 6.2 %collective-permute-start.5 = (f32[1,1152]{1,0:T(1,128)S(1)}, f32[1,1152]{1,0:T(1,128)S(1)}, u32[]{:S(2)}, u32[]{:S(2)}) collective-permute-start(f32[1,1152]{1,0:T(1,128)S(1)} %get-tuple-element.32), channel_id=1, source_target_pairs={{1,0},{2,1},{3,2},{4,3},{5,4},{6,5},{7,6},{8,7},{9,8},{10,9},{11,1... | collective-permute-start | bytes 13832 | tf_op jit(solution)/shard_map/ppermute | solution.py:26
  17.1 1.3 %collective-permute-done.5.arrived_ref = f32[1,1152]{1,0:T(1,128)S(1)} collective-permute-done((f32[1,1152]{1,0:T(1,128)S(1)}, f32[1,1152]{1,0:T(1,128)S(1)}, u32[]{:S(2)}, u32[]{:S(2)}) %collective-permute-start.5) | collective-permute-done | bytes 4640 | tf_op jit(solution)/shard_map/ppermute | solution.py:26
  18.4 0.9 %shard_map.103 = (bf16[16,8,1280]{2,1,0:T(8,128)(2,1)}, f32[8,1152]{1,0:T(8,128)S(1)}, f32[8,1]{1,0:T(8,128)S(1)}) custom-call(bf16[8,128]{1,0:T(8,128)(2,1)S(1)} %get-tuple-element.30.tile_ref, f32[8,1152]{1,0:T(8,128)S(1)} %get-tuple-element.31.pooled_ref, f32[1,1152]{1,0:T(1,128)S(1)} %collective-permute-done.5.arrived_ref, ...), custom_call_target="tpu_custom_call" | custom-call | tf_op jit(solution)/shard_map/pallas_call | solution.py:247
  19.2 6.9 %all-to-all-start = ((bf16[16,8,1280]{2,1,0:T(8,128)(2,1)}), bf16[16,8,1280]{2,1,0:T(8,128)(2,1)S(1)}, u32[]{:S(2)}, u32[]{:S(2)}) async-start(bf16[16,8,1280]{2,1,0:T(8,128)(2,1)} %get-tuple-element.34), calls=%async_computation | async-start | bytes 655360 | tf_op jit(solution)/shard_map/all_to_all | solution.py:36
  26.1 0.0 collective-permute-done.2
  26.2 0.0 collective-permute-done.1
  26.2 0.0 collective-permute-done
  26.2 0.1 collective-permute-start.3
  26.3 4.4 %collective-permute-done.3 = bf16[32,1280]{1,0:T(8,128)(2,1)S(1)} collective-permute-done((bf16[32,1280]{1,0:T(8,128)(2,1)S(1)}, bf16[32,1280]{1,0:T(8,128)(2,1)S(1)}, u32[]{:S(2)}, u32[]{:S(2)}) %collective-permute-start.3) | collective-permute-done | bytes 81952 | tf_op jit(solution)/shard_map/ppermute | solution.py:30
  30.7 0.0 collective-permute-start.4
  32.0 0.1 collective-permute-done.4.far_ref
  32.1 0.0 all-to-all-done
  32.1 1.5 %shard_map.104 = (bf16[128,1408]{1,0:T(8,128)(2,1)}, f32[64,1152]{1,0:T(8,128)S(1)}, bf16[64,1152]{1,0:T(8,128)(2,1)S(1)}) custom-call(f32[1,128]{1,0:T(1,128)S(1)} %compare_select_fusion.knobs_ref, bf16[64,1280]{1,0:T(8,128)(2,1)S(1)} %constant_dynamic-update-slice_fusion.near_ref, bf16[64,1280]{1,0:T(8,128)(2,1)S(1)} %collective-permute-done.4.far_ref, ...), custom_call_target="tpu_custom_call" | custom-call | tf_op jit(solution)/shard_map/pallas_call | solution.py:257
  33.7 7.4 %all-to-all-start.1 = ((bf16[16,8,1408]{2,1,0:T(8,128)(2,1)}), bf16[16,8,1408]{2,1,0:T(8,128)(2,1)S(1)}, u32[]{:S(2)}, u32[]{:S(2)}) async-start(bf16[16,8,1408]{2,1,0:T(8,128)(2,1)} %bitcast.5), calls=%async_computation.1 | async-start | bytes 720896 | tf_op jit(solution)/shard_map/all_to_all | solution.py:36
  41.0 0.0 collective-permute-start.6
  41.0 6.3 %all-to-all-done.1.back_ref = bf16[16,8,1408]{2,1,0:T(8,128)(2,1)S(1)} async-done(((bf16[16,8,1408]{2,1,0:T(8,128)(2,1)}), bf16[16,8,1408]{2,1,0:T(8,128)(2,1)S(1)}, u32[]{:S(2)}, u32[]{:S(2)}) %all-to-all-start.1) | async-done | bytes 360480 | tf_op jit(solution)/shard_map/all_to_all | solution.py:36
  47.3 0.1 shard_map.105
  47.4 0.1 collective-permute-start.7
  47.5 0.0 collective-permute-done.6.came_ref
  47.5 1.1 %collective-permute-done.7.other_ref = f32[8,256]{1,0:T(8,128)S(1)} collective-permute-done((f32[8,256]{1,0:T(8,128)S(1)}, f32[8,256]{1,0:T(8,128)S(1)}, u32[]{:S(2)}, u32[]{:S(2)}) %collective-permute-start.7) | collective-permute-done | bytes 8224 | tf_op jit(solution)/shard_map/ppermute | solution.py:30
  48.7 0.7 %shard_map.106 = bf16[8,8,1664]{2,1,0:T(8,128)(2,1)} custom-call(s32[1]{0:T(128)} %bitcast.place_ref, f32[64,1152]{1,0:T(8,128)S(1)} %get-tuple-element.35.keep_ref, bf16[64,1152]{1,0:T(8,128)(2,1)S(1)} %collective-permute-done.6.came_ref, f32[8,256]{1,0:T(8,128)S(1)} %get-tuple-element.40.totals_ref, f32[8,256]{1,0:T(8,128)S(1)} %collective-permute-done.7.other_ref), custom_call_target="tpu_custom_call" | custom-call | tf_op jit(solution)/shard_map/pallas_call | solution.py:269
  49.4 5.5 %all-to-all-start.2 = ((bf16[8,8,1664]{2,1,0:T(8,128)(2,1)}), bf16[8,8,1664]{2,1,0:T(8,128)(2,1)S(1)}, u32[]{:S(2)}, u32[]{:S(2)}) async-start(bf16[8,8,1664]{2,1,0:T(8,128)(2,1)} %shard_map.106), calls=%async_computation.2 | async-start | bytes 425984 | tf_op jit(solution)/shard_map/all_to_all | solution.py:36
  54.9 1.9 %collective-permute-start.8 = (f32[1,1152]{1,0:T(1,128)S(1)}, f32[1,1152]{1,0:T(1,128)S(1)}, u32[]{:S(2)}, u32[]{:S(2)}) collective-permute-start(f32[1,1152]{1,0:T(1,128)S(1)} %get-tuple-element.45), channel_id=1, source_target_pairs={{0,1},{1,2},{2,3},{3,4},{4,5},{5,6},{6,7},{7,8},{8,9},{9,10},{10,1... | collective-permute-start | bytes 13832 | tf_op jit(solution)/shard_map/ppermute | solution.py:26
  56.8 7.5 %collective-permute-done.8.behind_ref = f32[1,1152]{1,0:T(1,128)S(1)} collective-permute-done((f32[1,1152]{1,0:T(1,128)S(1)}, f32[1,1152]{1,0:T(1,128)S(1)}, u32[]{:S(2)}, u32[]{:S(2)}) %collective-permute-start.8) | collective-permute-done | bytes 4640 | tf_op jit(solution)/shard_map/ppermute | solution.py:26
  64.3 0.0 copy-done
  64.3 1.4 %shard_map.108 = f32[256,1152]{1,0:T(8,128)} custom-call(s32[1,256]{1,0:T(1,128)S(1)} %bitcast.10, f32[8,1152]{1,0:T(8,128)S(1)} %get-tuple-element.44.grad_ref, f32[1,1152]{1,0:T(1,128)S(1)} %collective-permute-done.8.behind_ref), custom_call_target="tpu_custom_call" | custom-call | tf_op jit(solution)/shard_map/pallas_call | solution.py:274
  65.7 0.0 all-to-all-done.2.back_ref
  65.7 0.7 %shard_map.107 = (f32[8,1152]{1,0:T(8,128)}, f32[1152]{0:T(1024)}, f32[3]{0:T(128)}) custom-call(bf16[8,8,1664]{2,1,0:T(8,128)(2,1)S(1)} %all-to-all-done.2.back_ref, f32[8,1152]{1,0:T(8,128)S(1)} %get-tuple-element.41.unit_ref, f32[8,1]{1,0:T(8,128)S(1)} %get-tuple-element.42.norm_ref), custom_call_target="tpu_custom_call" | custom-call | tf_op jit(solution)/shard_map/pallas_call | solution.py:275
  (8 shorter events, 0.0 us)
Async XLA Ops:
  2.0 24.1 %collective-permute-start.2 = (bf16[8,1280]{1,0:T(8,128)(2,1)S(1)}, bf16[8,1280]{1,0:T(8,128)(2,1)S(1)}, u32[]{:S(2)}, u32[]{:S(2)}) collective-permute-start(bf16[8,1280]{1,0:T(8,128)(2,1)S(1)} %get-tuple-element.26), channel_id=1, source_target_pairs={{0,12},{2,14},{4,8},{6,10},{8,4},{10,6},{12,0},{14,2},{1,13},{3,15... | collective-permute-start | bytes 61448 | tf_op jit(solution)/shard_map/ppermute | solution.py:30
  8.4 17.7 %collective-permute-start.1 = (bf16[8,1280]{1,0:T(8,128)(2,1)S(1)}, bf16[8,1280]{1,0:T(8,128)(2,1)S(1)}, u32[]{:S(2)}, u32[]{:S(2)}) collective-permute-start(bf16[8,1280]{1,0:T(8,128)(2,1)S(1)} %get-tuple-element.26), channel_id=1, source_target_pairs={{0,8},{2,10},{4,12},{6,14},{8,0},{10,2},{12,4},{14,6},{1,9},{3,11}... | collective-permute-start | bytes 61448 | tf_op jit(solution)/shard_map/ppermute | solution.py:30
  9.4 16.8 %collective-permute-start = (bf16[8,1280]{1,0:T(8,128)(2,1)S(1)}, bf16[8,1280]{1,0:T(8,128)(2,1)S(1)}, u32[]{:S(2)}, u32[]{:S(2)}) collective-permute-start(bf16[8,1280]{1,0:T(8,128)(2,1)S(1)} %get-tuple-element.26), channel_id=1, source_target_pairs={{0,4},{2,6},{4,0},{6,2},{8,12},{10,14},{12,8},{14,10},{1,5},{3,7},... | collective-permute-start | bytes 61448 | tf_op jit(solution)/shard_map/ppermute | solution.py:30
  10.9 7.5 %collective-permute-start.5 = (f32[1,1152]{1,0:T(1,128)S(1)}, f32[1,1152]{1,0:T(1,128)S(1)}, u32[]{:S(2)}, u32[]{:S(2)}) collective-permute-start(f32[1,1152]{1,0:T(1,128)S(1)} %get-tuple-element.32), channel_id=1, source_target_pairs={{1,0},{2,1},{3,2},{4,3},{5,4},{6,5},{7,6},{8,7},{9,8},{10,9},{11,1... | collective-permute-start | bytes 13832 | tf_op jit(solution)/shard_map/ppermute | solution.py:26
  19.2 12.9 %all-to-all-start = ((bf16[16,8,1280]{2,1,0:T(8,128)(2,1)}), bf16[16,8,1280]{2,1,0:T(8,128)(2,1)S(1)}, u32[]{:S(2)}, u32[]{:S(2)}) async-start(bf16[16,8,1280]{2,1,0:T(8,128)(2,1)} %get-tuple-element.34), calls=%async_computation | async-start | bytes 655360 | tf_op jit(solution)/shard_map/all_to_all | solution.py:36
  26.2 4.5 %collective-permute-start.3 = (bf16[32,1280]{1,0:T(8,128)(2,1)S(1)}, bf16[32,1280]{1,0:T(8,128)(2,1)S(1)}, u32[]{:S(2)}, u32[]{:S(2)}) collective-permute-start(bf16[32,1280]{1,0:T(8,128)(2,1)S(1)} %pad_maximum_fusion), channel_id=1, source_target_pairs={{0,2},{2,0},{4,6},{6,4},{8,10},{10,8},{12,14},{14,12},{1,3},{3,1},... | collective-permute-start | bytes 245768 | tf_op jit(solution)/shard_map/ppermute | solution.py:30
  30.7 1.4 %collective-permute-start.4 = (bf16[64,1280]{1,0:T(8,128)(2,1)S(1)}, bf16[64,1280]{1,0:T(8,128)(2,1)S(1)}, u32[]{:S(2)}, u32[]{:S(2)}) collective-permute-start(bf16[64,1280]{1,0:T(8,128)(2,1)S(1)} %constant_dynamic-update-slice_fusion.near_ref), channel_id=1, source_target_pairs={{0,1},{1,0},{2,3},{3,2},{4,5},{5,4},{6,7},{7,6},{8,9},{9,8},{10,11... | collective-permute-start | bytes 491528 | tf_op jit(solution)/shard_map/ppermute | solution.py:30
  33.7 30.7 %copy-start = (s32[256]{0:T(256)S(1)}, s32[256]{0:T(256)}, u32[]{:S(2)}) copy-start(s32[256]{0:T(256)} %param.9) | copy-start | bytes 3076
  33.7 13.6 %all-to-all-start.1 = ((bf16[16,8,1408]{2,1,0:T(8,128)(2,1)}), bf16[16,8,1408]{2,1,0:T(8,128)(2,1)S(1)}, u32[]{:S(2)}, u32[]{:S(2)}) async-start(bf16[16,8,1408]{2,1,0:T(8,128)(2,1)} %bitcast.5), calls=%async_computation.1 | async-start | bytes 720896 | tf_op jit(solution)/shard_map/all_to_all | solution.py:36
  41.0 6.5 %collective-permute-start.6 = (bf16[64,1152]{1,0:T(8,128)(2,1)S(1)}, bf16[64,1152]{1,0:T(8,128)(2,1)S(1)}, u32[]{:S(2)}, u32[]{:S(2)}) collective-permute-start(bf16[64,1152]{1,0:T(8,128)(2,1)S(1)} %get-tuple-element.36), channel_id=1, source_target_pairs={{0,1},{1,0},{2,3},{3,2},{4,5},{5,4},{6,7},{7,6},{8,9},{9,8},{10,11... | collective-permute-start | bytes 442376 | tf_op jit(solution)/shard_map/ppermute | solution.py:30
  47.4 1.3 %collective-permute-start.7 = (f32[8,256]{1,0:T(8,128)S(1)}, f32[8,256]{1,0:T(8,128)S(1)}, u32[]{:S(2)}, u32[]{:S(2)}) collective-permute-start(f32[8,256]{1,0:T(8,128)S(1)} %get-tuple-element.40.totals_ref), channel_id=1, source_target_pairs={{0,1},{1,0},{2,3},{3,2},{4,5},{5,4},{6,7},{7,6},{8,9},{9,8},{10,11... | collective-permute-start | bytes 24584 | tf_op jit(solution)/shard_map/ppermute | solution.py:30
  49.4 16.4 %all-to-all-start.2 = ((bf16[8,8,1664]{2,1,0:T(8,128)(2,1)}), bf16[8,8,1664]{2,1,0:T(8,128)(2,1)S(1)}, u32[]{:S(2)}, u32[]{:S(2)}) async-start(bf16[8,8,1664]{2,1,0:T(8,128)(2,1)} %shard_map.106), calls=%async_computation.2 | async-start | bytes 425984 | tf_op jit(solution)/shard_map/all_to_all | solution.py:36
  54.9 9.4 %collective-permute-start.8 = (f32[1,1152]{1,0:T(1,128)S(1)}, f32[1,1152]{1,0:T(1,128)S(1)}, u32[]{:S(2)}, u32[]{:S(2)}) collective-permute-start(f32[1,1152]{1,0:T(1,128)S(1)} %get-tuple-element.45), channel_id=1, source_target_pairs={{0,1},{1,2},{2,3},{3,4},{4,5},{5,6},{6,7},{7,8},{8,9},{9,10},{10,1... | collective-permute-start | bytes 13832 | tf_op jit(solution)/shard_map/ppermute | solution.py:26

commit v7 on v6

--- a/solution.py
+++ b/solution.py
@@ -20,10 +20,14 @@
 FROM = (0, 2, 4, 6, 1, 3, 5, 7)
 
 
-def from_behind(value, by):
-    count = lax.axis_size(DP)
-    pairs = [(i, i + by) for i in range(count) if 0 <= i + by < count]
-    return lax.ppermute(value, DP, pairs)
+def from_beside(value, by):
+    count, parts = lax.axis_size(DP), []
+    for within in (False, True):
+        pairs = [
+            (i, i + by) for i in range(count) if 0 <= i + by < count and (i // 2 == (i + by) // 2) == within
+        ]
+        parts.append(lax.ppermute(value, DP, pairs))
+    return parts
 
 
 def exchange(value, axis, bit):
@@ -93,10 +97,10 @@
     spill_ref[...] = sums[pairs : pairs + 1]
 
 
-def text_rows(tile_ref, pooled_ref, arrived_ref, gain_ref, rows_ref, unit_ref, norm_ref):
+def text_rows(tile_ref, pooled_ref, chip_ref, core_ref, gain_ref, rows_ref, unit_ref, norm_ref):
     pairs, width = pooled_ref.shape
     last = lax.broadcasted_iota(jnp.int32, (pairs, 1), 0) == pairs - 1
-    pooled = pooled_ref[...] + jnp.where(last, arrived_ref[...], 0.0)
+    pooled = pooled_ref[...] + jnp.where(last, chip_ref[...] + core_ref[...], 0.0)
     embedded = pooled * gain_ref[...]
     norm = jnp.sqrt(jnp.sum(embedded * embedded, axis=1, keepdims=True))
     unit = embedded / norm
@@ -177,10 +181,10 @@
         out_ref[place, :, width + 2 * LANES :] = low
 
 
-def token_rows(ids_ref, grad_ref, behind_ref, token_out):
+def token_rows(ids_ref, grad_ref, chip_ref, core_ref, token_out):
     pairs, width = grad_ref.shape
     table = jnp.concatenate(
-        [grad_ref[...], jnp.broadcast_to(behind_ref[...], (pairs, width))], axis=0
+        [grad_ref[...], jnp.broadcast_to(chip_ref[...] + core_ref[...], (pairs, width))], axis=0
     )
     high = table.astype(BF16)
     low = (table - high.astype(F32)).astype(BF16)
@@ -238,16 +242,16 @@
         )
     )
 
-    arrived = from_behind(spill, -1)
+    arrived = from_beside(spill, -1)
     near = [row]
     for step in FROM[1:4]:
         near.append(exchange(row, Z, step))
     near = jnp.concatenate(near, axis=0)
     near = jnp.concatenate([near, exchange(near, Z, 1)], axis=0)
     rows, unit_text, text_norm = local(
-        text_rows, [VMEM] * 4,
+        text_rows, [VMEM] * 5,
         ((plane, pairs, wide), BF16), ((pairs, width), F32), ((pairs, 1), F32),
-    )(tile, pooled, arrived, gain)
+    )(tile, pooled, *arrived, gain)
     texts = to_all(rows, PLANE).reshape(plane * pairs, wide)
 
     far = exchange(near, C, 1)
@@ -270,8 +274,8 @@
         lax.axis_index(Z)[None], keep, came, totals, other
     )
     line_back = to_all(blocks, Z)
-    behind = from_behind(last, 1)
-    (token_grad,) = local(token_rows, [VMEM] * 3, ((tokens, width), F32))(ids, pooled_grad, behind)
+    behind = from_beside(last, 1)
+    (token_grad,) = local(token_rows, [VMEM] * 4, ((tokens, width), F32))(ids, pooled_grad, *behind)
     image_grad, gain_grad, scalars = local(
         functools.partial(finish, count=float(total_pairs * total_pairs)), [VMEM] * 3,
         ((pairs, width), F32), ((width,), F32), ((3,), F32),

time: 67 us -> 69.4 us (1.036)
  starting transfers between devices: 36.9 us -> 40.2 us
  waiting for transfers between devices: 20.7 us -> 19.7 us
    ppermute x2 -> x4, starting transfers between devices: 8.08 us -> 14.7 us  [from_beside(): parts.append(lax.ppermute(value, DP, pairs))]
    ppermute x7, starting transfers between devices: 9.04 us -> 6.76 us  [exchange(): lax.ppermute(value, axis, [(i, i ^ bit) for i in range(lax.axis_size(axis...]
    all_to_all x3, starting transfers between devices: 19.8 us -> 18.8 us  [to_all(): lax.all_to_all(blocks, axes, 0, 0, tiled=True, axis_index_groups=backward)]
    ppermute x2 -> x4, waiting for transfers between devices: 8.81 us -> 7.85 us  [from_beside(): parts.append(lax.ppermute(value, DP, pairs))]
  transfers between devices with their start and end apart: 12 -> 14, of which waited for: 6 -> 5; matrix products, arithmetic and copies ran while one was open for 0% -> 0% of each run, Pallas kernels for 4% -> 4%
where the time goes in v7:
time: 69.4 us; the launch traced here: 68.9 us
  starting transfers between devices  40.2 us (58%)
  waiting for transfers between devices  19.7 us (28%)
  Pallas kernels  6.78 us (10%)
  between operations  2.1 us (3%)
    all_to_all x3, starting transfers between devices, to_all(): lax.all_to_all(blocks, axes, 0, 0, tiled=True, axis_index_groups=backward)  18.8 us
    ppermute x4, starting transfers between devices, from_beside(): parts.append(lax.ppermute(value, DP, pairs))  14.7 us
    ppermute x4, waiting for transfers between devices, from_beside(): parts.append(lax.ppermute(value, DP, pairs))  7.85 us
    ppermute x7, starting transfers between devices, exchange(): lax.ppermute(value, axis, [(i, i ^ bit) for i in range(lax.axis_size(axis...  6.76 us
    all_to_all x3, waiting for transfers between devices, to_all(): lax.all_to_all(blocks, axes, 0, 0, tiled=True, axis_index_groups=backward)  6.26 us
    ppermute x7, waiting for transfers between devices, exchange(): lax.ppermute(value, axis, [(i, i ^ bit) for i in range(lax.axis_size(axis...  5.63 us
    pallas_call x1, Pallas kernels, per_device(): local(pair_math, [VMEM] * 5, ((plane * pairs, wide + LANES), BF16), ((dep...  1.53 us
    pallas_call x1, Pallas kernels, per_device(): local(token_rows, [VMEM] * 4, ((tokens, width), F32))  1.43 us
  transfers between devices with their start and end apart: 14, of which 5 were waited for; matrix products, arithmetic and copies ran while one was open for 0% of the time, Pallas kernels for 4%

profile of v7, /device:TPU:8, one launch (start us, length us, event | category | flops | bytes accessed | tf_op | source)
XLA Modules:
  0.0 68.9 jit_solution(17609943963769404829)
XLA Ops:
  0.6 1.4 %shard_map.102 = (bf16[8,1280]{1,0:T(8,128)(2,1)S(1)}, f32[8,1152]{1,0:T(8,128)S(1)}, f32[8,1]{1,0:T(8,128)S(1)}, f32[8,1152]{1,0:T(8,128)S(1)}, f32[1,1152]{1,0...) custom-call(s32[8]{0:T(128)} %groups_hbm.1, s32[1,256]{1,0:T(1,128)} %bitcast.9, ...), custom_call_target="tpu_custom_call" | custom-call | tf_op jit(solution)/shard_map/pallas_call | solution.py:229
  2.0 1.3 %collective-permute-start.6 = (f32[1,1152]{1,0:T(1,128)S(1)}, f32[1,1152]{1,0:T(1,128)S(1)}, u32[]{:S(2)}, u32[]{:S(2)}) collective-permute-start(f32[1,1152]{1,0:T(1,128)S(1)} %get-tuple-element.32), channel_id=1, source_target_pairs={{1,0},{3,2},{5,4},{7,6},{9,8},{11,10},{13,12},{15,14},{17,16},{19,... | collective-permute-start | bytes 13832 | tf_op jit(solution)/shard_map/ppermute | solution.py:29
  3.3 10.6 %collective-permute-start.5 = (f32[1,1152]{1,0:T(1,128)S(1)}, f32[1,1152]{1,0:T(1,128)S(1)}, u32[]{:S(2)}, u32[]{:S(2)}) collective-permute-start(f32[1,1152]{1,0:T(1,128)S(1)} %get-tuple-element.32), channel_id=1, source_target_pairs={{2,1},{4,3},{6,5},{8,7},{10,9},{12,11},{14,13},{16,15},{18,17},{20... | collective-permute-start | bytes 13832 | tf_op jit(solution)/shard_map/ppermute | solution.py:29
  13.9 0.1 collective-permute-start.2
  14.0 0.1 collective-permute-start.1
  14.1 6.4 %collective-permute-start = (bf16[8,1280]{1,0:T(8,128)(2,1)S(1)}, bf16[8,1280]{1,0:T(8,128)(2,1)S(1)}, u32[]{:S(2)}, u32[]{:S(2)}) collective-permute-start(bf16[8,1280]{1,0:T(8,128)(2,1)S(1)} %get-tuple-element.26), channel_id=1, source_target_pairs={{0,4},{2,6},{4,0},{6,2},{8,12},{10,14},{12,8},{14,10},{1,5},{3,7},... | collective-permute-start | bytes 61448 | tf_op jit(solution)/shard_map/ppermute | solution.py:34
  20.5 0.0 collective-permute-done.6.core_ref
  20.5 0.0 collective-permute-done.5.chip_ref
  20.5 0.9 %shard_map.103 = (bf16[16,8,1280]{2,1,0:T(8,128)(2,1)}, f32[8,1152]{1,0:T(8,128)S(1)}, f32[8,1]{1,0:T(8,128)S(1)}) custom-call(bf16[8,128]{1,0:T(8,128)(2,1)S(1)} %get-tuple-element.30.tile_ref, f32[8,1152]{1,0:T(8,128)S(1)} %get-tuple-element.31.pooled_ref, f32[1,1152]{1,0:T(1,128)S(1)} %collective-permute-done.5.chip_ref, ...), custom_call_target="tpu_custom_call" | custom-call | tf_op jit(solution)/shard_map/pallas_call | solution.py:251
  21.4 6.9 %all-to-all-start = ((bf16[16,8,1280]{2,1,0:T(8,128)(2,1)}), bf16[16,8,1280]{2,1,0:T(8,128)(2,1)S(1)}, u32[]{:S(2)}, u32[]{:S(2)}) async-start(bf16[16,8,1280]{2,1,0:T(8,128)(2,1)} %get-tuple-element.34), calls=%async_computation | async-start | bytes 655360 | tf_op jit(solution)/shard_map/all_to_all | solution.py:40
  28.3 0.0 collective-permute-done.2
  28.3 0.0 collective-permute-done
  28.3 0.1 collective-permute-start.3
  28.5 4.4 %collective-permute-done.3 = bf16[32,1280]{1,0:T(8,128)(2,1)S(1)} collective-permute-done((bf16[32,1280]{1,0:T(8,128)(2,1)S(1)}, bf16[32,1280]{1,0:T(8,128)(2,1)S(1)}, u32[]{:S(2)}, u32[]{:S(2)}) %collective-permute-start.3) | collective-permute-done | bytes 81952 | tf_op jit(solution)/shard_map/ppermute | solution.py:34
  32.9 0.0 collective-permute-start.4
  34.2 0.1 collective-permute-done.4.far_ref
  34.3 1.5 %shard_map.104 = (bf16[128,1408]{1,0:T(8,128)(2,1)}, f32[64,1152]{1,0:T(8,128)S(1)}, bf16[64,1152]{1,0:T(8,128)(2,1)S(1)}) custom-call(f32[1,128]{1,0:T(1,128)S(1)} %compare_select_fusion.knobs_ref, bf16[64,1280]{1,0:T(8,128)(2,1)S(1)} %constant_dynamic-update-slice_fusion.near_ref, bf16[64,1280]{1,0:T(8,128)(2,1)S(1)} %collective-permute-done.4.far_ref, ...), custom_call_target="tpu_custom_call" | custom-call | tf_op jit(solution)/shard_map/pallas_call | solution.py:261
  35.8 7.4 %all-to-all-start.1 = ((bf16[16,8,1408]{2,1,0:T(8,128)(2,1)}), bf16[16,8,1408]{2,1,0:T(8,128)(2,1)S(1)}, u32[]{:S(2)}, u32[]{:S(2)}) async-start(bf16[16,8,1408]{2,1,0:T(8,128)(2,1)} %bitcast.5), calls=%async_computation.1 | async-start | bytes 720896 | tf_op jit(solution)/shard_map/all_to_all | solution.py:40
  43.2 6.2 %all-to-all-done.1.back_ref = bf16[16,8,1408]{2,1,0:T(8,128)(2,1)S(1)} async-done(((bf16[16,8,1408]{2,1,0:T(8,128)(2,1)}), bf16[16,8,1408]{2,1,0:T(8,128)(2,1)S(1)}, u32[]{:S(2)}, u32[]{:S(2)}) %all-to-all-start.1) | async-done | bytes 360480 | tf_op jit(solution)/shard_map/all_to_all | solution.py:40
  49.4 0.1 shard_map.105
  49.6 0.1 collective-permute-start.8
  49.7 0.0 collective-permute-done.7.came_ref
  49.7 1.1 %collective-permute-done.8.other_ref = f32[8,256]{1,0:T(8,128)S(1)} collective-permute-done((f32[8,256]{1,0:T(8,128)S(1)}, f32[8,256]{1,0:T(8,128)S(1)}, u32[]{:S(2)}, u32[]{:S(2)}) %collective-permute-start.8) | collective-permute-done | bytes 8224 | tf_op jit(solution)/shard_map/ppermute | solution.py:34
  50.8 0.7 %shard_map.106 = bf16[8,8,1664]{2,1,0:T(8,128)(2,1)} custom-call(s32[1]{0:T(128)} %bitcast.place_ref, f32[64,1152]{1,0:T(8,128)S(1)} %get-tuple-element.35.keep_ref, bf16[64,1152]{1,0:T(8,128)(2,1)S(1)} %collective-permute-done.7.came_ref, f32[8,256]{1,0:T(8,128)S(1)} %get-tuple-element.40.totals_ref, f32[8,256]{1,0:T(8,128)S(1)} %collective-permute-done.8.other_ref), custom_call_target="tpu_custom_call" | custom-call | tf_op jit(solution)/shard_map/pallas_call | solution.py:273
  51.5 4.5 %all-to-all-start.2 = ((bf16[8,8,1664]{2,1,0:T(8,128)(2,1)}), bf16[8,8,1664]{2,1,0:T(8,128)(2,1)S(1)}, u32[]{:S(2)}, u32[]{:S(2)}) async-start(bf16[8,8,1664]{2,1,0:T(8,128)(2,1)} %shard_map.106), calls=%async_computation.2 | async-start | bytes 425984 | tf_op jit(solution)/shard_map/all_to_all | solution.py:40
  56.0 1.5 %collective-permute-start.10 = (f32[1,1152]{1,0:T(1,128)S(1)}, f32[1,1152]{1,0:T(1,128)S(1)}, u32[]{:S(2)}, u32[]{:S(2)}) collective-permute-start(f32[1,1152]{1,0:T(1,128)S(1)} %get-tuple-element.45), channel_id=1, source_target_pairs={{0,1},{2,3},{4,5},{6,7},{8,9},{10,11},{12,13},{14,15},{16,17},{18,... | collective-permute-start | bytes 13832 | tf_op jit(solution)/shard_map/ppermute | solution.py:29
  57.5 1.3 %collective-permute-start.9 = (f32[1,1152]{1,0:T(1,128)S(1)}, f32[1,1152]{1,0:T(1,128)S(1)}, u32[]{:S(2)}, u32[]{:S(2)}) collective-permute-start(f32[1,1152]{1,0:T(1,128)S(1)} %get-tuple-element.45), channel_id=1, source_target_pairs={{1,2},{3,4},{5,6},{7,8},{9,10},{11,12},{13,14},{15,16},{17,18},{19... | collective-permute-start | bytes 13832 | tf_op jit(solution)/shard_map/ppermute | solution.py:29
  58.8 0.0 collective-permute-done.10.core_ref
  58.9 7.8 %collective-permute-done.9.chip_ref = f32[1,1152]{1,0:T(1,128)S(1)} collective-permute-done((f32[1,1152]{1,0:T(1,128)S(1)}, f32[1,1152]{1,0:T(1,128)S(1)}, u32[]{:S(2)}, u32[]{:S(2)}) %collective-permute-start.9) | collective-permute-done | bytes 4640 | tf_op jit(solution)/shard_map/ppermute | solution.py:29
  66.7 1.4 %shard_map.108 = f32[256,1152]{1,0:T(8,128)} custom-call(s32[1,256]{1,0:T(1,128)S(1)} %bitcast.10, f32[8,1152]{1,0:T(8,128)S(1)} %get-tuple-element.44.grad_ref, f32[1,1152]{1,0:T(1,128)S(1)} %collective-permute-done.9.chip_ref, f32[1,1152]{1,0:T(1,128)S(1)} %collective-permute-done.10.core_ref), custom_call_target="tpu_custom_call" | custom-call | tf_op jit(solution)/shard_map/pallas_call | solution.py:278
  68.1 0.0 all-to-all-done.2.back_ref
  68.1 0.7 %shard_map.107 = (f32[8,1152]{1,0:T(8,128)}, f32[1152]{0:T(1024)}, f32[3]{0:T(128)}) custom-call(bf16[8,8,1664]{2,1,0:T(8,128)(2,1)S(1)} %all-to-all-done.2.back_ref, f32[8,1152]{1,0:T(8,128)S(1)} %get-tuple-element.41.unit_ref, f32[8,1]{1,0:T(8,128)S(1)} %get-tuple-element.42.norm_ref), custom_call_target="tpu_custom_call" | custom-call | tf_op jit(solution)/shard_map/pallas_call | solution.py:279
  (12 shorter events, 0.0 us)
Async XLA Ops:
  2.0 18.5 %collective-permute-start.6 = (f32[1,1152]{1,0:T(1,128)S(1)}, f32[1,1152]{1,0:T(1,128)S(1)}, u32[]{:S(2)}, u32[]{:S(2)}) collective-permute-start(f32[1,1152]{1,0:T(1,128)S(1)} %get-tuple-element.32), channel_id=1, source_target_pairs={{1,0},{3,2},{5,4},{7,6},{9,8},{11,10},{13,12},{15,14},{17,16},{19,... | collective-permute-start | bytes 13832 | tf_op jit(solution)/shard_map/ppermute | solution.py:29
  3.3 17.2 %collective-permute-start.5 = (f32[1,1152]{1,0:T(1,128)S(1)}, f32[1,1152]{1,0:T(1,128)S(1)}, u32[]{:S(2)}, u32[]{:S(2)}) collective-permute-start(f32[1,1152]{1,0:T(1,128)S(1)} %get-tuple-element.32), channel_id=1, source_target_pairs={{2,1},{4,3},{6,5},{8,7},{10,9},{12,11},{14,13},{16,15},{18,17},{20... | collective-permute-start | bytes 13832 | tf_op jit(solution)/shard_map/ppermute | solution.py:29
  13.9 14.4 %collective-permute-start.2 = (bf16[8,1280]{1,0:T(8,128)(2,1)S(1)}, bf16[8,1280]{1,0:T(8,128)(2,1)S(1)}, u32[]{:S(2)}, u32[]{:S(2)}) collective-permute-start(bf16[8,1280]{1,0:T(8,128)(2,1)S(1)} %get-tuple-element.26), channel_id=1, source_target_pairs={{0,12},{2,14},{4,8},{6,10},{8,4},{10,6},{12,0},{14,2},{1,13},{3,15... | collective-permute-start | bytes 61448 | tf_op jit(solution)/shard_map/ppermute | solution.py:34
  14.0 14.3 %collective-permute-start.1 = (bf16[8,1280]{1,0:T(8,128)(2,1)S(1)}, bf16[8,1280]{1,0:T(8,128)(2,1)S(1)}, u32[]{:S(2)}, u32[]{:S(2)}) collective-permute-start(bf16[8,1280]{1,0:T(8,128)(2,1)S(1)} %get-tuple-element.26), channel_id=1, source_target_pairs={{0,8},{2,10},{4,12},{6,14},{8,0},{10,2},{12,4},{14,6},{1,9},{3,11}... | collective-permute-start | bytes 61448 | tf_op jit(solution)/shard_map/ppermute | solution.py:34
  14.1 14.2 %collective-permute-start = (bf16[8,1280]{1,0:T(8,128)(2,1)S(1)}, bf16[8,1280]{1,0:T(8,128)(2,1)S(1)}, u32[]{:S(2)}, u32[]{:S(2)}) collective-permute-start(bf16[8,1280]{1,0:T(8,128)(2,1)S(1)} %get-tuple-element.26), channel_id=1, source_target_pairs={{0,4},{2,6},{4,0},{6,2},{8,12},{10,14},{12,8},{14,10},{1,5},{3,7},... | collective-permute-start | bytes 61448 | tf_op jit(solution)/shard_map/ppermute | solution.py:34
  21.4 12.9 %all-to-all-start = ((bf16[16,8,1280]{2,1,0:T(8,128)(2,1)}), bf16[16,8,1280]{2,1,0:T(8,128)(2,1)S(1)}, u32[]{:S(2)}, u32[]{:S(2)}) async-start(bf16[16,8,1280]{2,1,0:T(8,128)(2,1)} %get-tuple-element.34), calls=%async_computation | async-start | bytes 655360 | tf_op jit(solution)/shard_map/all_to_all | solution.py:40
  28.3 4.5 %collective-permute-start.3 = (bf16[32,1280]{1,0:T(8,128)(2,1)S(1)}, bf16[32,1280]{1,0:T(8,128)(2,1)S(1)}, u32[]{:S(2)}, u32[]{:S(2)}) collective-permute-start(bf16[32,1280]{1,0:T(8,128)(2,1)S(1)} %pad_maximum_fusion), channel_id=1, source_target_pairs={{0,2},{2,0},{4,6},{6,4},{8,10},{10,8},{12,14},{14,12},{1,3},{3,1},... | collective-permute-start | bytes 245768 | tf_op jit(solution)/shard_map/ppermute | solution.py:34
  32.9 1.4 %collective-permute-start.4 = (bf16[64,1280]{1,0:T(8,128)(2,1)S(1)}, bf16[64,1280]{1,0:T(8,128)(2,1)S(1)}, u32[]{:S(2)}, u32[]{:S(2)}) collective-permute-start(bf16[64,1280]{1,0:T(8,128)(2,1)S(1)} %constant_dynamic-update-slice_fusion.near_ref), channel_id=1, source_target_pairs={{0,1},{1,0},{2,3},{3,2},{4,5},{5,4},{6,7},{7,6},{8,9},{9,8},{10,11... | collective-permute-start | bytes 491528 | tf_op jit(solution)/shard_map/ppermute | solution.py:34
  35.8 30.9 %copy-start = (s32[256]{0:T(256)S(1)}, s32[256]{0:T(256)}, u32[]{:S(2)}) copy-start(s32[256]{0:T(256)} %param.9) | copy-start | bytes 3076
  35.8 13.6 %all-to-all-start.1 = ((bf16[16,8,1408]{2,1,0:T(8,128)(2,1)}), bf16[16,8,1408]{2,1,0:T(8,128)(2,1)S(1)}, u32[]{:S(2)}, u32[]{:S(2)}) async-start(bf16[16,8,1408]{2,1,0:T(8,128)(2,1)} %bitcast.5), calls=%async_computation.1 | async-start | bytes 720896 | tf_op jit(solution)/shard_map/all_to_all | solution.py:40
  43.2 6.5 %collective-permute-start.7 = (bf16[64,1152]{1,0:T(8,128)(2,1)S(1)}, bf16[64,1152]{1,0:T(8,128)(2,1)S(1)}, u32[]{:S(2)}, u32[]{:S(2)}) collective-permute-start(bf16[64,1152]{1,0:T(8,128)(2,1)S(1)} %get-tuple-element.36), channel_id=1, source_target_pairs={{0,1},{1,0},{2,3},{3,2},{4,5},{5,4},{6,7},{7,6},{8,9},{9,8},{10,11... | collective-permute-start | bytes 442376 | tf_op jit(solution)/shard_map/ppermute | solution.py:34
  49.6 1.3 %collective-permute-start.8 = (f32[8,256]{1,0:T(8,128)S(1)}, f32[8,256]{1,0:T(8,128)S(1)}, u32[]{:S(2)}, u32[]{:S(2)}) collective-permute-start(f32[8,256]{1,0:T(8,128)S(1)} %get-tuple-element.40.totals_ref), channel_id=1, source_target_pairs={{0,1},{1,0},{2,3},{3,2},{4,5},{5,4},{6,7},{7,6},{8,9},{9,8},{10,11... | collective-permute-start | bytes 24584 | tf_op jit(solution)/shard_map/ppermute | solution.py:34
  51.5 16.6 %all-to-all-start.2 = ((bf16[8,8,1664]{2,1,0:T(8,128)(2,1)}), bf16[8,8,1664]{2,1,0:T(8,128)(2,1)S(1)}, u32[]{:S(2)}, u32[]{:S(2)}) async-start(bf16[8,8,1664]{2,1,0:T(8,128)(2,1)} %shard_map.106), calls=%async_computation.2 | async-start | bytes 425984 | tf_op jit(solution)/shard_map/all_to_all | solution.py:40
  56.0 2.8 %collective-permute-start.10 = (f32[1,1152]{1,0:T(1,128)S(1)}, f32[1,1152]{1,0:T(1,128)S(1)}, u32[]{:S(2)}, u32[]{:S(2)}) collective-permute-start(f32[1,1152]{1,0:T(1,128)S(1)} %get-tuple-element.45), channel_id=1, source_target_pairs={{0,1},{2,3},{4,5},{6,7},{8,9},{10,11},{12,13},{14,15},{16,17},{18,... | collective-permute-start | bytes 13832 | tf_op jit(solution)/shard_map/ppermute | solution.py:29
  57.5 9.2 %collective-permute-start.9 = (f32[1,1152]{1,0:T(1,128)S(1)}, f32[1,1152]{1,0:T(1,128)S(1)}, u32[]{:S(2)}, u32[]{:S(2)}) collective-permute-start(f32[1,1152]{1,0:T(1,128)S(1)} %get-tuple-element.45), channel_id=1, source_target_pairs={{1,2},{3,4},{5,6},{7,8},{9,10},{11,12},{13,14},{15,16},{17,18},{19... | collective-permute-start | bytes 13832 | tf_op jit(solution)/shard_map/ppermute | solution.py:29

commit v8 on v6

--- a/solution.py
+++ b/solution.py
@@ -20,10 +20,9 @@
 FROM = (0, 2, 4, 6, 1, 3, 5, 7)
 
 
-def from_behind(value, by):
+def from_beside(value, by):
     count = lax.axis_size(DP)
-    pairs = [(i, i + by) for i in range(count) if 0 <= i + by < count]
-    return lax.ppermute(value, DP, pairs)
+    return lax.ppermute(value, DP, [(i, (i + by) % count) for i in range(count)])
 
 
 def exchange(value, axis, bit):
@@ -238,7 +237,7 @@
         )
     )
 
-    arrived = from_behind(spill, -1)
+    arrived = from_beside(spill, -1)
     near = [row]
     for step in FROM[1:4]:
         near.append(exchange(row, Z, step))
@@ -270,7 +269,7 @@
         lax.axis_index(Z)[None], keep, came, totals, other
     )
     line_back = to_all(blocks, Z)
-    behind = from_behind(last, 1)
+    behind = from_beside(last, 1)
     (token_grad,) = local(token_rows, [VMEM] * 3, ((tokens, width), F32))(ids, pooled_grad, behind)
     image_grad, gain_grad, scalars = local(
         functools.partial(finish, count=float(total_pairs * total_pairs)), [VMEM] * 3,

time: 67 us -> 65.5 us (0.978)
  starting transfers between devices: 36.9 us -> 35.5 us
    ppermute x2, starting transfers between devices: 8.08 us -> 4.27 us  [from_beside(): lax.ppermute(value, DP, [(i, (i + by) % count) for i in range(count)])]
    all_to_all x3, starting transfers between devices: 19.8 us -> 22.1 us  [to_all(): lax.all_to_all(blocks, axes, 0, 0, tiled=True, axis_index_groups=backward)]
where the time goes in v8:
time: 65.5 us; the launch traced here: 64.8 us
  starting transfers between devices  35.5 us (54%)
  waiting for transfers between devices  20.5 us (31%)
  Pallas kernels  6.78 us (10%)
  between operations  2.05 us (3%)
    all_to_all x3, starting transfers between devices, to_all(): lax.all_to_all(blocks, axes, 0, 0, tiled=True, axis_index_groups=backward)  22.1 us
    ppermute x7, starting transfers between devices, exchange(): lax.ppermute(value, axis, [(i, i ^ bit) for i in range(lax.axis_size(axis...  9.04 us
    ppermute x2, waiting for transfers between devices, from_beside(): lax.ppermute(value, DP, [(i, (i + by) % count) for i in range(count)])  8.63 us
    all_to_all x3, waiting for transfers between devices, to_all(): lax.all_to_all(blocks, axes, 0, 0, tiled=True, axis_index_groups=backward)  6.26 us
    ppermute x7, waiting for transfers between devices, exchange(): lax.ppermute(value, axis, [(i, i ^ bit) for i in range(lax.axis_size(axis...  5.63 us
    ppermute x2, starting transfers between devices, from_beside(): lax.ppermute(value, DP, [(i, (i + by) % count) for i in range(count)])  4.27 us
    pallas_call x1, Pallas kernels, per_device(): local(pair_math, [VMEM] * 5, ((plane * pairs, wide + LANES), BF16), ((dep...  1.53 us
    pallas_call x1, Pallas kernels, per_device(): local(token_rows, [VMEM] * 3, ((tokens, width), F32))  1.43 us
  transfers between devices with their start and end apart: 12, of which 6 were waited for; matrix products, arithmetic and copies ran while one was open for 0% of the time, Pallas kernels for 4%

profile of v8, /device:TPU:8, one launch (start us, length us, event | category | flops | bytes accessed | tf_op | source)
XLA Modules:
  0.0 64.8 jit_solution(12484862633277510082)
XLA Ops:
  0.6 1.4 %shard_map.102 = (bf16[8,1280]{1,0:T(8,128)(2,1)S(1)}, f32[8,1152]{1,0:T(8,128)S(1)}, f32[8,1]{1,0:T(8,128)S(1)}, f32[8,1152]{1,0:T(8,128)S(1)}, f32[1,1152]{1,0...) custom-call(s32[8]{0:T(128)} %groups_hbm.1, s32[1,256]{1,0:T(1,128)} %bitcast.9, ...), custom_call_target="tpu_custom_call" | custom-call | tf_op jit(solution)/shard_map/pallas_call | solution.py:224
  2.0 6.4 %collective-permute-start.2 = (bf16[8,1280]{1,0:T(8,128)(2,1)S(1)}, bf16[8,1280]{1,0:T(8,128)(2,1)S(1)}, u32[]{:S(2)}, u32[]{:S(2)}) collective-permute-start(bf16[8,1280]{1,0:T(8,128)(2,1)S(1)} %get-tuple-element.26), channel_id=1, source_target_pairs={{0,12},{2,14},{4,8},{6,10},{8,4},{10,6},{12,0},{14,2},{1,13},{3,15... | collective-permute-start | bytes 61448 | tf_op jit(solution)/shard_map/ppermute | solution.py:29
  8.4 1.0 %collective-permute-start.1 = (bf16[8,1280]{1,0:T(8,128)(2,1)S(1)}, bf16[8,1280]{1,0:T(8,128)(2,1)S(1)}, u32[]{:S(2)}, u32[]{:S(2)}) collective-permute-start(bf16[8,1280]{1,0:T(8,128)(2,1)S(1)} %get-tuple-element.26), channel_id=1, source_target_pairs={{0,8},{2,10},{4,12},{6,14},{8,0},{10,2},{12,4},{14,6},{1,9},{3,11}... | collective-permute-start | bytes 61448 | tf_op jit(solution)/shard_map/ppermute | solution.py:29
  9.4 1.5 %collective-permute-start = (bf16[8,1280]{1,0:T(8,128)(2,1)S(1)}, bf16[8,1280]{1,0:T(8,128)(2,1)S(1)}, u32[]{:S(2)}, u32[]{:S(2)}) collective-permute-start(bf16[8,1280]{1,0:T(8,128)(2,1)S(1)} %get-tuple-element.26), channel_id=1, source_target_pairs={{0,4},{2,6},{4,0},{6,2},{8,12},{10,14},{12,8},{14,10},{1,5},{3,7},... | collective-permute-start | bytes 61448 | tf_op jit(solution)/shard_map/ppermute | solution.py:29
  10.9 4.3 %collective-permute-start.5 = (f32[1,1152]{1,0:T(1,128)S(1)}, f32[1,1152]{1,0:T(1,128)S(1)}, u32[]{:S(2)}, u32[]{:S(2)}) collective-permute-start(f32[1,1152]{1,0:T(1,128)S(1)} %get-tuple-element.32), channel_id=1, source_target_pairs={{0,255},{1,0},{2,1},{3,2},{4,3},{5,4},{6,5},{7,6},{8,7},{9,8},{10,... | collective-permute-start | bytes 13832 | tf_op jit(solution)/shard_map/ppermute | solution.py:25
  15.1 1.3 %collective-permute-done.5.arrived_ref = f32[1,1152]{1,0:T(1,128)S(1)} collective-permute-done((f32[1,1152]{1,0:T(1,128)S(1)}, f32[1,1152]{1,0:T(1,128)S(1)}, u32[]{:S(2)}, u32[]{:S(2)}) %collective-permute-start.5) | collective-permute-done | bytes 4640 | tf_op jit(solution)/shard_map/ppermute | solution.py:25
  16.5 0.9 %shard_map.103 = (bf16[16,8,1280]{2,1,0:T(8,128)(2,1)}, f32[8,1152]{1,0:T(8,128)S(1)}, f32[8,1]{1,0:T(8,128)S(1)}) custom-call(bf16[8,128]{1,0:T(8,128)(2,1)S(1)} %get-tuple-element.30.tile_ref, f32[8,1152]{1,0:T(8,128)S(1)} %get-tuple-element.31.pooled_ref, f32[1,1152]{1,0:T(1,128)S(1)} %collective-permute-done.5.arrived_ref, ...), custom_call_target="tpu_custom_call" | custom-call | tf_op jit(solution)/shard_map/pallas_call | solution.py:246
  17.3 8.5 %all-to-all-start = ((bf16[16,8,1280]{2,1,0:T(8,128)(2,1)}), bf16[16,8,1280]{2,1,0:T(8,128)(2,1)S(1)}, u32[]{:S(2)}, u32[]{:S(2)}) async-start(bf16[16,8,1280]{2,1,0:T(8,128)(2,1)} %get-tuple-element.34), calls=%async_computation | async-start | bytes 655360 | tf_op jit(solution)/shard_map/all_to_all | solution.py:35
  25.8 0.0 collective-permute-done.2
  25.8 0.0 collective-permute-done.1
  25.8 0.0 collective-permute-done
  25.9 0.1 collective-permute-start.3
  26.0 4.4 %collective-permute-done.3 = bf16[32,1280]{1,0:T(8,128)(2,1)S(1)} collective-permute-done((bf16[32,1280]{1,0:T(8,128)(2,1)S(1)}, bf16[32,1280]{1,0:T(8,128)(2,1)S(1)}, u32[]{:S(2)}, u32[]{:S(2)}) %collective-permute-start.3) | collective-permute-done | bytes 81952 | tf_op jit(solution)/shard_map/ppermute | solution.py:29
  30.4 0.0 collective-permute-start.4
  31.7 0.1 collective-permute-done.4.far_ref
  31.8 0.0 all-to-all-done
  31.8 1.5 %shard_map.104 = (bf16[128,1408]{1,0:T(8,128)(2,1)}, f32[64,1152]{1,0:T(8,128)S(1)}, bf16[64,1152]{1,0:T(8,128)(2,1)S(1)}) custom-call(f32[1,128]{1,0:T(1,128)S(1)} %compare_select_fusion.knobs_ref, bf16[64,1280]{1,0:T(8,128)(2,1)S(1)} %constant_dynamic-update-slice_fusion.near_ref, bf16[64,1280]{1,0:T(8,128)(2,1)S(1)} %collective-permute-done.4.far_ref, ...), custom_call_target="tpu_custom_call" | custom-call | tf_op jit(solution)/shard_map/pallas_call | solution.py:256
  33.3 7.4 %all-to-all-start.1 = ((bf16[16,8,1408]{2,1,0:T(8,128)(2,1)}), bf16[16,8,1408]{2,1,0:T(8,128)(2,1)S(1)}, u32[]{:S(2)}, u32[]{:S(2)}) async-start(bf16[16,8,1408]{2,1,0:T(8,128)(2,1)} %bitcast.5), calls=%async_computation.1 | async-start | bytes 720896 | tf_op jit(solution)/shard_map/all_to_all | solution.py:35
  40.7 0.0 collective-permute-start.6
  40.7 6.3 %all-to-all-done.1.back_ref = bf16[16,8,1408]{2,1,0:T(8,128)(2,1)S(1)} async-done(((bf16[16,8,1408]{2,1,0:T(8,128)(2,1)}), bf16[16,8,1408]{2,1,0:T(8,128)(2,1)S(1)}, u32[]{:S(2)}, u32[]{:S(2)}) %all-to-all-start.1) | async-done | bytes 360480 | tf_op jit(solution)/shard_map/all_to_all | solution.py:35
  46.9 0.1 shard_map.105
  47.1 0.1 collective-permute-start.7
  47.2 0.0 collective-permute-done.6.came_ref
  47.2 1.1 %collective-permute-done.7.other_ref = f32[8,256]{1,0:T(8,128)S(1)} collective-permute-done((f32[8,256]{1,0:T(8,128)S(1)}, f32[8,256]{1,0:T(8,128)S(1)}, u32[]{:S(2)}, u32[]{:S(2)}) %collective-permute-start.7) | collective-permute-done | bytes 8224 | tf_op jit(solution)/shard_map/ppermute | solution.py:29
  48.4 0.7 %shard_map.106 = bf16[8,8,1664]{2,1,0:T(8,128)(2,1)} custom-call(s32[1]{0:T(128)} %bitcast.place_ref, f32[64,1152]{1,0:T(8,128)S(1)} %get-tuple-element.35.keep_ref, bf16[64,1152]{1,0:T(8,128)(2,1)S(1)} %collective-permute-done.6.came_ref, f32[8,256]{1,0:T(8,128)S(1)} %get-tuple-element.40.totals_ref, f32[8,256]{1,0:T(8,128)S(1)} %collective-permute-done.7.other_ref), custom_call_target="tpu_custom_call" | custom-call | tf_op jit(solution)/shard_map/pallas_call | solution.py:268
  49.1 6.3 %all-to-all-start.2 = ((bf16[8,8,1664]{2,1,0:T(8,128)(2,1)}), bf16[8,8,1664]{2,1,0:T(8,128)(2,1)S(1)}, u32[]{:S(2)}, u32[]{:S(2)}) async-start(bf16[8,8,1664]{2,1,0:T(8,128)(2,1)} %shard_map.106), calls=%async_computation.2 | async-start | bytes 425984 | tf_op jit(solution)/shard_map/all_to_all | solution.py:35
  55.4 0.0 collective-permute-start.8
  55.4 7.3 %collective-permute-done.8.behind_ref = f32[1,1152]{1,0:T(1,128)S(1)} collective-permute-done((f32[1,1152]{1,0:T(1,128)S(1)}, f32[1,1152]{1,0:T(1,128)S(1)}, u32[]{:S(2)}, u32[]{:S(2)}) %collective-permute-start.8) | collective-permute-done | bytes 4640 | tf_op jit(solution)/shard_map/ppermute | solution.py:25
  62.7 0.0 copy-done
  62.7 1.4 %shard_map.108 = f32[256,1152]{1,0:T(8,128)} custom-call(s32[1,256]{1,0:T(1,128)S(1)} %bitcast.10, f32[8,1152]{1,0:T(8,128)S(1)} %get-tuple-element.44.grad_ref, f32[1,1152]{1,0:T(1,128)S(1)} %collective-permute-done.8.behind_ref), custom_call_target="tpu_custom_call" | custom-call | tf_op jit(solution)/shard_map/pallas_call | solution.py:273
  64.1 0.0 all-to-all-done.2.back_ref
  64.1 0.7 %shard_map.107 = (f32[8,1152]{1,0:T(8,128)}, f32[1152]{0:T(1024)}, f32[3]{0:T(128)}) custom-call(bf16[8,8,1664]{2,1,0:T(8,128)(2,1)S(1)} %all-to-all-done.2.back_ref, f32[8,1152]{1,0:T(8,128)S(1)} %get-tuple-element.41.unit_ref, f32[8,1]{1,0:T(8,128)S(1)} %get-tuple-element.42.norm_ref), custom_call_target="tpu_custom_call" | custom-call | tf_op jit(solution)/shard_map/pallas_call | solution.py:274
  (8 shorter events, 0.0 us)
Async XLA Ops:
  2.0 23.8 %collective-permute-start.2 = (bf16[8,1280]{1,0:T(8,128)(2,1)S(1)}, bf16[8,1280]{1,0:T(8,128)(2,1)S(1)}, u32[]{:S(2)}, u32[]{:S(2)}) collective-permute-start(bf16[8,1280]{1,0:T(8,128)(2,1)S(1)} %get-tuple-element.26), channel_id=1, source_target_pairs={{0,12},{2,14},{4,8},{6,10},{8,4},{10,6},{12,0},{14,2},{1,13},{3,15... | collective-permute-start | bytes 61448 | tf_op jit(solution)/shard_map/ppermute | solution.py:29
  8.4 17.4 %collective-permute-start.1 = (bf16[8,1280]{1,0:T(8,128)(2,1)S(1)}, bf16[8,1280]{1,0:T(8,128)(2,1)S(1)}, u32[]{:S(2)}, u32[]{:S(2)}) collective-permute-start(bf16[8,1280]{1,0:T(8,128)(2,1)S(1)} %get-tuple-element.26), channel_id=1, source_target_pairs={{0,8},{2,10},{4,12},{6,14},{8,0},{10,2},{12,4},{14,6},{1,9},{3,11}... | collective-permute-start | bytes 61448 | tf_op jit(solution)/shard_map/ppermute | solution.py:29
  9.4 16.4 %collective-permute-start = (bf16[8,1280]{1,0:T(8,128)(2,1)S(1)}, bf16[8,1280]{1,0:T(8,128)(2,1)S(1)}, u32[]{:S(2)}, u32[]{:S(2)}) collective-permute-start(bf16[8,1280]{1,0:T(8,128)(2,1)S(1)} %get-tuple-element.26), channel_id=1, source_target_pairs={{0,4},{2,6},{4,0},{6,2},{8,12},{10,14},{12,8},{14,10},{1,5},{3,7},... | collective-permute-start | bytes 61448 | tf_op jit(solution)/shard_map/ppermute | solution.py:29
  10.9 5.6 %collective-permute-start.5 = (f32[1,1152]{1,0:T(1,128)S(1)}, f32[1,1152]{1,0:T(1,128)S(1)}, u32[]{:S(2)}, u32[]{:S(2)}) collective-permute-start(f32[1,1152]{1,0:T(1,128)S(1)} %get-tuple-element.32), channel_id=1, source_target_pairs={{0,255},{1,0},{2,1},{3,2},{4,3},{5,4},{6,5},{7,6},{8,7},{9,8},{10,... | collective-permute-start | bytes 13832 | tf_op jit(solution)/shard_map/ppermute | solution.py:25
  17.3 14.5 %all-to-all-start = ((bf16[16,8,1280]{2,1,0:T(8,128)(2,1)}), bf16[16,8,1280]{2,1,0:T(8,128)(2,1)S(1)}, u32[]{:S(2)}, u32[]{:S(2)}) async-start(bf16[16,8,1280]{2,1,0:T(8,128)(2,1)} %get-tuple-element.34), calls=%async_computation | async-start | bytes 655360 | tf_op jit(solution)/shard_map/all_to_all | solution.py:35
  25.9 4.5 %collective-permute-start.3 = (bf16[32,1280]{1,0:T(8,128)(2,1)S(1)}, bf16[32,1280]{1,0:T(8,128)(2,1)S(1)}, u32[]{:S(2)}, u32[]{:S(2)}) collective-permute-start(bf16[32,1280]{1,0:T(8,128)(2,1)S(1)} %pad_maximum_fusion), channel_id=1, source_target_pairs={{0,2},{2,0},{4,6},{6,4},{8,10},{10,8},{12,14},{14,12},{1,3},{3,1},... | collective-permute-start | bytes 245768 | tf_op jit(solution)/shard_map/ppermute | solution.py:29
  30.4 1.4 %collective-permute-start.4 = (bf16[64,1280]{1,0:T(8,128)(2,1)S(1)}, bf16[64,1280]{1,0:T(8,128)(2,1)S(1)}, u32[]{:S(2)}, u32[]{:S(2)}) collective-permute-start(bf16[64,1280]{1,0:T(8,128)(2,1)S(1)} %constant_dynamic-update-slice_fusion.near_ref), channel_id=1, source_target_pairs={{0,1},{1,0},{2,3},{3,2},{4,5},{5,4},{6,7},{7,6},{8,9},{9,8},{10,11... | collective-permute-start | bytes 491528 | tf_op jit(solution)/shard_map/ppermute | solution.py:29
  33.3 29.3 %copy-start = (s32[256]{0:T(256)S(1)}, s32[256]{0:T(256)}, u32[]{:S(2)}) copy-start(s32[256]{0:T(256)} %param.9) | copy-start | bytes 3076
  33.3 13.6 %all-to-all-start.1 = ((bf16[16,8,1408]{2,1,0:T(8,128)(2,1)}), bf16[16,8,1408]{2,1,0:T(8,128)(2,1)S(1)}, u32[]{:S(2)}, u32[]{:S(2)}) async-start(bf16[16,8,1408]{2,1,0:T(8,128)(2,1)} %bitcast.5), calls=%async_computation.1 | async-start | bytes 720896 | tf_op jit(solution)/shard_map/all_to_all | solution.py:35
  40.7 6.5 %collective-permute-start.6 = (bf16[64,1152]{1,0:T(8,128)(2,1)S(1)}, bf16[64,1152]{1,0:T(8,128)(2,1)S(1)}, u32[]{:S(2)}, u32[]{:S(2)}) collective-permute-start(bf16[64,1152]{1,0:T(8,128)(2,1)S(1)} %get-tuple-element.36), channel_id=1, source_target_pairs={{0,1},{1,0},{2,3},{3,2},{4,5},{5,4},{6,7},{7,6},{8,9},{9,8},{10,11... | collective-permute-start | bytes 442376 | tf_op jit(solution)/shard_map/ppermute | solution.py:29
  47.1 1.3 %collective-permute-start.7 = (f32[8,256]{1,0:T(8,128)S(1)}, f32[8,256]{1,0:T(8,128)S(1)}, u32[]{:S(2)}, u32[]{:S(2)}) collective-permute-start(f32[8,256]{1,0:T(8,128)S(1)} %get-tuple-element.40.totals_ref), channel_id=1, source_target_pairs={{0,1},{1,0},{2,3},{3,2},{4,5},{5,4},{6,7},{7,6},{8,9},{9,8},{10,11... | collective-permute-start | bytes 24584 | tf_op jit(solution)/shard_map/ppermute | solution.py:29
  49.1 15.1 %all-to-all-start.2 = ((bf16[8,8,1664]{2,1,0:T(8,128)(2,1)}), bf16[8,8,1664]{2,1,0:T(8,128)(2,1)S(1)}, u32[]{:S(2)}, u32[]{:S(2)}) async-start(bf16[8,8,1664]{2,1,0:T(8,128)(2,1)} %shard_map.106), calls=%async_computation.2 | async-start | bytes 425984 | tf_op jit(solution)/shard_map/all_to_all | solution.py:35
  55.4 7.3 %collective-permute-start.8 = (f32[1,1152]{1,0:T(1,128)S(1)}, f32[1,1152]{1,0:T(1,128)S(1)}, u32[]{:S(2)}, u32[]{:S(2)}) collective-permute-start(f32[1,1152]{1,0:T(1,128)S(1)} %get-tuple-element.45), channel_id=1, source_target_pairs={{0,1},{1,2},{2,3},{3,4},{4,5},{5,6},{6,7},{7,8},{8,9},{9,10},{10,1... | collective-permute-start | bytes 13832 | tf_op jit(solution)/shard_map/ppermute | solution.py:25

commit v9 on v8

--- a/solution.py
+++ b/solution.py
@@ -20,9 +20,12 @@
 FROM = (0, 2, 4, 6, 1, 3, 5, 7)
 
 
-def from_beside(value, by):
+def beside(value):
     count = lax.axis_size(DP)
-    return lax.ppermute(value, DP, [(i, (i + by) % count) for i in range(count)])
+    across = [(i, min(max(i - 1 + 2 * (i % 2), 0), count - 1)) for i in range(count)]
+    chip = lax.ppermute(value, DP, across)
+    core = exchange(value, C, 1)
+    return chip, core
 
 
 def exchange(value, axis, bit):
@@ -58,8 +61,8 @@
 
 def prepare(
     groups_hbm, ids_hbm, image_hbm, tokens_hbm, gain_hbm,
-    row_ref, unit_ref, norm_ref, pooled_ref, spill_ref, tile_ref, gain_out,
-    groups_ref, ids_ref, image_ref, tokens_ref, gain_ref, sems,
+    row_ref, unit_ref, norm_ref, pooled_ref, spill_ref, tile_ref, gain_out, sides_out,
+    groups_ref, ids_ref, image_ref, tokens_ref, gain_ref, sems, *, captions,
 ):
     pairs, width = image_hbm.shape
     moves = [
@@ -87,15 +90,21 @@
     gain_out[...] = gain_ref[...][None, :]
     moves[2].wait()
     moves[3].wait()
+    last = ids_ref[:, ids_ref.shape[1] - 1 :]
+    lane = lax.broadcasted_iota(jnp.int32, (1, LANES), 1)
+    odd = (last // pairs) % 2
+    sides_out[...] = jnp.where(lane == 0, 1 - odd, jnp.where(last == captions - 1, 0, odd))
     sums = jnp.dot(members(ids_ref[...], pairs, 1), tokens_ref[...], preferred_element_type=F32)
     pooled_ref[...] = sums[:pairs]
     spill_ref[...] = sums[pairs : pairs + 1]
 
 
-def text_rows(tile_ref, pooled_ref, arrived_ref, gain_ref, rows_ref, unit_ref, norm_ref):
+def text_rows(tile_ref, sides_ref, pooled_ref, chip_ref, core_ref, gain_ref, rows_ref, unit_ref, norm_ref):
     pairs, width = pooled_ref.shape
     last = lax.broadcasted_iota(jnp.int32, (pairs, 1), 0) == pairs - 1
-    pooled = pooled_ref[...] + jnp.where(last, arrived_ref[...], 0.0)
+    sides = sides_ref[...]
+    arrived = jnp.where(sides[:, :1] > 0, core_ref[...], jnp.where(sides[:, 1:2] > 0, chip_ref[...], 0.0))
+    pooled = pooled_ref[...] + jnp.where(last, arrived, 0.0)
     embedded = pooled * gain_ref[...]
     norm = jnp.sqrt(jnp.sum(embedded * embedded, axis=1, keepdims=True))
     unit = embedded / norm
@@ -176,10 +185,11 @@
         out_ref[place, :, width + 2 * LANES :] = low
 
 
-def token_rows(ids_ref, grad_ref, behind_ref, token_out):
+def token_rows(ids_ref, sides_ref, grad_ref, chip_ref, core_ref, token_out):
     pairs, width = grad_ref.shape
+    behind = jnp.where(sides_ref[:, :1] > 0, chip_ref[...], core_ref[...])
     table = jnp.concatenate(
-        [grad_ref[...], jnp.broadcast_to(behind_ref[...], (pairs, width))], axis=0
+        [grad_ref[...], jnp.broadcast_to(behind, (pairs, width))], axis=0
     )
     high = table.astype(BF16)
     low = (table - high.astype(F32)).astype(BF16)
@@ -221,10 +231,10 @@
     plane, depth = lax.axis_size(PLANE), lax.axis_size(Z)
     wide = width + LANES
     ids = caption_ids[None, :]
-    row, unit_image, image_norm, pooled, spill, tile, gain = local(
-        prepare, [HBM] * 5,
+    row, unit_image, image_norm, pooled, spill, tile, gain, sides = local(
+        functools.partial(prepare, captions=total_pairs), [HBM] * 5,
         ((pairs, wide), BF16), ((pairs, width), F32), ((pairs, 1), F32), ((pairs, width), F32),
-        ((1, width), F32), ((pairs, LANES), BF16), ((1, width), F32),
+        ((1, width), F32), ((pairs, LANES), BF16), ((1, width), F32), ((1, LANES), jnp.int32),
         scratch=(
             pltpu.SMEM((pairs,), jnp.int32), pltpu.VMEM((1, tokens), jnp.int32),
             pltpu.VMEM((pairs, width), BF16), pltpu.VMEM((tokens, width), BF16), pltpu.VMEM((width,), F32),
@@ -237,16 +247,16 @@
         )
     )
 
-    arrived = from_beside(spill, -1)
+    arrived = beside(spill)
     near = [row]
     for step in FROM[1:4]:
         near.append(exchange(row, Z, step))
     near = jnp.concatenate(near, axis=0)
     near = jnp.concatenate([near, exchange(near, Z, 1)], axis=0)
     rows, unit_text, text_norm = local(
-        text_rows, [VMEM] * 4,
+        text_rows, [VMEM] * 6,
         ((plane, pairs, wide), BF16), ((pairs, width), F32), ((pairs, 1), F32),
-    )(tile, pooled, arrived, gain)
+    )(tile, sides, pooled, *arrived, gain)
     texts = to_all(rows, PLANE).reshape(plane * pairs, wide)
 
     far = exchange(near, C, 1)
@@ -269,8 +279,8 @@
         lax.axis_index(Z)[None], keep, came, totals, other
     )
     line_back = to_all(blocks, Z)
-    behind = from_beside(last, 1)
-    (token_grad,) = local(token_rows, [VMEM] * 3, ((tokens, width), F32))(ids, pooled_grad, behind)
+    behind = beside(last)
+    (token_grad,) = local(token_rows, [VMEM] * 5, ((tokens, width), F32))(ids, sides, pooled_grad, *behind)
     image_grad, gain_grad, scalars = local(
         functools.partial(finish, count=float(total_pairs * total_pairs)), [VMEM] * 3,
         ((pairs, width), F32), ((width,), F32), ((3,), F32),

time: 65.5 us -> 66.1 us (level)
  starting transfers between devices: 35.5 us -> 40 us
  waiting for transfers between devices: 20.5 us -> 16.6 us
    ppermute x2, starting transfers between devices: 4.27 us -> 14.3 us  [beside(): chip = lax.ppermute(value, DP, across)]
    ppermute x2, waiting for transfers between devices: 8.63 us -> 4.75 us  [beside(): chip = lax.ppermute(value, DP, across)]
    all_to_all x3, starting transfers between devices: 22.1 us -> 18.8 us  [to_all(): lax.all_to_all(blocks, axes, 0, 0, tiled=True, axis_index_groups=backward)]
    ppermute x7 -> x9, starting transfers between devices: 9.04 us -> 6.86 us  [exchange(): lax.ppermute(value, axis, [(i, i ^ bit) for i in range(lax.axis_size(axis...]
    ppermute x7 -> x9, waiting for transfers between devices: 5.63 us -> 5.63 us  [exchange(): lax.ppermute(value, axis, [(i, i ^ bit) for i in range(lax.axis_size(axis...]
  transfers between devices with their start and end apart: 12 -> 14, of which waited for: 6 -> 5; matrix products, arithmetic and copies ran while one was open for 0% -> 0% of each run, Pallas kernels for 4% -> 4%
where the time goes in v9:
time: 66.1 us; the launch traced here: 65.6 us
  starting transfers between devices  40 us (61%)
  waiting for transfers between devices  16.6 us (25%)
  Pallas kernels  6.87 us (10%)
  between operations  2.1 us (3%)
    all_to_all x3, starting transfers between devices, to_all(): lax.all_to_all(blocks, axes, 0, 0, tiled=True, axis_index_groups=backward)  18.8 us
    ppermute x2, starting transfers between devices, beside(): chip = lax.ppermute(value, DP, across)  14.3 us
    ppermute x9, starting transfers between devices, exchange(): lax.ppermute(value, axis, [(i, i ^ bit) for i in range(lax.axis_size(axis...  6.86 us
    all_to_all x3, waiting for transfers between devices, to_all(): lax.all_to_all(blocks, axes, 0, 0, tiled=True, axis_index_groups=backward)  6.25 us
    ppermute x9, waiting for transfers between devices, exchange(): lax.ppermute(value, axis, [(i, i ^ bit) for i in range(lax.axis_size(axis...  5.63 us
    ppermute x2, waiting for transfers between devices, beside(): chip = lax.ppermute(value, DP, across)  4.75 us
    pallas_call x1, Pallas kernels, per_device(): local(pair_math, [VMEM] * 5, ((plane * pairs, wide + LANES), BF16), ((dep...  1.53 us
    pallas_call x1, Pallas kernels, per_device(): local(token_rows, [VMEM] * 5, ((tokens, width), F32))  1.44 us
  transfers between devices with their start and end apart: 14, of which 5 were waited for; matrix products, arithmetic and copies ran while one was open for 0% of the time, Pallas kernels for 4%

profile of v9, /device:TPU:8, one launch (start us, length us, event | category | flops | bytes accessed | tf_op | source)
XLA Modules:
  0.0 65.6 jit_solution(2013796023200091144)
XLA Ops:
  0.6 1.4 %shard_map.102 = (bf16[8,1280]{1,0:T(8,128)(2,1)S(1)}, f32[8,1152]{1,0:T(8,128)S(1)}, f32[8,1]{1,0:T(8,128)S(1)}, f32[8,1152]{1,0:T(8,128)S(1)}, f32[1,1152]{1,0...) custom-call(s32[8]{0:T(128)} %groups_hbm.1, s32[1,256]{1,0:T(1,128)} %bitcast.9, ...), custom_call_target="tpu_custom_call" | custom-call | tf_op jit(solution)/shard_map/pallas_call | solution.py:234
  2.0 0.1 collective-permute-start.6
  2.1 9.9 %collective-permute-start.5 = (f32[1,1152]{1,0:T(1,128)S(1)}, f32[1,1152]{1,0:T(1,128)S(1)}, u32[]{:S(2)}, u32[]{:S(2)}) collective-permute-start(f32[1,1152]{1,0:T(1,128)S(1)} %get-tuple-element.34), channel_id=1, source_target_pairs={{0,0},{1,2},{2,1},{3,4},{4,3},{5,6},{6,5},{7,8},{8,7},{9,10},{10,9... | collective-permute-start | bytes 13832 | tf_op jit(solution)/shard_map/ppermute | solution.py:26
  12.1 0.1 collective-permute-start.2
  12.2 0.1 collective-permute-start.1
  12.3 6.4 %collective-permute-start = (bf16[8,1280]{1,0:T(8,128)(2,1)S(1)}, bf16[8,1280]{1,0:T(8,128)(2,1)S(1)}, u32[]{:S(2)}, u32[]{:S(2)}) collective-permute-start(bf16[8,1280]{1,0:T(8,128)(2,1)S(1)} %get-tuple-element.27), channel_id=1, source_target_pairs={{0,4},{2,6},{4,0},{6,2},{8,12},{10,14},{12,8},{14,10},{1,5},{3,7},... | collective-permute-start | bytes 61448 | tf_op jit(solution)/shard_map/ppermute | solution.py:32
  18.7 0.0 collective-permute-done.6.core_ref
  18.7 0.0 collective-permute-done.5.chip_ref
  18.7 0.9 %shard_map.103 = (bf16[16,8,1280]{2,1,0:T(8,128)(2,1)}, f32[8,1152]{1,0:T(8,128)S(1)}, f32[8,1]{1,0:T(8,128)S(1)}) custom-call(bf16[8,128]{1,0:T(8,128)(2,1)S(1)} %get-tuple-element.31.tile_ref, s32[1,128]{1,0:T(1,128)S(1)} %get-tuple-element.32.sides_ref, f32[8,1152]{1,0:T(8,128)S(1)} %get-tuple-element.33.pooled_ref, ...), custom_call_target="tpu_custom_call" | custom-call | tf_op jit(solution)/shard_map/pallas_call | solution.py:256
  19.6 6.9 %all-to-all-start = ((bf16[16,8,1280]{2,1,0:T(8,128)(2,1)}), bf16[16,8,1280]{2,1,0:T(8,128)(2,1)S(1)}, u32[]{:S(2)}, u32[]{:S(2)}) async-start(bf16[16,8,1280]{2,1,0:T(8,128)(2,1)} %get-tuple-element.36), calls=%async_computation | async-start | bytes 655360 | tf_op jit(solution)/shard_map/all_to_all | solution.py:38
  26.5 0.0 collective-permute-done.2
  26.5 0.0 collective-permute-done.1
  26.6 0.1 collective-permute-start.3
  26.7 4.4 %collective-permute-done.3 = bf16[32,1280]{1,0:T(8,128)(2,1)S(1)} collective-permute-done((bf16[32,1280]{1,0:T(8,128)(2,1)S(1)}, bf16[32,1280]{1,0:T(8,128)(2,1)S(1)}, u32[]{:S(2)}, u32[]{:S(2)}) %collective-permute-start.3) | collective-permute-done | bytes 81952 | tf_op jit(solution)/shard_map/ppermute | solution.py:32
  31.1 0.0 collective-permute-start.4
  32.4 0.1 collective-permute-done.4.far_ref
  32.5 0.0 all-to-all-done
  32.5 1.5 %shard_map.104 = (bf16[128,1408]{1,0:T(8,128)(2,1)}, f32[64,1152]{1,0:T(8,128)S(1)}, bf16[64,1152]{1,0:T(8,128)(2,1)S(1)}) custom-call(f32[1,128]{1,0:T(1,128)S(1)} %compare_select_fusion.knobs_ref, bf16[64,1280]{1,0:T(8,128)(2,1)S(1)} %constant_dynamic-update-slice_fusion.near_ref, bf16[64,1280]{1,0:T(8,128)(2,1)S(1)} %collective-permute-done.4.far_ref, ...), custom_call_target="tpu_custom_call" | custom-call | tf_op jit(solution)/shard_map/pallas_call | solution.py:266
  34.0 7.4 %all-to-all-start.1 = ((bf16[16,8,1408]{2,1,0:T(8,128)(2,1)}), bf16[16,8,1408]{2,1,0:T(8,128)(2,1)S(1)}, u32[]{:S(2)}, u32[]{:S(2)}) async-start(bf16[16,8,1408]{2,1,0:T(8,128)(2,1)} %bitcast.5), calls=%async_computation.1 | async-start | bytes 720896 | tf_op jit(solution)/shard_map/all_to_all | solution.py:38
  41.4 6.2 %all-to-all-done.1.back_ref = bf16[16,8,1408]{2,1,0:T(8,128)(2,1)S(1)} async-done(((bf16[16,8,1408]{2,1,0:T(8,128)(2,1)}), bf16[16,8,1408]{2,1,0:T(8,128)(2,1)S(1)}, u32[]{:S(2)}, u32[]{:S(2)}) %all-to-all-start.1) | async-done | bytes 360480 | tf_op jit(solution)/shard_map/all_to_all | solution.py:38
  47.7 0.1 shard_map.105
  47.8 0.1 collective-permute-start.8
  47.9 0.0 collective-permute-done.7.came_ref
  47.9 1.1 %collective-permute-done.8.other_ref = f32[8,256]{1,0:T(8,128)S(1)} collective-permute-done((f32[8,256]{1,0:T(8,128)S(1)}, f32[8,256]{1,0:T(8,128)S(1)}, u32[]{:S(2)}, u32[]{:S(2)}) %collective-permute-start.8) | collective-permute-done | bytes 8224 | tf_op jit(solution)/shard_map/ppermute | solution.py:32
  49.1 0.7 %shard_map.106 = bf16[8,8,1664]{2,1,0:T(8,128)(2,1)} custom-call(s32[1]{0:T(128)} %bitcast.place_ref, f32[64,1152]{1,0:T(8,128)S(1)} %get-tuple-element.37.keep_ref, bf16[64,1152]{1,0:T(8,128)(2,1)S(1)} %collective-permute-done.7.came_ref, f32[8,256]{1,0:T(8,128)S(1)} %get-tuple-element.42.totals_ref, f32[8,256]{1,0:T(8,128)S(1)} %collective-permute-done.8.other_ref), custom_call_target="tpu_custom_call" | custom-call | tf_op jit(solution)/shard_map/pallas_call | solution.py:278
  49.8 4.5 %all-to-all-start.2 = ((bf16[8,8,1664]{2,1,0:T(8,128)(2,1)}), bf16[8,8,1664]{2,1,0:T(8,128)(2,1)S(1)}, u32[]{:S(2)}, u32[]{:S(2)}) async-start(bf16[8,8,1664]{2,1,0:T(8,128)(2,1)} %shard_map.106), calls=%async_computation.2 | async-start | bytes 425984 | tf_op jit(solution)/shard_map/all_to_all | solution.py:38
  54.3 0.0 collective-permute-start.10
  54.3 4.4 %collective-permute-start.9 = (f32[1,1152]{1,0:T(1,128)S(1)}, f32[1,1152]{1,0:T(1,128)S(1)}, u32[]{:S(2)}, u32[]{:S(2)}) collective-permute-start(f32[1,1152]{1,0:T(1,128)S(1)} %get-tuple-element.47), channel_id=1, source_target_pairs={{0,0},{1,2},{2,1},{3,4},{4,3},{5,6},{6,5},{7,8},{8,7},{9,10},{10,9... | collective-permute-start | bytes 13832 | tf_op jit(solution)/shard_map/ppermute | solution.py:26
  58.7 4.8 %collective-permute-done.9.chip_ref = f32[1,1152]{1,0:T(1,128)S(1)} collective-permute-done((f32[1,1152]{1,0:T(1,128)S(1)}, f32[1,1152]{1,0:T(1,128)S(1)}, u32[]{:S(2)}, u32[]{:S(2)}) %collective-permute-start.9) | collective-permute-done | bytes 4640 | tf_op jit(solution)/shard_map/ppermute | solution.py:26
  63.5 1.4 %shard_map.108 = f32[256,1152]{1,0:T(8,128)} custom-call(s32[1,256]{1,0:T(1,128)S(1)} %bitcast.10, s32[1,128]{1,0:T(1,128)S(1)} %get-tuple-element.32.sides_ref, f32[8,1152]{1,0:T(8,128)S(1)} %get-tuple-element.46.grad_ref, f32[1,1152]{1,0:T(1,128)S(1)} %collective-permute-done.9.chip_ref, f32[1,1152]{1,0:T(1,128)S(1)} %collective-permute-done.10.core_ref), custom_call_target="tpu_custom_call" | custom-call | tf_op jit(solution)/shard_map/pallas_call | solution.py:283
  64.9 0.0 all-to-all-done.2.back_ref
  64.9 0.7 %shard_map.107 = (f32[8,1152]{1,0:T(8,128)}, f32[1152]{0:T(1024)}, f32[3]{0:T(128)}) custom-call(bf16[8,8,1664]{2,1,0:T(8,128)(2,1)S(1)} %all-to-all-done.2.back_ref, f32[8,1152]{1,0:T(8,128)S(1)} %get-tuple-element.43.unit_ref, f32[8,1]{1,0:T(8,128)S(1)} %get-tuple-element.44.norm_ref), custom_call_target="tpu_custom_call" | custom-call | tf_op jit(solution)/shard_map/pallas_call | solution.py:284
  (12 shorter events, 0.0 us)
Async XLA Ops:
  2.0 16.6 %collective-permute-start.6 = (f32[1,1152]{1,0:T(1,128)S(1)}, f32[1,1152]{1,0:T(1,128)S(1)}, u32[]{:S(2)}, u32[]{:S(2)}) collective-permute-start(f32[1,1152]{1,0:T(1,128)S(1)} %get-tuple-element.34), channel_id=1, source_target_pairs={{0,1},{1,0},{2,3},{3,2},{4,5},{5,4},{6,7},{7,6},{8,9},{9,8},{10,11... | collective-permute-start | bytes 13832 | tf_op jit(solution)/shard_map/ppermute | solution.py:32
  2.1 16.5 %collective-permute-start.5 = (f32[1,1152]{1,0:T(1,128)S(1)}, f32[1,1152]{1,0:T(1,128)S(1)}, u32[]{:S(2)}, u32[]{:S(2)}) collective-permute-start(f32[1,1152]{1,0:T(1,128)S(1)} %get-tuple-element.34), channel_id=1, source_target_pairs={{0,0},{1,2},{2,1},{3,4},{4,3},{5,6},{6,5},{7,8},{8,7},{9,10},{10,9... | collective-permute-start | bytes 13832 | tf_op jit(solution)/shard_map/ppermute | solution.py:26
  12.1 14.5 %collective-permute-start.2 = (bf16[8,1280]{1,0:T(8,128)(2,1)S(1)}, bf16[8,1280]{1,0:T(8,128)(2,1)S(1)}, u32[]{:S(2)}, u32[]{:S(2)}) collective-permute-start(bf16[8,1280]{1,0:T(8,128)(2,1)S(1)} %get-tuple-element.27), channel_id=1, source_target_pairs={{0,12},{2,14},{4,8},{6,10},{8,4},{10,6},{12,0},{14,2},{1,13},{3,15... | collective-permute-start | bytes 61448 | tf_op jit(solution)/shard_map/ppermute | solution.py:32
  12.2 14.4 %collective-permute-start.1 = (bf16[8,1280]{1,0:T(8,128)(2,1)S(1)}, bf16[8,1280]{1,0:T(8,128)(2,1)S(1)}, u32[]{:S(2)}, u32[]{:S(2)}) collective-permute-start(bf16[8,1280]{1,0:T(8,128)(2,1)S(1)} %get-tuple-element.27), channel_id=1, source_target_pairs={{0,8},{2,10},{4,12},{6,14},{8,0},{10,2},{12,4},{14,6},{1,9},{3,11}... | collective-permute-start | bytes 61448 | tf_op jit(solution)/shard_map/ppermute | solution.py:32
  12.3 14.3 %collective-permute-start = (bf16[8,1280]{1,0:T(8,128)(2,1)S(1)}, bf16[8,1280]{1,0:T(8,128)(2,1)S(1)}, u32[]{:S(2)}, u32[]{:S(2)}) collective-permute-start(bf16[8,1280]{1,0:T(8,128)(2,1)S(1)} %get-tuple-element.27), channel_id=1, source_target_pairs={{0,4},{2,6},{4,0},{6,2},{8,12},{10,14},{12,8},{14,10},{1,5},{3,7},... | collective-permute-start | bytes 61448 | tf_op jit(solution)/shard_map/ppermute | solution.py:32
  19.6 12.9 %all-to-all-start = ((bf16[16,8,1280]{2,1,0:T(8,128)(2,1)}), bf16[16,8,1280]{2,1,0:T(8,128)(2,1)S(1)}, u32[]{:S(2)}, u32[]{:S(2)}) async-start(bf16[16,8,1280]{2,1,0:T(8,128)(2,1)} %get-tuple-element.36), calls=%async_computation | async-start | bytes 655360 | tf_op jit(solution)/shard_map/all_to_all | solution.py:38
  26.6 4.5 %collective-permute-start.3 = (bf16[32,1280]{1,0:T(8,128)(2,1)S(1)}, bf16[32,1280]{1,0:T(8,128)(2,1)S(1)}, u32[]{:S(2)}, u32[]{:S(2)}) collective-permute-start(bf16[32,1280]{1,0:T(8,128)(2,1)S(1)} %pad_maximum_fusion), channel_id=1, source_target_pairs={{0,2},{2,0},{4,6},{6,4},{8,10},{10,8},{12,14},{14,12},{1,3},{3,1},... | collective-permute-start | bytes 245768 | tf_op jit(solution)/shard_map/ppermute | solution.py:32
  31.1 1.4 %collective-permute-start.4 = (bf16[64,1280]{1,0:T(8,128)(2,1)S(1)}, bf16[64,1280]{1,0:T(8,128)(2,1)S(1)}, u32[]{:S(2)}, u32[]{:S(2)}) collective-permute-start(bf16[64,1280]{1,0:T(8,128)(2,1)S(1)} %constant_dynamic-update-slice_fusion.near_ref), channel_id=1, source_target_pairs={{0,1},{1,0},{2,3},{3,2},{4,5},{5,4},{6,7},{7,6},{8,9},{9,8},{10,11... | collective-permute-start | bytes 491528 | tf_op jit(solution)/shard_map/ppermute | solution.py:32
  34.0 29.4 %copy-start = (s32[256]{0:T(256)S(1)}, s32[256]{0:T(256)}, u32[]{:S(2)}) copy-start(s32[256]{0:T(256)} %param.9) | copy-start | bytes 3076
  34.0 13.6 %all-to-all-start.1 = ((bf16[16,8,1408]{2,1,0:T(8,128)(2,1)}), bf16[16,8,1408]{2,1,0:T(8,128)(2,1)S(1)}, u32[]{:S(2)}, u32[]{:S(2)}) async-start(bf16[16,8,1408]{2,1,0:T(8,128)(2,1)} %bitcast.5), calls=%async_computation.1 | async-start | bytes 720896 | tf_op jit(solution)/shard_map/all_to_all | solution.py:38
  41.4 6.5 %collective-permute-start.7 = (bf16[64,1152]{1,0:T(8,128)(2,1)S(1)}, bf16[64,1152]{1,0:T(8,128)(2,1)S(1)}, u32[]{:S(2)}, u32[]{:S(2)}) collective-permute-start(bf16[64,1152]{1,0:T(8,128)(2,1)S(1)} %get-tuple-element.38), channel_id=1, source_target_pairs={{0,1},{1,0},{2,3},{3,2},{4,5},{5,4},{6,7},{7,6},{8,9},{9,8},{10,11... | collective-permute-start | bytes 442376 | tf_op jit(solution)/shard_map/ppermute | solution.py:32
  47.8 1.3 %collective-permute-start.8 = (f32[8,256]{1,0:T(8,128)S(1)}, f32[8,256]{1,0:T(8,128)S(1)}, u32[]{:S(2)}, u32[]{:S(2)}) collective-permute-start(f32[8,256]{1,0:T(8,128)S(1)} %get-tuple-element.42.totals_ref), channel_id=1, source_target_pairs={{0,1},{1,0},{2,3},{3,2},{4,5},{5,4},{6,7},{7,6},{8,9},{9,8},{10,11... | collective-permute-start | bytes 24584 | tf_op jit(solution)/shard_map/ppermute | solution.py:32
  49.8 15.1 %all-to-all-start.2 = ((bf16[8,8,1664]{2,1,0:T(8,128)(2,1)}), bf16[8,8,1664]{2,1,0:T(8,128)(2,1)S(1)}, u32[]{:S(2)}, u32[]{:S(2)}) async-start(bf16[8,8,1664]{2,1,0:T(8,128)(2,1)} %shard_map.106), calls=%async_computation.2 | async-start | bytes 425984 | tf_op jit(solution)/shard_map/all_to_all | solution.py:38
  54.3 4.4 %collective-permute-start.10 = (f32[1,1152]{1,0:T(1,128)S(1)}, f32[1,1152]{1,0:T(1,128)S(1)}, u32[]{:S(2)}, u32[]{:S(2)}) collective-permute-start(f32[1,1152]{1,0:T(1,128)S(1)} %get-tuple-element.47), channel_id=1, source_target_pairs={{0,1},{1,0},{2,3},{3,2},{4,5},{5,4},{6,7},{7,6},{8,9},{9,8},{10,11... | collective-permute-start | bytes 13832 | tf_op jit(solution)/shard_map/ppermute | solution.py:32
  54.3 9.2 %collective-permute-start.9 = (f32[1,1152]{1,0:T(1,128)S(1)}, f32[1,1152]{1,0:T(1,128)S(1)}, u32[]{:S(2)}, u32[]{:S(2)}) collective-permute-start(f32[1,1152]{1,0:T(1,128)S(1)} %get-tuple-element.47), channel_id=1, source_target_pairs={{0,0},{1,2},{2,1},{3,4},{4,3},{5,6},{6,5},{7,8},{8,7},{9,10},{10,9... | collective-permute-start | bytes 13832 | tf_op jit(solution)/shard_map/ppermute | solution.py:26

commit v10 on v9

--- a/solution.py
+++ b/solution.py
@@ -20,10 +20,11 @@
 FROM = (0, 2, 4, 6, 1, 3, 5, 7)
 
 
-def beside(value):
+def beside(value, ahead):
     count = lax.axis_size(DP)
-    across = [(i, min(max(i - 1 + 2 * (i % 2), 0), count - 1)) for i in range(count)]
-    chip = lax.ppermute(value, DP, across)
+    across = [(i, i - 1 if i % 2 == 0 else i + 1) for i in range(2, count - 3)]
+    across += [(0, 2), (1, 0), (count - 3, count - 1), (count - 2, count - 3), (count - 1, count - 2)]
+    chip = lax.ppermute(value, DP, across if ahead else [(b, a) for a, b in across])
     core = exchange(value, C, 1)
     return chip, core
 
@@ -174,15 +175,19 @@
     places, pairs, _ = out_ref.shape
     width = keep_ref.shape[1]
     total = totals_ref[...] + other_ref[...]
-    high = total.astype(BF16)
-    low = (total - high.astype(F32)).astype(BF16)
+    second = total[:, LANES:]
+    row = lax.broadcasted_iota(jnp.int32, (pairs, LANES), 0)
+    rest, cells = second[1:2] + second[2:3], jnp.where(row == 0, second, 0.0)
+    for r in (1, 2, 3):
+        part = rest.astype(BF16).astype(F32)
+        rest, cells = rest - part, jnp.where(row == r, part, cells)
+    packed = jnp.concatenate([total[:, :LANES], cells], axis=1).astype(BF16)
     for k in range(places):
         rows = slice(pairs * k, pairs * (k + 1))
         block = keep_ref[rows] + came_ref[rows].astype(F32)
         place = places - 1 - (place_ref[0] ^ FROM[k])
         out_ref[place, :, :width] = block.astype(BF16)
-        out_ref[place, :, width : width + 2 * LANES] = high
-        out_ref[place, :, width + 2 * LANES :] = low
+        out_ref[place, :, width:] = packed
 
 
 def token_rows(ids_ref, sides_ref, grad_ref, chip_ref, core_ref, token_out):
@@ -204,10 +209,9 @@
 def finish(back_ref, unit_ref, norm_ref, image_out, gain_out, scalars_out, *, count):
     width = unit_ref.shape[1]
     total = jnp.sum(back_ref[...].astype(F32), axis=0)
-    first = total[:, width : width + LANES] + total[:, width + 2 * LANES : width + 3 * LANES]
-    second = total[:, width + LANES : width + 2 * LANES] + total[:, width + 3 * LANES :]
+    first, second = total[:, width : width + LANES], total[:, width + LANES :]
     gain_out[...] = jnp.concatenate([first[r] for r in range(8)] + [second[0]])
-    scalars_out[...] = ((second[1] + second[2]) / count)[:3]
+    scalars_out[...] = ((second[1] + second[2] + second[3]) / count)[:3]
     grad, unit = total[:, :width], unit_ref[...]
     grad = grad - unit * jnp.sum(unit * grad, axis=1, keepdims=True)
     image_out[...] = grad / norm_ref[...]
@@ -247,7 +251,7 @@
         )
     )
 
-    arrived = beside(spill)
+    arrived = beside(spill, True)
     near = [row]
     for step in FROM[1:4]:
         near.append(exchange(row, Z, step))
@@ -275,11 +279,11 @@
         ((pairs, width), F32), ((1, width), F32), ((pairs, 2 * LANES), F32),
     )(back, unit_text, text_norm, gain)
     other = exchange(totals, C, 1)
-    (blocks,) = local(pack, [SMEM] + [VMEM] * 4, ((depth, pairs, width + 4 * LANES), BF16))(
+    (blocks,) = local(pack, [SMEM] + [VMEM] * 4, ((depth, pairs, width + 2 * LANES), BF16))(
         lax.axis_index(Z)[None], keep, came, totals, other
     )
     line_back = to_all(blocks, Z)
-    behind = beside(last)
+    behind = beside(last, False)
     (token_grad,) = local(token_rows, [VMEM] * 5, ((tokens, width), F32))(ids, sides, pooled_grad, *behind)
     image_grad, gain_grad, scalars = local(
         functools.partial(finish, count=float(total_pairs * total_pairs)), [VMEM] * 3,

time: 66.1 us -> 62.4 us (0.944)
  starting transfers between devices: 40 us -> 36.1 us
    ppermute x2, starting transfers between devices: 14.3 us -> 10.6 us  [beside(): lax.ppermute(value, DP, across if ahead else [(b, a) for a, b in across])]
where the time goes in v10:
time: 62.4 us; the launch traced here: 62 us
  starting transfers between devices  36.1 us (58%)
  waiting for transfers between devices  16.9 us (27%)
  Pallas kernels  6.86 us (11%)
  between operations  2.06 us (3%)
    all_to_all x3, starting transfers between devices, to_all(): lax.all_to_all(blocks, axes, 0, 0, tiled=True, axis_index_groups=backward)  18.8 us
    ppermute x2, starting transfers between devices, beside(): lax.ppermute(value, DP, across if ahead else [(b, a) for a, b in across])  10.6 us
    ppermute x9, starting transfers between devices, exchange(): lax.ppermute(value, axis, [(i, i ^ bit) for i in range(lax.axis_size(axis...  6.78 us
    all_to_all x3, waiting for transfers between devices, to_all(): lax.all_to_all(blocks, axes, 0, 0, tiled=True, axis_index_groups=backward)  6.26 us
    ppermute x9, waiting for transfers between devices, exchange(): lax.ppermute(value, axis, [(i, i ^ bit) for i in range(lax.axis_size(axis...  5.63 us
    ppermute x2, waiting for transfers between devices, beside(): lax.ppermute(value, DP, across if ahead else [(b, a) for a, b in across])  4.98 us
    pallas_call x1, Pallas kernels, per_device(): local(pair_math, [VMEM] * 5, ((plane * pairs, wide + LANES), BF16), ((dep...  1.53 us
    pallas_call x1, Pallas kernels, per_device(): local(token_rows, [VMEM] * 5, ((tokens, width), F32))  1.44 us
  transfers between devices with their start and end apart: 14, of which 5 were waited for; matrix products, arithmetic and copies ran while one was open for 0% of the time, Pallas kernels for 4%

profile of v10, /device:TPU:8, one launch (start us, length us, event | category | flops | bytes accessed | tf_op | source)
XLA Modules:
  0.0 62.0 jit_solution(15244990323526350838)
XLA Ops:
  0.6 1.4 %shard_map.102 = (bf16[8,1280]{1,0:T(8,128)(2,1)S(1)}, f32[8,1152]{1,0:T(8,128)S(1)}, f32[8,1]{1,0:T(8,128)S(1)}, f32[8,1152]{1,0:T(8,128)S(1)}, f32[1,1152]{1,0...) custom-call(s32[8]{0:T(128)} %groups_hbm.1, s32[1,256]{1,0:T(1,128)} %bitcast.9, ...), custom_call_target="tpu_custom_call" | custom-call | tf_op jit(solution)/shard_map/pallas_call | solution.py:238
  2.0 0.1 collective-permute-start.6
  2.1 8.0 %collective-permute-start.5 = (f32[1,1152]{1,0:T(1,128)S(1)}, f32[1,1152]{1,0:T(1,128)S(1)}, u32[]{:S(2)}, u32[]{:S(2)}) collective-permute-start(f32[1,1152]{1,0:T(1,128)S(1)} %get-tuple-element.34), channel_id=1, source_target_pairs={{2,1},{3,4},{4,3},{5,6},{6,5},{7,8},{8,7},{9,10},{10,9},{11,12},{1... | collective-permute-start | bytes 13832 | tf_op jit(solution)/shard_map/ppermute | solution.py:27
  10.2 0.0 collective-permute-start.2
  10.2 0.0 collective-permute-start.1
  10.2 6.5 %collective-permute-start = (bf16[8,1280]{1,0:T(8,128)(2,1)S(1)}, bf16[8,1280]{1,0:T(8,128)(2,1)S(1)}, u32[]{:S(2)}, u32[]{:S(2)}) collective-permute-start(bf16[8,1280]{1,0:T(8,128)(2,1)S(1)} %get-tuple-element.27), channel_id=1, source_target_pairs={{0,4},{2,6},{4,0},{6,2},{8,12},{10,14},{12,8},{14,10},{1,5},{3,7},... | collective-permute-start | bytes 61448 | tf_op jit(solution)/shard_map/ppermute | solution.py:33
  16.7 0.0 collective-permute-done.6.core_ref
  16.7 0.0 collective-permute-done.5.chip_ref
  16.7 0.9 %shard_map.103 = (bf16[16,8,1280]{2,1,0:T(8,128)(2,1)}, f32[8,1152]{1,0:T(8,128)S(1)}, f32[8,1]{1,0:T(8,128)S(1)}) custom-call(bf16[8,128]{1,0:T(8,128)(2,1)S(1)} %get-tuple-element.31.tile_ref, s32[1,128]{1,0:T(1,128)S(1)} %get-tuple-element.32.sides_ref, f32[8,1152]{1,0:T(8,128)S(1)} %get-tuple-element.33.pooled_ref, ...), custom_call_target="tpu_custom_call" | custom-call | tf_op jit(solution)/shard_map/pallas_call | solution.py:260
  17.6 6.9 %all-to-all-start = ((bf16[16,8,1280]{2,1,0:T(8,128)(2,1)}), bf16[16,8,1280]{2,1,0:T(8,128)(2,1)S(1)}, u32[]{:S(2)}, u32[]{:S(2)}) async-start(bf16[16,8,1280]{2,1,0:T(8,128)(2,1)} %get-tuple-element.36), calls=%async_computation | async-start | bytes 655360 | tf_op jit(solution)/shard_map/all_to_all | solution.py:39
  24.5 0.0 collective-permute-done.2
  24.5 0.0 collective-permute-done.1
  24.6 0.1 collective-permute-start.3
  24.7 4.4 %collective-permute-done.3 = bf16[32,1280]{1,0:T(8,128)(2,1)S(1)} collective-permute-done((bf16[32,1280]{1,0:T(8,128)(2,1)S(1)}, bf16[32,1280]{1,0:T(8,128)(2,1)S(1)}, u32[]{:S(2)}, u32[]{:S(2)}) %collective-permute-start.3) | collective-permute-done | bytes 81952 | tf_op jit(solution)/shard_map/ppermute | solution.py:33
  30.4 0.1 collective-permute-done.4.far_ref
  30.5 0.0 all-to-all-done
  30.5 1.5 %shard_map.104 = (bf16[128,1408]{1,0:T(8,128)(2,1)}, f32[64,1152]{1,0:T(8,128)S(1)}, bf16[64,1152]{1,0:T(8,128)(2,1)S(1)}) custom-call(f32[1,128]{1,0:T(1,128)S(1)} %compare_select_fusion.knobs_ref, bf16[64,1280]{1,0:T(8,128)(2,1)S(1)} %constant_dynamic-update-slice_fusion.near_ref, bf16[64,1280]{1,0:T(8,128)(2,1)S(1)} %collective-permute-done.4.far_ref, ...), custom_call_target="tpu_custom_call" | custom-call | tf_op jit(solution)/shard_map/pallas_call | solution.py:270
  32.1 7.4 %all-to-all-start.1 = ((bf16[16,8,1408]{2,1,0:T(8,128)(2,1)}), bf16[16,8,1408]{2,1,0:T(8,128)(2,1)S(1)}, u32[]{:S(2)}, u32[]{:S(2)}) async-start(bf16[16,8,1408]{2,1,0:T(8,128)(2,1)} %bitcast.5), calls=%async_computation.1 | async-start | bytes 720896 | tf_op jit(solution)/shard_map/all_to_all | solution.py:39
  39.4 6.3 %all-to-all-done.1.back_ref = bf16[16,8,1408]{2,1,0:T(8,128)(2,1)S(1)} async-done(((bf16[16,8,1408]{2,1,0:T(8,128)(2,1)}), bf16[16,8,1408]{2,1,0:T(8,128)(2,1)S(1)}, u32[]{:S(2)}, u32[]{:S(2)}) %all-to-all-start.1) | async-done | bytes 360480 | tf_op jit(solution)/shard_map/all_to_all | solution.py:39
  45.7 0.1 shard_map.105
  45.8 0.1 collective-permute-start.8
  45.9 0.0 collective-permute-done.7.came_ref
  45.9 1.1 %collective-permute-done.8.other_ref = f32[8,256]{1,0:T(8,128)S(1)} collective-permute-done((f32[8,256]{1,0:T(8,128)S(1)}, f32[8,256]{1,0:T(8,128)S(1)}, u32[]{:S(2)}, u32[]{:S(2)}) %collective-permute-start.8) | collective-permute-done | bytes 8224 | tf_op jit(solution)/shard_map/ppermute | solution.py:33
  47.1 0.7 %shard_map.106 = bf16[8,8,1408]{2,1,0:T(8,128)(2,1)} custom-call(s32[1]{0:T(128)} %bitcast.place_ref, f32[64,1152]{1,0:T(8,128)S(1)} %get-tuple-element.37.keep_ref, bf16[64,1152]{1,0:T(8,128)(2,1)S(1)} %collective-permute-done.7.came_ref, f32[8,256]{1,0:T(8,128)S(1)} %get-tuple-element.42.totals_ref, f32[8,256]{1,0:T(8,128)S(1)} %collective-permute-done.8.other_ref), custom_call_target="tpu_custom_call" | custom-call | tf_op jit(solution)/shard_map/pallas_call | solution.py:282
  47.8 4.5 %all-to-all-start.2 = ((bf16[8,8,1408]{2,1,0:T(8,128)(2,1)}), bf16[8,8,1408]{2,1,0:T(8,128)(2,1)S(1)}, u32[]{:S(2)}, u32[]{:S(2)}) async-start(bf16[8,8,1408]{2,1,0:T(8,128)(2,1)} %shard_map.106), calls=%async_computation.2 | async-start | bytes 360448 | tf_op jit(solution)/shard_map/all_to_all | solution.py:39
  52.3 0.0 collective-permute-start.10
  52.3 2.5 %collective-permute-start.9 = (f32[1,1152]{1,0:T(1,128)S(1)}, f32[1,1152]{1,0:T(1,128)S(1)}, u32[]{:S(2)}, u32[]{:S(2)}) collective-permute-start(f32[1,1152]{1,0:T(1,128)S(1)} %get-tuple-element.47), channel_id=1, source_target_pairs={{1,2},{4,3},{3,4},{6,5},{5,6},{8,7},{7,8},{10,9},{9,10},{12,11},{1... | collective-permute-start | bytes 13832 | tf_op jit(solution)/shard_map/ppermute | solution.py:27
  54.8 0.0 collective-permute-done.10.core_ref
  54.8 5.0 %collective-permute-done.9.chip_ref = f32[1,1152]{1,0:T(1,128)S(1)} collective-permute-done((f32[1,1152]{1,0:T(1,128)S(1)}, f32[1,1152]{1,0:T(1,128)S(1)}, u32[]{:S(2)}, u32[]{:S(2)}) %collective-permute-start.9) | collective-permute-done | bytes 4640 | tf_op jit(solution)/shard_map/ppermute | solution.py:27
  59.8 1.4 %shard_map.108 = f32[256,1152]{1,0:T(8,128)} custom-call(s32[1,256]{1,0:T(1,128)S(1)} %bitcast.10, s32[1,128]{1,0:T(1,128)S(1)} %get-tuple-element.32.sides_ref, f32[8,1152]{1,0:T(8,128)S(1)} %get-tuple-element.46.grad_ref, f32[1,1152]{1,0:T(1,128)S(1)} %collective-permute-done.9.chip_ref, f32[1,1152]{1,0:T(1,128)S(1)} %collective-permute-done.10.core_ref), custom_call_target="tpu_custom_call" | custom-call | tf_op jit(solution)/shard_map/pallas_call | solution.py:287
  61.2 0.0 all-to-all-done.2.back_ref
  61.2 0.7 %shard_map.107 = (f32[8,1152]{1,0:T(8,128)}, f32[1152]{0:T(1024)}, f32[3]{0:T(128)}) custom-call(bf16[8,8,1408]{2,1,0:T(8,128)(2,1)S(1)} %all-to-all-done.2.back_ref, f32[8,1152]{1,0:T(8,128)S(1)} %get-tuple-element.43.unit_ref, f32[8,1]{1,0:T(8,128)S(1)} %get-tuple-element.44.norm_ref), custom_call_target="tpu_custom_call" | custom-call | tf_op jit(solution)/shard_map/pallas_call | solution.py:288
  (12 shorter events, 0.0 us)
Async XLA Ops:
  2.0 14.6 %collective-permute-start.6 = (f32[1,1152]{1,0:T(1,128)S(1)}, f32[1,1152]{1,0:T(1,128)S(1)}, u32[]{:S(2)}, u32[]{:S(2)}) collective-permute-start(f32[1,1152]{1,0:T(1,128)S(1)} %get-tuple-element.34), channel_id=1, source_target_pairs={{0,1},{1,0},{2,3},{3,2},{4,5},{5,4},{6,7},{7,6},{8,9},{9,8},{10,11... | collective-permute-start | bytes 13832 | tf_op jit(solution)/shard_map/ppermute | solution.py:33
  2.1 14.5 %collective-permute-start.5 = (f32[1,1152]{1,0:T(1,128)S(1)}, f32[1,1152]{1,0:T(1,128)S(1)}, u32[]{:S(2)}, u32[]{:S(2)}) collective-permute-start(f32[1,1152]{1,0:T(1,128)S(1)} %get-tuple-element.34), channel_id=1, source_target_pairs={{2,1},{3,4},{4,3},{5,6},{6,5},{7,8},{8,7},{9,10},{10,9},{11,12},{1... | collective-permute-start | bytes 13832 | tf_op jit(solution)/shard_map/ppermute | solution.py:27
  10.2 14.4 %collective-permute-start.2 = (bf16[8,1280]{1,0:T(8,128)(2,1)S(1)}, bf16[8,1280]{1,0:T(8,128)(2,1)S(1)}, u32[]{:S(2)}, u32[]{:S(2)}) collective-permute-start(bf16[8,1280]{1,0:T(8,128)(2,1)S(1)} %get-tuple-element.27), channel_id=1, source_target_pairs={{0,12},{2,14},{4,8},{6,10},{8,4},{10,6},{12,0},{14,2},{1,13},{3,15... | collective-permute-start | bytes 61448 | tf_op jit(solution)/shard_map/ppermute | solution.py:33
  10.2 14.4 %collective-permute-start.1 = (bf16[8,1280]{1,0:T(8,128)(2,1)S(1)}, bf16[8,1280]{1,0:T(8,128)(2,1)S(1)}, u32[]{:S(2)}, u32[]{:S(2)}) collective-permute-start(bf16[8,1280]{1,0:T(8,128)(2,1)S(1)} %get-tuple-element.27), channel_id=1, source_target_pairs={{0,8},{2,10},{4,12},{6,14},{8,0},{10,2},{12,4},{14,6},{1,9},{3,11}... | collective-permute-start | bytes 61448 | tf_op jit(solution)/shard_map/ppermute | solution.py:33
  10.2 14.4 %collective-permute-start = (bf16[8,1280]{1,0:T(8,128)(2,1)S(1)}, bf16[8,1280]{1,0:T(8,128)(2,1)S(1)}, u32[]{:S(2)}, u32[]{:S(2)}) collective-permute-start(bf16[8,1280]{1,0:T(8,128)(2,1)S(1)} %get-tuple-element.27), channel_id=1, source_target_pairs={{0,4},{2,6},{4,0},{6,2},{8,12},{10,14},{12,8},{14,10},{1,5},{3,7},... | collective-permute-start | bytes 61448 | tf_op jit(solution)/shard_map/ppermute | solution.py:33
  17.6 12.9 %all-to-all-start = ((bf16[16,8,1280]{2,1,0:T(8,128)(2,1)}), bf16[16,8,1280]{2,1,0:T(8,128)(2,1)S(1)}, u32[]{:S(2)}, u32[]{:S(2)}) async-start(bf16[16,8,1280]{2,1,0:T(8,128)(2,1)} %get-tuple-element.36), calls=%async_computation | async-start | bytes 655360 | tf_op jit(solution)/shard_map/all_to_all | solution.py:39
  24.6 4.5 %collective-permute-start.3 = (bf16[32,1280]{1,0:T(8,128)(2,1)S(1)}, bf16[32,1280]{1,0:T(8,128)(2,1)S(1)}, u32[]{:S(2)}, u32[]{:S(2)}) collective-permute-start(bf16[32,1280]{1,0:T(8,128)(2,1)S(1)} %pad_maximum_fusion), channel_id=1, source_target_pairs={{0,2},{2,0},{4,6},{6,4},{8,10},{10,8},{12,14},{14,12},{1,3},{3,1},... | collective-permute-start | bytes 245768 | tf_op jit(solution)/shard_map/ppermute | solution.py:33
  29.1 1.4 %collective-permute-start.4 = (bf16[64,1280]{1,0:T(8,128)(2,1)S(1)}, bf16[64,1280]{1,0:T(8,128)(2,1)S(1)}, u32[]{:S(2)}, u32[]{:S(2)}) collective-permute-start(bf16[64,1280]{1,0:T(8,128)(2,1)S(1)} %constant_dynamic-update-slice_fusion.near_ref), channel_id=1, source_target_pairs={{0,1},{1,0},{2,3},{3,2},{4,5},{5,4},{6,7},{7,6},{8,9},{9,8},{10,11... | collective-permute-start | bytes 491528 | tf_op jit(solution)/shard_map/ppermute | solution.py:33
  32.0 27.7 %copy-start = (s32[256]{0:T(256)S(1)}, s32[256]{0:T(256)}, u32[]{:S(2)}) copy-start(s32[256]{0:T(256)} %param.9) | copy-start | bytes 3076
  32.1 13.6 %all-to-all-start.1 = ((bf16[16,8,1408]{2,1,0:T(8,128)(2,1)}), bf16[16,8,1408]{2,1,0:T(8,128)(2,1)S(1)}, u32[]{:S(2)}, u32[]{:S(2)}) async-start(bf16[16,8,1408]{2,1,0:T(8,128)(2,1)} %bitcast.5), calls=%async_computation.1 | async-start | bytes 720896 | tf_op jit(solution)/shard_map/all_to_all | solution.py:39
  39.4 6.5 %collective-permute-start.7 = (bf16[64,1152]{1,0:T(8,128)(2,1)S(1)}, bf16[64,1152]{1,0:T(8,128)(2,1)S(1)}, u32[]{:S(2)}, u32[]{:S(2)}) collective-permute-start(bf16[64,1152]{1,0:T(8,128)(2,1)S(1)} %get-tuple-element.38), channel_id=1, source_target_pairs={{0,1},{1,0},{2,3},{3,2},{4,5},{5,4},{6,7},{7,6},{8,9},{9,8},{10,11... | collective-permute-start | bytes 442376 | tf_op jit(solution)/shard_map/ppermute | solution.py:33
  45.8 1.3 %collective-permute-start.8 = (f32[8,256]{1,0:T(8,128)S(1)}, f32[8,256]{1,0:T(8,128)S(1)}, u32[]{:S(2)}, u32[]{:S(2)}) collective-permute-start(f32[8,256]{1,0:T(8,128)S(1)} %get-tuple-element.42.totals_ref), channel_id=1, source_target_pairs={{0,1},{1,0},{2,3},{3,2},{4,5},{5,4},{6,7},{7,6},{8,9},{9,8},{10,11... | collective-permute-start | bytes 24584 | tf_op jit(solution)/shard_map/ppermute | solution.py:33
  47.8 13.5 %all-to-all-start.2 = ((bf16[8,8,1408]{2,1,0:T(8,128)(2,1)}), bf16[8,8,1408]{2,1,0:T(8,128)(2,1)S(1)}, u32[]{:S(2)}, u32[]{:S(2)}) async-start(bf16[8,8,1408]{2,1,0:T(8,128)(2,1)} %shard_map.106), calls=%async_computation.2 | async-start | bytes 360448 | tf_op jit(solution)/shard_map/all_to_all | solution.py:39
  52.3 2.5 %collective-permute-start.10 = (f32[1,1152]{1,0:T(1,128)S(1)}, f32[1,1152]{1,0:T(1,128)S(1)}, u32[]{:S(2)}, u32[]{:S(2)}) collective-permute-start(f32[1,1152]{1,0:T(1,128)S(1)} %get-tuple-element.47), channel_id=1, source_target_pairs={{0,1},{1,0},{2,3},{3,2},{4,5},{5,4},{6,7},{7,6},{8,9},{9,8},{10,11... | collective-permute-start | bytes 13832 | tf_op jit(solution)/shard_map/ppermute | solution.py:33
  52.3 7.5 %collective-permute-start.9 = (f32[1,1152]{1,0:T(1,128)S(1)}, f32[1,1152]{1,0:T(1,128)S(1)}, u32[]{:S(2)}, u32[]{:S(2)}) collective-permute-start(f32[1,1152]{1,0:T(1,128)S(1)} %get-tuple-element.47), channel_id=1, source_target_pairs={{1,2},{4,3},{3,4},{6,5},{5,6},{8,7},{7,8},{10,9},{9,10},{12,11},{1... | collective-permute-start | bytes 13832 | tf_op jit(solution)/shard_map/ppermute | solution.py:27

commit v11 on v10

--- a/solution.py
+++ b/solution.py
@@ -24,9 +24,7 @@
     count = lax.axis_size(DP)
     across = [(i, i - 1 if i % 2 == 0 else i + 1) for i in range(2, count - 3)]
     across += [(0, 2), (1, 0), (count - 3, count - 1), (count - 2, count - 3), (count - 1, count - 2)]
-    chip = lax.ppermute(value, DP, across if ahead else [(b, a) for a, b in across])
-    core = exchange(value, C, 1)
-    return chip, core
+    return lax.ppermute(value, DP, across if ahead else [(b, a) for a, b in across])
 
 
 def exchange(value, axis, bit):
@@ -84,8 +82,8 @@
     unit = image / norm
     unit_ref[...] = unit
     norm_ref[...] = norm
-    row_ref[:, :width] = unit.astype(BF16)
-    row_ref[:, width:] = id_tile(groups_ref, pairs, False)
+    row_ref[:pairs, :width] = unit.astype(BF16)
+    row_ref[:pairs, width:] = id_tile(groups_ref, pairs, False)
     tile_ref[...] = id_tile(groups_ref, pairs, True)
     moves[4].wait()
     gain_out[...] = gain_ref[...][None, :]
@@ -97,14 +95,22 @@
     sides_out[...] = jnp.where(lane == 0, 1 - odd, jnp.where(last == captions - 1, 0, odd))
     sums = jnp.dot(members(ids_ref[...], pairs, 1), tokens_ref[...], preferred_element_type=F32)
     pooled_ref[...] = sums[:pairs]
-    spill_ref[...] = sums[pairs : pairs + 1]
-
-
-def text_rows(tile_ref, sides_ref, pooled_ref, chip_ref, core_ref, gain_ref, rows_ref, unit_ref, norm_ref):
+    spill = sums[pairs : pairs + 1]
+    spill_ref[...] = spill
+    high = spill.astype(BF16).astype(F32)
+    row = lax.broadcasted_iota(jnp.int32, (pairs, width), 0)
+    cells = jnp.where(row == 0, high, jnp.where(row == 1, spill - high, 0.0))
+    row_ref[pairs:, :width] = cells.astype(BF16)
+    row_ref[pairs:, width:] = jnp.zeros((pairs, LANES), BF16)
+
+
+def text_rows(tile_ref, sides_ref, pooled_ref, chip_ref, other_ref, gain_ref, rows_ref, unit_ref, norm_ref):
     pairs, width = pooled_ref.shape
     last = lax.broadcasted_iota(jnp.int32, (pairs, 1), 0) == pairs - 1
     sides = sides_ref[...]
-    arrived = jnp.where(sides[:, :1] > 0, core_ref[...], jnp.where(sides[:, 1:2] > 0, chip_ref[...], 0.0))
+    parts = other_ref[pairs:, :width].astype(F32)
+    core = parts[:1] + parts[1:2]
+    arrived = jnp.where(sides[:, :1] > 0, core, jnp.where(sides[:, 1:2] > 0, chip_ref[...], 0.0))
     pooled = pooled_ref[...] + jnp.where(last, arrived, 0.0)
     embedded = pooled * gain_ref[...]
     norm = jnp.sqrt(jnp.sum(embedded * embedded, axis=1, keepdims=True))
@@ -117,7 +123,9 @@
         rows_ref[k, :, width:] = ids
 
 
-def pair_math(knobs_ref, near_ref, far_ref, text_ref, gain_ref, text_out, keep_out, send_out):
+def pair_math(
+    knobs_ref, near_ref, far_ref, text_ref, gain_ref, text_hbm, keep_out, send_out, part_ref, packed_ref, sems
+):
     width = gain_ref.shape[1]
     scale = jnp.exp(knobs_ref[:, :1])
     rows = jnp.concatenate([near_ref[...], far_ref[...]], axis=0)
@@ -134,12 +142,10 @@
     losses = jnp.maximum(margin, 0.0) + jnp.log1p(tail)
     sigmoid = jnp.where(margin >= 0.0, 1.0, tail) / (1.0 + tail)
     coeffs = jnp.where(match, -sigmoid, sigmoid)
-    image_part = scale * jnp.dot(coeffs.astype(BF16), text, preferred_element_type=F32)
     text_part = scale * jnp.dot(coeffs.T.astype(BF16), image, preferred_element_type=F32)
-    half = keep_out.shape[0]
-    keep_out[...] = image_part[:half]
-    send_out[...] = image_part[half:].astype(BF16)
-    text_out[:, :width] = text_part.astype(BF16)
+    part_ref[...] = text_part.astype(BF16)
+    move = pltpu.make_async_copy(part_ref, text_hbm.at[:, pl.ds(0, width)], sems.at[0])
+    move.start()
 
     unit = text.astype(F32)
     along = jnp.sum(unit * text_part, axis=1, keepdims=True)
@@ -156,8 +162,16 @@
         second = jnp.where((row == 1) & (lane == i), high, second)
         second = jnp.where((row == 2) & (lane == i), total - high, second)
     packed = jnp.concatenate([first, second], axis=1).astype(BF16)
-    for k in range(text_out.shape[0] // 8):
-        text_out[8 * k : 8 * (k + 1), width:] = packed
+    for k in range(packed_ref.shape[0] // 8):
+        packed_ref[8 * k : 8 * (k + 1)] = packed
+    rest = pltpu.make_async_copy(packed_ref, text_hbm.at[:, pl.ds(width, 2 * LANES)], sems.at[1])
+    rest.start()
+    image_part = scale * jnp.dot(coeffs.astype(BF16), text, preferred_element_type=F32)
+    for k in range(keep_out.shape[0] // 8):
+        keep_out[8 * k : 8 * (k + 1)] = image_part[16 * k : 16 * k + 8]
+        send_out[8 * k : 8 * (k + 1)] = image_part[16 * k + 8 : 16 * (k + 1)].astype(BF16)
+    move.wait()
+    rest.wait()
 
 
 def text_gradient(back_ref, unit_ref, norm_ref, gain_ref, grad_out, last_out, totals_out):
@@ -217,11 +231,11 @@
     image_out[...] = grad / norm_ref[...]
 
 
-def local(kernel, specs, *outs, scratch=()):
+def local(kernel, specs, *outs, scratch=(), to=None):
     return pl.pallas_call(
         kernel,
         in_specs=specs,
-        out_specs=[VMEM] * len(outs),
+        out_specs=to or [VMEM] * len(outs),
         out_shape=[jax.ShapeDtypeStruct(*o) for o in outs],
         scratch_shapes=scratch,
         compiler_params=pltpu.CompilerParams(vmem_limit_bytes=16 << 20),
@@ -237,7 +251,7 @@
     ids = caption_ids[None, :]
     row, unit_image, image_norm, pooled, spill, tile, gain, sides = local(
         functools.partial(prepare, captions=total_pairs), [HBM] * 5,
-        ((pairs, wide), BF16), ((pairs, width), F32), ((pairs, 1), F32), ((pairs, width), F32),
+        ((2 * pairs, wide), BF16), ((pairs, width), F32), ((pairs, 1), F32), ((pairs, width), F32),
         ((1, width), F32), ((pairs, LANES), BF16), ((1, width), F32), ((1, LANES), jnp.int32),
         scratch=(
             pltpu.SMEM((pairs,), jnp.int32), pltpu.VMEM((1, tokens), jnp.int32),
@@ -251,25 +265,32 @@
         )
     )
 
+    other = exchange(row, C, 1)
     arrived = beside(spill, True)
-    near = [row]
+    chip = jnp.concatenate([row[:pairs], other[:pairs]], axis=0)
+    near = [chip]
     for step in FROM[1:4]:
-        near.append(exchange(row, Z, step))
+        near.append(exchange(chip, Z, step))
     near = jnp.concatenate(near, axis=0)
-    near = jnp.concatenate([near, exchange(near, Z, 1)], axis=0)
+    far = exchange(near, Z, 1)
+    far, log_scale, logit_bias = lax.optimization_barrier((far, log_scale, logit_bias))
+    lane = lax.broadcasted_iota(jnp.int32, (1, LANES), 1)
+    knobs = jnp.where(lane == 0, log_scale[0], logit_bias[0])
+
     rows, unit_text, text_norm = local(
         text_rows, [VMEM] * 6,
         ((plane, pairs, wide), BF16), ((pairs, width), F32), ((pairs, 1), F32),
-    )(tile, sides, pooled, *arrived, gain)
+    )(tile, sides, pooled, arrived, other, gain)
     texts = to_all(rows, PLANE).reshape(plane * pairs, wide)
 
-    far = exchange(near, C, 1)
-    far, log_scale, logit_bias = lax.optimization_barrier((far, log_scale, logit_bias))
-    lane = lax.broadcasted_iota(jnp.int32, (1, LANES), 1)
-    knobs = jnp.where(lane == 0, log_scale[0], logit_bias[0])
     text_part, keep, send = local(
         pair_math, [VMEM] * 5,
         ((plane * pairs, wide + LANES), BF16), ((depth * pairs, width), F32), ((depth * pairs, width), BF16),
+        to=[HBM, VMEM, VMEM],
+        scratch=(
+            pltpu.VMEM((plane * pairs, width), BF16), pltpu.VMEM((plane * pairs, 2 * LANES), BF16),
+            pltpu.SemaphoreType.DMA((2,)),
+        ),
     )(knobs, near, far, texts, gain)
 
     back = to_all(text_part.reshape(plane, pairs, wide + LANES), PLANE)
@@ -283,8 +304,9 @@
         lax.axis_index(Z)[None], keep, came, totals, other
     )
     line_back = to_all(blocks, Z)
-    behind = beside(last, False)
-    (token_grad,) = local(token_rows, [VMEM] * 5, ((tokens, width), F32))(ids, sides, pooled_grad, *behind)
+    behind_chip = beside(last, False)
+    behind_core = exchange(last, C, 1)
+    (token_grad,) = local(token_rows, [VMEM] * 5, ((tokens, width), F32))(ids, sides, pooled_grad, behind_chip, behind_core)
     image_grad, gain_grad, scalars = local(
         functools.partial(finish, count=float(total_pairs * total_pairs)), [VMEM] * 3,
         ((pairs, width), F32), ((width,), F32), ((3,), F32),

time: 62.4 us -> 62.2 us (level)
  starting transfers between devices: 36.1 us -> 33.7 us
  waiting for transfers between devices: 16.9 us -> 19.1 us
    ppermute x2, starting transfers between devices: 10.6 us -> 8.11 us  [beside(): lax.ppermute(value, DP, across if ahead else [(b, a) for a, b in across])]
    ppermute x9 -> x8, starting transfers between devices: 6.78 us -> 4.94 us  [exchange(): lax.ppermute(value, axis, [(i, i ^ bit) for i in range(lax.axis_size(axis...]
    all_to_all x3, starting transfers between devices: 18.8 us -> 20.6 us  [to_all(): lax.all_to_all(blocks, axes, 0, 0, tiled=True, axis_index_groups=backward)]
    ppermute x9 -> x8, waiting for transfers between devices: 5.63 us -> 7.41 us  [exchange(): lax.ppermute(value, axis, [(i, i ^ bit) for i in range(lax.axis_size(axis...]
    ppermute x2, waiting for transfers between devices: 4.98 us -> 5.8 us  [beside(): lax.ppermute(value, DP, across if ahead else [(b, a) for a, b in across])]
  transfers between devices with their start and end apart: 14 -> 13, of which waited for: 5 -> 6; matrix products, arithmetic and copies ran while one was open for 0% -> 0% of each run, Pallas kernels for 4% -> 4%
where the time goes in v11:
time: 62.2 us; the launch traced here: 61.7 us
  starting transfers between devices  33.7 us (54%)
  waiting for transfers between devices  19.1 us (31%)
  Pallas kernels  6.81 us (11%)
  between operations  2.06 us (3%)
    all_to_all x3, starting transfers between devices, to_all(): lax.all_to_all(blocks, axes, 0, 0, tiled=True, axis_index_groups=backward)  20.6 us
    ppermute x2, starting transfers between devices, beside(): lax.ppermute(value, DP, across if ahead else [(b, a) for a, b in across])  8.11 us
    ppermute x8, waiting for transfers between devices, exchange(): lax.ppermute(value, axis, [(i, i ^ bit) for i in range(lax.axis_size(axis...  7.41 us
    all_to_all x3, waiting for transfers between devices, to_all(): lax.all_to_all(blocks, axes, 0, 0, tiled=True, axis_index_groups=backward)  5.93 us
    ppermute x2, waiting for transfers between devices, beside(): lax.ppermute(value, DP, across if ahead else [(b, a) for a, b in across])  5.8 us
    ppermute x8, starting transfers between devices, exchange(): lax.ppermute(value, axis, [(i, i ^ bit) for i in range(lax.axis_size(axis...  4.94 us
    pallas_call x1, Pallas kernels, per_device(): local(pair_math, [VMEM] * 5, ((plane * pairs, wide + LANES), BF16), ((dep...  1.47 us
    pallas_call x1, Pallas kernels, per_device(): local(token_rows, [VMEM] * 5, ((tokens, width), F32))  1.44 us
  transfers between devices with their start and end apart: 13, of which 6 were waited for; matrix products, arithmetic and copies ran while one was open for 0% of the time, Pallas kernels for 4%

profile of v11, /device:TPU:8, one launch (start us, length us, event | category | flops | bytes accessed | tf_op | source)
XLA Modules:
  0.0 61.7 jit_solution(12409545374608849902)
XLA Ops:
  0.6 1.4 %shard_map.102 = (bf16[16,1280]{1,0:T(8,128)(2,1)S(1)}, f32[8,1152]{1,0:T(8,128)S(1)}, f32[8,1]{1,0:T(8,128)S(1)}, f32[8,1152]{1,0:T(8,128)S(1)}, f32[1,1152]{1,...) custom-call(s32[8]{0:T(128)} %groups_hbm.1, s32[1,256]{1,0:T(1,128)} %bitcast.9, ...), custom_call_target="tpu_custom_call" | custom-call | tf_op jit(solution)/shard_map/pallas_call | solution.py:252
  2.0 0.1 collective-permute-start
  2.1 1.2 %collective-permute-done.other_ref = bf16[16,1280]{1,0:T(8,128)(2,1)S(1)} collective-permute-done((bf16[16,1280]{1,0:T(8,128)(2,1)S(1)}, bf16[16,1280]{1,0:T(8,128)(2,1)S(1)}, u32[]{:S(2)}, u32[]{:S(2)}) %collective-permute-start) | collective-permute-done | bytes 40992 | tf_op jit(solution)/shard_map/ppermute | solution.py:31
  3.3 3.4 %collective-permute-start.1 = (bf16[16,1280]{1,0:T(8,128)(2,1)S(1)}, bf16[16,1280]{1,0:T(8,128)(2,1)S(1)}, u32[]{:S(2)}, u32[]{:S(2)}) collective-permute-start(bf16[16,1280]{1,0:T(8,128)(2,1)S(1)} %pad_maximum_fusion), channel_id=1, source_target_pairs={{0,4},{2,6},{4,0},{6,2},{8,12},{10,14},{12,8},{14,10},{1,5},{3,7},... | collective-permute-start | bytes 122888 | tf_op jit(solution)/shard_map/ppermute | solution.py:31
  6.7 5.6 %collective-permute-start.5 = (f32[1,1152]{1,0:T(1,128)S(1)}, f32[1,1152]{1,0:T(1,128)S(1)}, u32[]{:S(2)}, u32[]{:S(2)}) collective-permute-start(f32[1,1152]{1,0:T(1,128)S(1)} %get-tuple-element.34), channel_id=1, source_target_pairs={{2,1},{3,4},{4,3},{5,6},{6,5},{7,8},{8,7},{9,10},{10,9},{11,12},{1... | collective-permute-start | bytes 13832 | tf_op jit(solution)/shard_map/ppermute | solution.py:27
  12.3 0.0 collective-permute-start.3
  12.3 0.8 %collective-permute-start.2 = (bf16[16,1280]{1,0:T(8,128)(2,1)S(1)}, bf16[16,1280]{1,0:T(8,128)(2,1)S(1)}, u32[]{:S(2)}, u32[]{:S(2)}) collective-permute-start(bf16[16,1280]{1,0:T(8,128)(2,1)S(1)} %pad_maximum_fusion), channel_id=1, source_target_pairs={{0,8},{2,10},{4,12},{6,14},{8,0},{10,2},{12,4},{14,6},{1,9},{3,11}... | collective-permute-start | bytes 122888 | tf_op jit(solution)/shard_map/ppermute | solution.py:31
  13.1 0.8 %collective-permute-done.5.chip_ref = f32[1,1152]{1,0:T(1,128)S(1)} collective-permute-done((f32[1,1152]{1,0:T(1,128)S(1)}, f32[1,1152]{1,0:T(1,128)S(1)}, u32[]{:S(2)}, u32[]{:S(2)}) %collective-permute-start.5) | collective-permute-done | bytes 4640 | tf_op jit(solution)/shard_map/ppermute | solution.py:27
  14.0 0.9 %shard_map.103 = (bf16[16,8,1280]{2,1,0:T(8,128)(2,1)}, f32[8,1152]{1,0:T(8,128)S(1)}, f32[8,1]{1,0:T(8,128)S(1)}) custom-call(bf16[8,128]{1,0:T(8,128)(2,1)S(1)} %get-tuple-element.31.tile_ref, s32[1,128]{1,0:T(1,128)S(1)} %get-tuple-element.32.sides_ref, f32[8,1152]{1,0:T(8,128)S(1)} %get-tuple-element.33.pooled_ref, ...), custom_call_target="tpu_custom_call" | custom-call | tf_op jit(solution)/shard_map/pallas_call | solution.py:280
  14.9 7.1 %all-to-all-start = ((bf16[16,8,1280]{2,1,0:T(8,128)(2,1)}), bf16[16,8,1280]{2,1,0:T(8,128)(2,1)S(1)}, u32[]{:S(2)}, u32[]{:S(2)}) async-start(bf16[16,8,1280]{2,1,0:T(8,128)(2,1)} %get-tuple-element.36), calls=%async_computation | async-start | bytes 655360 | tf_op jit(solution)/shard_map/all_to_all | solution.py:37
  22.0 0.0 collective-permute-done.1
  22.0 0.0 collective-permute-done.2
  22.0 0.0 collective-permute-done.3
  22.0 0.6 collective-permute-start.4
  23.9 5.1 %collective-permute-done.4.far_ref = bf16[64,1280]{1,0:T(8,128)(2,1)S(1)} collective-permute-done((bf16[64,1280]{1,0:T(8,128)(2,1)S(1)}, bf16[64,1280]{1,0:T(8,128)(2,1)S(1)}, u32[]{:S(2)}, u32[]{:S(2)}) %collective-permute-start.4) | collective-permute-done | bytes 163872 | tf_op jit(solution)/shard_map/ppermute | solution.py:31
  29.0 0.0 all-to-all-done
  29.0 1.5 %shard_map.104 = (bf16[128,1408]{1,0:T(8,128)(2,1)}, f32[64,1152]{1,0:T(8,128)S(1)}, bf16[64,1152]{1,0:T(8,128)(2,1)S(1)}) custom-call(f32[1,128]{1,0:T(1,128)S(1)} %compare_select_fusion.knobs_ref, bf16[64,1280]{1,0:T(8,128)(2,1)S(1)} %constant_dynamic-update-slice_fusion.near_ref, bf16[64,1280]{1,0:T(8,128)(2,1)S(1)} %collective-permute-done.4.far_ref, ...), custom_call_target="tpu_custom_call" | custom-call | tf_op jit(solution)/shard_map/pallas_call | solution.py:286
  30.4 0.0 copy-start
  30.5 7.2 %all-to-all-start.1 = ((bf16[16,8,1408]{2,1,0:T(8,128)(2,1)}), bf16[16,8,1408]{2,1,0:T(8,128)(2,1)S(1)}, u32[]{:S(2)}, u32[]{:S(2)}) async-start(bf16[16,8,1408]{2,1,0:T(8,128)(2,1)} %bitcast.5), calls=%async_computation.1 | async-start | bytes 720896 | tf_op jit(solution)/shard_map/all_to_all | solution.py:37
  37.7 0.0 collective-permute-start.6
  37.7 5.9 %all-to-all-done.1.back_ref = bf16[16,8,1408]{2,1,0:T(8,128)(2,1)S(1)} async-done(((bf16[16,8,1408]{2,1,0:T(8,128)(2,1)}), bf16[16,8,1408]{2,1,0:T(8,128)(2,1)S(1)}, u32[]{:S(2)}, u32[]{:S(2)}) %all-to-all-start.1) | async-done | bytes 360480 | tf_op jit(solution)/shard_map/all_to_all | solution.py:37
  43.6 0.1 shard_map.105
  43.8 0.1 collective-permute-start.7
  43.9 1.1 %collective-permute-done.7.other_ref = f32[8,256]{1,0:T(8,128)S(1)} collective-permute-done((f32[8,256]{1,0:T(8,128)S(1)}, f32[8,256]{1,0:T(8,128)S(1)}, u32[]{:S(2)}, u32[]{:S(2)}) %collective-permute-start.7) | collective-permute-done | bytes 8224 | tf_op jit(solution)/shard_map/ppermute | solution.py:31
  45.0 0.7 %shard_map.106 = bf16[8,8,1408]{2,1,0:T(8,128)(2,1)} custom-call(s32[1]{0:T(128)} %bitcast.place_ref, f32[64,1152]{1,0:T(8,128)S(1)} %get-tuple-element.37.keep_ref, bf16[64,1152]{1,0:T(8,128)(2,1)S(1)} %collective-permute-done.6.came_ref, f32[8,256]{1,0:T(8,128)S(1)} %get-tuple-element.42.totals_ref, f32[8,256]{1,0:T(8,128)S(1)} %collective-permute-done.7.other_ref), custom_call_target="tpu_custom_call" | custom-call | tf_op jit(solution)/shard_map/pallas_call | solution.py:303
  45.7 6.3 %all-to-all-start.2 = ((bf16[8,8,1408]{2,1,0:T(8,128)(2,1)}), bf16[8,8,1408]{2,1,0:T(8,128)(2,1)S(1)}, u32[]{:S(2)}, u32[]{:S(2)}) async-start(bf16[8,8,1408]{2,1,0:T(8,128)(2,1)} %shard_map.106), calls=%async_computation.2 | async-start | bytes 360448 | tf_op jit(solution)/shard_map/all_to_all | solution.py:37
  52.1 2.5 %collective-permute-start.8 = (f32[1,1152]{1,0:T(1,128)S(1)}, f32[1,1152]{1,0:T(1,128)S(1)}, u32[]{:S(2)}, u32[]{:S(2)}) collective-permute-start(f32[1,1152]{1,0:T(1,128)S(1)} %get-tuple-element.47), channel_id=1, source_target_pairs={{1,2},{4,3},{3,4},{6,5},{5,6},{8,7},{7,8},{10,9},{9,10},{12,11},{1... | collective-permute-start | bytes 13832 | tf_op jit(solution)/shard_map/ppermute | solution.py:27
  54.6 0.0 collective-permute-done.9.core_ref
  54.6 5.0 %collective-permute-done.8.chip_ref = f32[1,1152]{1,0:T(1,128)S(1)} collective-permute-done((f32[1,1152]{1,0:T(1,128)S(1)}, f32[1,1152]{1,0:T(1,128)S(1)}, u32[]{:S(2)}, u32[]{:S(2)}) %collective-permute-start.8) | collective-permute-done | bytes 4640 | tf_op jit(solution)/shard_map/ppermute | solution.py:27
  59.6 1.4 %shard_map.108 = f32[256,1152]{1,0:T(8,128)} custom-call(s32[1,256]{1,0:T(1,128)S(1)} %bitcast.10, s32[1,128]{1,0:T(1,128)S(1)} %get-tuple-element.32.sides_ref, f32[8,1152]{1,0:T(8,128)S(1)} %get-tuple-element.46.grad_ref, f32[1,1152]{1,0:T(1,128)S(1)} %collective-permute-done.8.chip_ref, f32[1,1152]{1,0:T(1,128)S(1)} %collective-permute-done.9.core_ref), custom_call_target="tpu_custom_call" | custom-call | tf_op jit(solution)/shard_map/pallas_call | solution.py:309
  61.0 0.0 all-to-all-done.2.back_ref
  61.0 0.7 %shard_map.107 = (f32[8,1152]{1,0:T(8,128)}, f32[1152]{0:T(1024)}, f32[3]{0:T(128)}) custom-call(bf16[8,8,1408]{2,1,0:T(8,128)(2,1)S(1)} %all-to-all-done.2.back_ref, f32[8,1152]{1,0:T(8,128)S(1)} %get-tuple-element.43.unit_ref, f32[8,1]{1,0:T(8,128)S(1)} %get-tuple-element.44.norm_ref), custom_call_target="tpu_custom_call" | custom-call | tf_op jit(solution)/shard_map/pallas_call | solution.py:310
  (10 shorter events, 0.0 us)
Async XLA Ops:
  2.0 1.3 %collective-permute-start = (bf16[16,1280]{1,0:T(8,128)(2,1)S(1)}, bf16[16,1280]{1,0:T(8,128)(2,1)S(1)}, u32[]{:S(2)}, u32[]{:S(2)}) collective-permute-start(bf16[16,1280]{1,0:T(8,128)(2,1)S(1)} %get-tuple-element.27), channel_id=1, source_target_pairs={{0,1},{1,0},{2,3},{3,2},{4,5},{5,4},{6,7},{7,6},{8,9},{9,8},{10,11... | collective-permute-start | bytes 122888 | tf_op jit(solution)/shard_map/ppermute | solution.py:31
  3.3 18.6 %collective-permute-start.1 = (bf16[16,1280]{1,0:T(8,128)(2,1)S(1)}, bf16[16,1280]{1,0:T(8,128)(2,1)S(1)}, u32[]{:S(2)}, u32[]{:S(2)}) collective-permute-start(bf16[16,1280]{1,0:T(8,128)(2,1)S(1)} %pad_maximum_fusion), channel_id=1, source_target_pairs={{0,4},{2,6},{4,0},{6,2},{8,12},{10,14},{12,8},{14,10},{1,5},{3,7},... | collective-permute-start | bytes 122888 | tf_op jit(solution)/shard_map/ppermute | solution.py:31
  6.7 7.3 %collective-permute-start.5 = (f32[1,1152]{1,0:T(1,128)S(1)}, f32[1,1152]{1,0:T(1,128)S(1)}, u32[]{:S(2)}, u32[]{:S(2)}) collective-permute-start(f32[1,1152]{1,0:T(1,128)S(1)} %get-tuple-element.34), channel_id=1, source_target_pairs={{2,1},{3,4},{4,3},{5,6},{6,5},{7,8},{8,7},{9,10},{10,9},{11,12},{1... | collective-permute-start | bytes 13832 | tf_op jit(solution)/shard_map/ppermute | solution.py:27
  12.3 9.7 %collective-permute-start.3 = (bf16[16,1280]{1,0:T(8,128)(2,1)S(1)}, bf16[16,1280]{1,0:T(8,128)(2,1)S(1)}, u32[]{:S(2)}, u32[]{:S(2)}) collective-permute-start(bf16[16,1280]{1,0:T(8,128)(2,1)S(1)} %pad_maximum_fusion), channel_id=1, source_target_pairs={{0,12},{2,14},{4,8},{6,10},{8,4},{10,6},{12,0},{14,2},{1,13},{3,15... | collective-permute-start | bytes 122888 | tf_op jit(solution)/shard_map/ppermute | solution.py:31
  12.3 9.7 %collective-permute-start.2 = (bf16[16,1280]{1,0:T(8,128)(2,1)S(1)}, bf16[16,1280]{1,0:T(8,128)(2,1)S(1)}, u32[]{:S(2)}, u32[]{:S(2)}) collective-permute-start(bf16[16,1280]{1,0:T(8,128)(2,1)S(1)} %pad_maximum_fusion), channel_id=1, source_target_pairs={{0,8},{2,10},{4,12},{6,14},{8,0},{10,2},{12,4},{14,6},{1,9},{3,11}... | collective-permute-start | bytes 122888 | tf_op jit(solution)/shard_map/ppermute | solution.py:31
  14.9 14.1 %all-to-all-start = ((bf16[16,8,1280]{2,1,0:T(8,128)(2,1)}), bf16[16,8,1280]{2,1,0:T(8,128)(2,1)S(1)}, u32[]{:S(2)}, u32[]{:S(2)}) async-start(bf16[16,8,1280]{2,1,0:T(8,128)(2,1)} %get-tuple-element.36), calls=%async_computation | async-start | bytes 655360 | tf_op jit(solution)/shard_map/all_to_all | solution.py:37
  22.0 6.9 %collective-permute-start.4 = (bf16[64,1280]{1,0:T(8,128)(2,1)S(1)}, bf16[64,1280]{1,0:T(8,128)(2,1)S(1)}, u32[]{:S(2)}, u32[]{:S(2)}) collective-permute-start(bf16[64,1280]{1,0:T(8,128)(2,1)S(1)} %constant_dynamic-update-slice_fusion.near_ref), channel_id=1, source_target_pairs={{0,2},{2,0},{4,6},{6,4},{8,10},{10,8},{12,14},{14,12},{1,3},{3,1},... | collective-permute-start | bytes 491528 | tf_op jit(solution)/shard_map/ppermute | solution.py:31
  30.4 29.1 %copy-start = (s32[256]{0:T(256)S(1)}, s32[256]{0:T(256)}, u32[]{:S(2)}) copy-start(s32[256]{0:T(256)} %param.9) | copy-start | bytes 3076
  30.5 13.2 %all-to-all-start.1 = ((bf16[16,8,1408]{2,1,0:T(8,128)(2,1)}), bf16[16,8,1408]{2,1,0:T(8,128)(2,1)S(1)}, u32[]{:S(2)}, u32[]{:S(2)}) async-start(bf16[16,8,1408]{2,1,0:T(8,128)(2,1)} %bitcast.5), calls=%async_computation.1 | async-start | bytes 720896 | tf_op jit(solution)/shard_map/all_to_all | solution.py:37
  37.7 6.2 %collective-permute-start.6 = (bf16[64,1152]{1,0:T(8,128)(2,1)S(1)}, bf16[64,1152]{1,0:T(8,128)(2,1)S(1)}, u32[]{:S(2)}, u32[]{:S(2)}) collective-permute-start(bf16[64,1152]{1,0:T(8,128)(2,1)S(1)} %get-tuple-element.38), channel_id=1, source_target_pairs={{0,1},{1,0},{2,3},{3,2},{4,5},{5,4},{6,7},{7,6},{8,9},{9,8},{10,11... | collective-permute-start | bytes 442376 | tf_op jit(solution)/shard_map/ppermute | solution.py:31
  43.8 1.3 %collective-permute-start.7 = (f32[8,256]{1,0:T(8,128)S(1)}, f32[8,256]{1,0:T(8,128)S(1)}, u32[]{:S(2)}, u32[]{:S(2)}) collective-permute-start(f32[8,256]{1,0:T(8,128)S(1)} %get-tuple-element.42.totals_ref), channel_id=1, source_target_pairs={{0,1},{1,0},{2,3},{3,2},{4,5},{5,4},{6,7},{7,6},{8,9},{9,8},{10,11... | collective-permute-start | bytes 24584 | tf_op jit(solution)/shard_map/ppermute | solution.py:31
  45.7 15.3 %all-to-all-start.2 = ((bf16[8,8,1408]{2,1,0:T(8,128)(2,1)}), bf16[8,8,1408]{2,1,0:T(8,128)(2,1)S(1)}, u32[]{:S(2)}, u32[]{:S(2)}) async-start(bf16[8,8,1408]{2,1,0:T(8,128)(2,1)} %shard_map.106), calls=%async_computation.2 | async-start | bytes 360448 | tf_op jit(solution)/shard_map/all_to_all | solution.py:37
  52.1 2.5 %collective-permute-start.9 = (f32[1,1152]{1,0:T(1,128)S(1)}, f32[1,1152]{1,0:T(1,128)S(1)}, u32[]{:S(2)}, u32[]{:S(2)}) collective-permute-start(f32[1,1152]{1,0:T(1,128)S(1)} %get-tuple-element.47), channel_id=1, source_target_pairs={{0,1},{1,0},{2,3},{3,2},{4,5},{5,4},{6,7},{7,6},{8,9},{9,8},{10,11... | collective-permute-start | bytes 13832 | tf_op jit(solution)/shard_map/ppermute | solution.py:31
  52.1 7.5 %collective-permute-start.8 = (f32[1,1152]{1,0:T(1,128)S(1)}, f32[1,1152]{1,0:T(1,128)S(1)}, u32[]{:S(2)}, u32[]{:S(2)}) collective-permute-start(f32[1,1152]{1,0:T(1,128)S(1)} %get-tuple-element.47), channel_id=1, source_target_pairs={{1,2},{4,3},{3,4},{6,5},{5,6},{8,7},{7,8},{10,9},{9,10},{12,11},{1... | collective-permute-start | bytes 13832 | tf_op jit(solution)/shard_map/ppermute | solution.py:27

commit v12 on v11

--- a/solution.py
+++ b/solution.py
@@ -168,8 +168,10 @@
     rest.start()
     image_part = scale * jnp.dot(coeffs.astype(BF16), text, preferred_element_type=F32)
     for k in range(keep_out.shape[0] // 8):
-        keep_out[8 * k : 8 * (k + 1)] = image_part[16 * k : 16 * k + 8]
-        send_out[8 * k : 8 * (k + 1)] = image_part[16 * k + 8 : 16 * (k + 1)].astype(BF16)
+        own = 16 * k + (8 if k % 4 == 3 else 0)
+        far = 32 * k + 8 - own
+        keep_out[8 * k : 8 * (k + 1)] = image_part[own : own + 8]
+        send_out[8 * k : 8 * (k + 1)] = image_part[far : far + 8].astype(BF16)
     move.wait()
     rest.wait()
 
@@ -197,9 +199,11 @@
         rest, cells = rest - part, jnp.where(row == r, part, cells)
     packed = jnp.concatenate([total[:, :LANES], cells], axis=1).astype(BF16)
     for k in range(places):
-        rows = slice(pairs * k, pairs * (k + 1))
-        block = keep_ref[rows] + came_ref[rows].astype(F32)
-        place = places - 1 - (place_ref[0] ^ FROM[k])
+        there = k ^ 2 if k % 2 else k
+        block = keep_ref[pairs * k : pairs * (k + 1)]
+        block = block + came_ref[pairs * there : pairs * (there + 1)].astype(F32)
+        turn = (1 - place_ref[0] % 2) * 4 if k % 2 else 0
+        place = places - 1 - ((place_ref[0] // 2) ^ FROM[k] ^ turn)
         out_ref[place, :, :width] = block.astype(BF16)
         out_ref[place, :, width:] = packed
 
@@ -268,10 +272,11 @@
     other = exchange(row, C, 1)
     arrived = beside(spill, True)
     chip = jnp.concatenate([row[:pairs], other[:pairs]], axis=0)
-    near = [chip]
-    for step in FROM[1:4]:
-        near.append(exchange(chip, Z, step))
-    near = jnp.concatenate(near, axis=0)
+    line = lax.axis_size((Z, C))
+    first = lax.ppermute(chip, (Z, C), [(i, i ^ (4 if i % 2 else 12)) for i in range(line)])
+    second = exchange(chip, Z, 4)
+    third = exchange(first, C, 1)
+    near = jnp.concatenate([chip, first, second, third], axis=0)
     far = exchange(near, Z, 1)
     far, log_scale, logit_bias = lax.optimization_barrier((far, log_scale, logit_bias))
     lane = lax.broadcasted_iota(jnp.int32, (1, LANES), 1)
@@ -301,7 +306,7 @@
     )(back, unit_text, text_norm, gain)
     other = exchange(totals, C, 1)
     (blocks,) = local(pack, [SMEM] + [VMEM] * 4, ((depth, pairs, width + 2 * LANES), BF16))(
-        lax.axis_index(Z)[None], keep, came, totals, other
+        lax.axis_index((Z, C))[None], keep, came, totals, other
     )
     line_back = to_all(blocks, Z)
     behind_chip = beside(last, False)

time: 62.2 us -> 63.1 us (1.014)
  waiting for transfers between devices: 19.1 us -> 23.5 us
  starting transfers between devices: 33.7 us -> 30.2 us
    ppermute x0 -> x1, starting transfers between devices: none -> 6.39 us  [per_device(): lax.ppermute(chip, (Z, C), [(i, i ^ (4 if i % 2 else 12)) for i in range(...]
    ppermute x8 -> x7, starting transfers between devices: 4.94 us -> 0.29 us  [exchange(): lax.ppermute(value, axis, [(i, i ^ bit) for i in range(lax.axis_size(axis...]
    ppermute x2, waiting for transfers between devices: 5.8 us -> 9.7 us  [beside(): lax.ppermute(value, DP, across if ahead else [(b, a) for a, b in across])]
    ppermute x2, starting transfers between devices: 8.11 us -> 4.89 us  [beside(): lax.ppermute(value, DP, across if ahead else [(b, a) for a, b in across])]
    all_to_all x3, starting transfers between devices: 20.6 us -> 18.7 us  [to_all(): lax.all_to_all(blocks, axes, 0, 0, tiled=True, axis_index_groups=backward)]
    ppermute x8 -> x7, waiting for transfers between devices: 7.41 us -> 8.46 us  [exchange(): lax.ppermute(value, axis, [(i, i ^ bit) for i in range(lax.axis_size(axis...]
  transfers between devices with their start and end apart: 13 -> 13, of which waited for: 6 -> 7; matrix products, arithmetic and copies ran while one was open for 0% -> 0% of each run, Pallas kernels for 4% -> 4%
where the time goes in v12:
time: 63.1 us; the launch traced here: 62.7 us
  starting transfers between devices  30.2 us (48%)
  waiting for transfers between devices  23.5 us (37%)
  Pallas kernels  6.82 us (11%)
  between operations  2.06 us (3%)
    all_to_all x3, starting transfers between devices, to_all(): lax.all_to_all(blocks, axes, 0, 0, tiled=True, axis_index_groups=backward)  18.7 us
    ppermute x2, waiting for transfers between devices, beside(): lax.ppermute(value, DP, across if ahead else [(b, a) for a, b in across])  9.7 us
    ppermute x7, waiting for transfers between devices, exchange(): lax.ppermute(value, axis, [(i, i ^ bit) for i in range(lax.axis_size(axis...  8.46 us
    ppermute x1, starting transfers between devices, per_device(): lax.ppermute(chip, (Z, C), [(i, i ^ (4 if i % 2 else 12)) for i in range(...  6.39 us
    all_to_all x3, waiting for transfers between devices, to_all(): lax.all_to_all(blocks, axes, 0, 0, tiled=True, axis_index_groups=backward)  5.32 us
    ppermute x2, starting transfers between devices, beside(): lax.ppermute(value, DP, across if ahead else [(b, a) for a, b in across])  4.89 us
    pallas_call x1, Pallas kernels, per_device(): local(pair_math, [VMEM] * 5, ((plane * pairs, wide + LANES), BF16), ((dep...  1.48 us
    pallas_call x1, Pallas kernels, per_device(): local(token_rows, [VMEM] * 5, ((tokens, width), F32))  1.44 us
  transfers between devices with their start and end apart: 13, of which 7 were waited for; matrix products, arithmetic and copies ran while one was open for 0% of the time, Pallas kernels for 4%

profile of v12, /device:TPU:8, one launch (start us, length us, event | category | flops | bytes accessed | tf_op | source)
XLA Modules:
  0.0 62.7 jit_solution(17063379616360987508)
XLA Ops:
  0.6 1.4 %shard_map.102 = (bf16[16,1280]{1,0:T(8,128)(2,1)S(1)}, f32[8,1152]{1,0:T(8,128)S(1)}, f32[8,1]{1,0:T(8,128)S(1)}, f32[8,1152]{1,0:T(8,128)S(1)}, f32[1,1152]{1,...) custom-call(s32[8]{0:T(128)} %groups_hbm.1, s32[1,256]{1,0:T(1,128)} %bitcast.9, ...), custom_call_target="tpu_custom_call" | custom-call | tf_op jit(solution)/shard_map/pallas_call | solution.py:256
  2.0 0.1 collective-permute-start
  2.1 1.2 %collective-permute-done.other_ref = bf16[16,1280]{1,0:T(8,128)(2,1)S(1)} collective-permute-done((bf16[16,1280]{1,0:T(8,128)(2,1)S(1)}, bf16[16,1280]{1,0:T(8,128)(2,1)S(1)}, u32[]{:S(2)}, u32[]{:S(2)}) %collective-permute-start) | collective-permute-done | bytes 40992 | tf_op jit(solution)/shard_map/ppermute | solution.py:31
  3.3 6.4 %collective-permute-start.1 = (bf16[16,1280]{1,0:T(8,128)(2,1)S(1)}, bf16[16,1280]{1,0:T(8,128)(2,1)S(1)}, u32[]{:S(2)}, u32[]{:S(2)}) collective-permute-start(bf16[16,1280]{1,0:T(8,128)(2,1)S(1)} %pad_maximum_fusion), channel_id=1, source_target_pairs={{0,12},{1,5},{2,14},{3,7},{4,8},{5,1},{6,10},{7,3},{8,4},{9,13},{1... | collective-permute-start | bytes 122888 | tf_op jit(solution)/shard_map/ppermute | solution.py:276
  9.7 2.6 %collective-permute-start.5 = (f32[1,1152]{1,0:T(1,128)S(1)}, f32[1,1152]{1,0:T(1,128)S(1)}, u32[]{:S(2)}, u32[]{:S(2)}) collective-permute-start(f32[1,1152]{1,0:T(1,128)S(1)} %get-tuple-element.34), channel_id=1, source_target_pairs={{2,1},{3,4},{4,3},{5,6},{6,5},{7,8},{8,7},{9,10},{10,9},{11,12},{1... | collective-permute-start | bytes 13832 | tf_op jit(solution)/shard_map/ppermute | solution.py:27
  12.3 0.0 collective-permute-start.2
  12.3 4.7 %collective-permute-done.5.chip_ref = f32[1,1152]{1,0:T(1,128)S(1)} collective-permute-done((f32[1,1152]{1,0:T(1,128)S(1)}, f32[1,1152]{1,0:T(1,128)S(1)}, u32[]{:S(2)}, u32[]{:S(2)}) %collective-permute-start.5) | collective-permute-done | bytes 4640 | tf_op jit(solution)/shard_map/ppermute | solution.py:27
  17.0 0.9 %shard_map.103 = (bf16[16,8,1280]{2,1,0:T(8,128)(2,1)}, f32[8,1152]{1,0:T(8,128)S(1)}, f32[8,1]{1,0:T(8,128)S(1)}) custom-call(bf16[8,128]{1,0:T(8,128)(2,1)S(1)} %get-tuple-element.31.tile_ref, s32[1,128]{1,0:T(1,128)S(1)} %get-tuple-element.32.sides_ref, f32[8,1152]{1,0:T(8,128)S(1)} %get-tuple-element.33.pooled_ref, ...), custom_call_target="tpu_custom_call" | custom-call | tf_op jit(solution)/shard_map/pallas_call | solution.py:285
  17.9 6.9 %all-to-all-start = ((bf16[16,8,1280]{2,1,0:T(8,128)(2,1)}), bf16[16,8,1280]{2,1,0:T(8,128)(2,1)S(1)}, u32[]{:S(2)}, u32[]{:S(2)}) async-start(bf16[16,8,1280]{2,1,0:T(8,128)(2,1)} %get-tuple-element.36), calls=%async_computation | async-start | bytes 655360 | tf_op jit(solution)/shard_map/all_to_all | solution.py:37
  24.9 0.0 collective-permute-done.1
  24.9 0.1 collective-permute-start.3
  25.0 1.2 %collective-permute-done.3 = bf16[16,1280]{1,0:T(8,128)(2,1)S(1)} collective-permute-done((bf16[16,1280]{1,0:T(8,128)(2,1)S(1)}, bf16[16,1280]{1,0:T(8,128)(2,1)S(1)}, u32[]{:S(2)}, u32[]{:S(2)}) %collective-permute-start.3) | collective-permute-done | bytes 40992 | tf_op jit(solution)/shard_map/ppermute | solution.py:31
  26.2 0.0 collective-permute-start.4
  27.5 5.0 %collective-permute-done.4.far_ref = bf16[64,1280]{1,0:T(8,128)(2,1)S(1)} collective-permute-done((bf16[64,1280]{1,0:T(8,128)(2,1)S(1)}, bf16[64,1280]{1,0:T(8,128)(2,1)S(1)}, u32[]{:S(2)}, u32[]{:S(2)}) %collective-permute-start.4) | collective-permute-done | bytes 163872 | tf_op jit(solution)/shard_map/ppermute | solution.py:31
  32.4 0.0 all-to-all-done
  32.4 1.5 %shard_map.104 = (bf16[128,1408]{1,0:T(8,128)(2,1)}, f32[64,1152]{1,0:T(8,128)S(1)}, bf16[64,1152]{1,0:T(8,128)(2,1)S(1)}) custom-call(f32[1,128]{1,0:T(1,128)S(1)} %compare_select_fusion.knobs_ref, bf16[64,1280]{1,0:T(8,128)(2,1)S(1)} %constant_dynamic-update-slice_fusion.near_ref, bf16[64,1280]{1,0:T(8,128)(2,1)S(1)} %collective-permute-done.4.far_ref, ...), custom_call_target="tpu_custom_call" | custom-call | tf_op jit(solution)/shard_map/pallas_call | solution.py:291
  33.9 0.0 copy-start
  33.9 7.2 %all-to-all-start.1 = ((bf16[16,8,1408]{2,1,0:T(8,128)(2,1)}), bf16[16,8,1408]{2,1,0:T(8,128)(2,1)S(1)}, u32[]{:S(2)}, u32[]{:S(2)}) async-start(bf16[16,8,1408]{2,1,0:T(8,128)(2,1)} %bitcast.5), calls=%async_computation.1 | async-start | bytes 720896 | tf_op jit(solution)/shard_map/all_to_all | solution.py:37
  41.2 0.0 collective-permute-start.6
  41.2 5.3 %all-to-all-done.1.back_ref = bf16[16,8,1408]{2,1,0:T(8,128)(2,1)S(1)} async-done(((bf16[16,8,1408]{2,1,0:T(8,128)(2,1)}), bf16[16,8,1408]{2,1,0:T(8,128)(2,1)S(1)}, u32[]{:S(2)}, u32[]{:S(2)}) %all-to-all-start.1) | async-done | bytes 360480 | tf_op jit(solution)/shard_map/all_to_all | solution.py:37
  46.5 0.1 shard_map.105
  46.7 0.1 collective-permute-start.7
  46.8 0.0 collective-permute-done.6.came_ref
  46.8 1.1 %collective-permute-done.7.other_ref = f32[8,256]{1,0:T(8,128)S(1)} collective-permute-done((f32[8,256]{1,0:T(8,128)S(1)}, f32[8,256]{1,0:T(8,128)S(1)}, u32[]{:S(2)}, u32[]{:S(2)}) %collective-permute-start.7) | collective-permute-done | bytes 8224 | tf_op jit(solution)/shard_map/ppermute | solution.py:31
  47.9 0.7 %shard_map.106 = bf16[8,8,1408]{2,1,0:T(8,128)(2,1)} custom-call(s32[1]{0:T(128)} %bitcast.place_ref, f32[64,1152]{1,0:T(8,128)S(1)} %get-tuple-element.37.keep_ref, bf16[64,1152]{1,0:T(8,128)(2,1)S(1)} %collective-permute-done.6.came_ref, f32[8,256]{1,0:T(8,128)S(1)} %get-tuple-element.42.totals_ref, f32[8,256]{1,0:T(8,128)S(1)} %collective-permute-done.7.other_ref), custom_call_target="tpu_custom_call" | custom-call | tf_op jit(solution)/shard_map/pallas_call | solution.py:308
  48.6 4.5 %all-to-all-start.2 = ((bf16[8,8,1408]{2,1,0:T(8,128)(2,1)}), bf16[8,8,1408]{2,1,0:T(8,128)(2,1)S(1)}, u32[]{:S(2)}, u32[]{:S(2)}) async-start(bf16[8,8,1408]{2,1,0:T(8,128)(2,1)} %shard_map.106), calls=%async_computation.2 | async-start | bytes 360448 | tf_op jit(solution)/shard_map/all_to_all | solution.py:37
  53.1 0.0 collective-permute-start.9
  53.1 2.3 %collective-permute-start.8 = (f32[1,1152]{1,0:T(1,128)S(1)}, f32[1,1152]{1,0:T(1,128)S(1)}, u32[]{:S(2)}, u32[]{:S(2)}) collective-permute-start(f32[1,1152]{1,0:T(1,128)S(1)} %get-tuple-element.47), channel_id=1, source_target_pairs={{1,2},{4,3},{3,4},{6,5},{5,6},{8,7},{7,8},{10,9},{9,10},{12,11},{1... | collective-permute-start | bytes 13832 | tf_op jit(solution)/shard_map/ppermute | solution.py:27
  55.5 0.0 collective-permute-done.9.core_ref
  55.5 5.0 %collective-permute-done.8.chip_ref = f32[1,1152]{1,0:T(1,128)S(1)} collective-permute-done((f32[1,1152]{1,0:T(1,128)S(1)}, f32[1,1152]{1,0:T(1,128)S(1)}, u32[]{:S(2)}, u32[]{:S(2)}) %collective-permute-start.8) | collective-permute-done | bytes 4640 | tf_op jit(solution)/shard_map/ppermute | solution.py:27
  60.5 1.4 %shard_map.108 = f32[256,1152]{1,0:T(8,128)} custom-call(s32[1,256]{1,0:T(1,128)S(1)} %bitcast.10, s32[1,128]{1,0:T(1,128)S(1)} %get-tuple-element.32.sides_ref, f32[8,1152]{1,0:T(8,128)S(1)} %get-tuple-element.46.grad_ref, f32[1,1152]{1,0:T(1,128)S(1)} %collective-permute-done.8.chip_ref, f32[1,1152]{1,0:T(1,128)S(1)} %collective-permute-done.9.core_ref), custom_call_target="tpu_custom_call" | custom-call | tf_op jit(solution)/shard_map/pallas_call | solution.py:314
  61.9 0.7 %shard_map.107 = (f32[8,1152]{1,0:T(8,128)}, f32[1152]{0:T(1024)}, f32[3]{0:T(128)}) custom-call(bf16[8,8,1408]{2,1,0:T(8,128)(2,1)S(1)} %all-to-all-done.2.back_ref, f32[8,1152]{1,0:T(8,128)S(1)} %get-tuple-element.43.unit_ref, f32[8,1]{1,0:T(8,128)S(1)} %get-tuple-element.44.norm_ref), custom_call_target="tpu_custom_call" | custom-call | tf_op jit(solution)/shard_map/pallas_call | solution.py:315
  (10 shorter events, 0.0 us)
Async XLA Ops:
  2.0 1.3 %collective-permute-start = (bf16[16,1280]{1,0:T(8,128)(2,1)S(1)}, bf16[16,1280]{1,0:T(8,128)(2,1)S(1)}, u32[]{:S(2)}, u32[]{:S(2)}) collective-permute-start(bf16[16,1280]{1,0:T(8,128)(2,1)S(1)} %get-tuple-element.27), channel_id=1, source_target_pairs={{0,1},{1,0},{2,3},{3,2},{4,5},{5,4},{6,7},{7,6},{8,9},{9,8},{10,11... | collective-permute-start | bytes 122888 | tf_op jit(solution)/shard_map/ppermute | solution.py:31
  3.3 21.5 %collective-permute-start.1 = (bf16[16,1280]{1,0:T(8,128)(2,1)S(1)}, bf16[16,1280]{1,0:T(8,128)(2,1)S(1)}, u32[]{:S(2)}, u32[]{:S(2)}) collective-permute-start(bf16[16,1280]{1,0:T(8,128)(2,1)S(1)} %pad_maximum_fusion), channel_id=1, source_target_pairs={{0,12},{1,5},{2,14},{3,7},{4,8},{5,1},{6,10},{7,3},{8,4},{9,13},{1... | collective-permute-start | bytes 122888 | tf_op jit(solution)/shard_map/ppermute | solution.py:276
  9.7 7.3 %collective-permute-start.5 = (f32[1,1152]{1,0:T(1,128)S(1)}, f32[1,1152]{1,0:T(1,128)S(1)}, u32[]{:S(2)}, u32[]{:S(2)}) collective-permute-start(f32[1,1152]{1,0:T(1,128)S(1)} %get-tuple-element.34), channel_id=1, source_target_pairs={{2,1},{3,4},{4,3},{5,6},{6,5},{7,8},{8,7},{9,10},{10,9},{11,12},{1... | collective-permute-start | bytes 13832 | tf_op jit(solution)/shard_map/ppermute | solution.py:27
  12.3 12.7 %collective-permute-start.2 = (bf16[16,1280]{1,0:T(8,128)(2,1)S(1)}, bf16[16,1280]{1,0:T(8,128)(2,1)S(1)}, u32[]{:S(2)}, u32[]{:S(2)}) collective-permute-start(bf16[16,1280]{1,0:T(8,128)(2,1)S(1)} %pad_maximum_fusion), channel_id=1, source_target_pairs={{0,8},{2,10},{4,12},{6,14},{8,0},{10,2},{12,4},{14,6},{1,9},{3,11}... | collective-permute-start | bytes 122888 | tf_op jit(solution)/shard_map/ppermute | solution.py:31
  17.9 14.5 %all-to-all-start = ((bf16[16,8,1280]{2,1,0:T(8,128)(2,1)}), bf16[16,8,1280]{2,1,0:T(8,128)(2,1)S(1)}, u32[]{:S(2)}, u32[]{:S(2)}) async-start(bf16[16,8,1280]{2,1,0:T(8,128)(2,1)} %get-tuple-element.36), calls=%async_computation | async-start | bytes 655360 | tf_op jit(solution)/shard_map/all_to_all | solution.py:37
  24.9 1.3 %collective-permute-start.3 = (bf16[16,1280]{1,0:T(8,128)(2,1)S(1)}, bf16[16,1280]{1,0:T(8,128)(2,1)S(1)}, u32[]{:S(2)}, u32[]{:S(2)}) collective-permute-start(bf16[16,1280]{1,0:T(8,128)(2,1)S(1)} %collective-permute-done.1), channel_id=1, source_target_pairs={{0,1},{1,0},{2,3},{3,2},{4,5},{5,4},{6,7},{7,6},{8,9},{9,8},{10,11... | collective-permute-start | bytes 122888 | tf_op jit(solution)/shard_map/ppermute | solution.py:31
  26.2 6.3 %collective-permute-start.4 = (bf16[64,1280]{1,0:T(8,128)(2,1)S(1)}, bf16[64,1280]{1,0:T(8,128)(2,1)S(1)}, u32[]{:S(2)}, u32[]{:S(2)}) collective-permute-start(bf16[64,1280]{1,0:T(8,128)(2,1)S(1)} %constant_dynamic-update-slice_fusion.near_ref), channel_id=1, source_target_pairs={{0,2},{2,0},{4,6},{6,4},{8,10},{10,8},{12,14},{14,12},{1,3},{3,1},... | collective-permute-start | bytes 491528 | tf_op jit(solution)/shard_map/ppermute | solution.py:31
  33.9 26.5 %copy-start = (s32[256]{0:T(256)S(1)}, s32[256]{0:T(256)}, u32[]{:S(2)}) copy-start(s32[256]{0:T(256)} %param.9) | copy-start | bytes 3076
  33.9 12.6 %all-to-all-start.1 = ((bf16[16,8,1408]{2,1,0:T(8,128)(2,1)}), bf16[16,8,1408]{2,1,0:T(8,128)(2,1)S(1)}, u32[]{:S(2)}, u32[]{:S(2)}) async-start(bf16[16,8,1408]{2,1,0:T(8,128)(2,1)} %bitcast.5), calls=%async_computation.1 | async-start | bytes 720896 | tf_op jit(solution)/shard_map/all_to_all | solution.py:37
  41.2 5.6 %collective-permute-start.6 = (bf16[64,1152]{1,0:T(8,128)(2,1)S(1)}, bf16[64,1152]{1,0:T(8,128)(2,1)S(1)}, u32[]{:S(2)}, u32[]{:S(2)}) collective-permute-start(bf16[64,1152]{1,0:T(8,128)(2,1)S(1)} %get-tuple-element.38), channel_id=1, source_target_pairs={{0,1},{1,0},{2,3},{3,2},{4,5},{5,4},{6,7},{7,6},{8,9},{9,8},{10,11... | collective-permute-start | bytes 442376 | tf_op jit(solution)/shard_map/ppermute | solution.py:31
  46.7 1.3 %collective-permute-start.7 = (f32[8,256]{1,0:T(8,128)S(1)}, f32[8,256]{1,0:T(8,128)S(1)}, u32[]{:S(2)}, u32[]{:S(2)}) collective-permute-start(f32[8,256]{1,0:T(8,128)S(1)} %get-tuple-element.42.totals_ref), channel_id=1, source_target_pairs={{0,1},{1,0},{2,3},{3,2},{4,5},{5,4},{6,7},{7,6},{8,9},{9,8},{10,11... | collective-permute-start | bytes 24584 | tf_op jit(solution)/shard_map/ppermute | solution.py:31
  48.6 13.3 %all-to-all-start.2 = ((bf16[8,8,1408]{2,1,0:T(8,128)(2,1)}), bf16[8,8,1408]{2,1,0:T(8,128)(2,1)S(1)}, u32[]{:S(2)}, u32[]{:S(2)}) async-start(bf16[8,8,1408]{2,1,0:T(8,128)(2,1)} %shard_map.106), calls=%async_computation.2 | async-start | bytes 360448 | tf_op jit(solution)/shard_map/all_to_all | solution.py:37
  53.1 2.3 %collective-permute-start.9 = (f32[1,1152]{1,0:T(1,128)S(1)}, f32[1,1152]{1,0:T(1,128)S(1)}, u32[]{:S(2)}, u32[]{:S(2)}) collective-permute-start(f32[1,1152]{1,0:T(1,128)S(1)} %get-tuple-element.47), channel_id=1, source_target_pairs={{0,1},{1,0},{2,3},{3,2},{4,5},{5,4},{6,7},{7,6},{8,9},{9,8},{10,11... | collective-permute-start | bytes 13832 | tf_op jit(solution)/shard_map/ppermute | solution.py:31
  53.1 7.3 %collective-permute-start.8 = (f32[1,1152]{1,0:T(1,128)S(1)}, f32[1,1152]{1,0:T(1,128)S(1)}, u32[]{:S(2)}, u32[]{:S(2)}) collective-permute-start(f32[1,1152]{1,0:T(1,128)S(1)} %get-tuple-element.47), channel_id=1, source_target_pairs={{1,2},{4,3},{3,4},{6,5},{5,6},{8,7},{7,8},{10,9},{9,10},{12,11},{1... | collective-permute-start | bytes 13832 | tf_op jit(solution)/shard_map/ppermute | solution.py:27

commit v13 on v12

--- a/solution.py
+++ b/solution.py
@@ -124,11 +124,11 @@
 
 
 def pair_math(
-    knobs_ref, near_ref, far_ref, text_ref, gain_ref, text_hbm, keep_out, send_out, part_ref, packed_ref, sems
+    knobs_ref, chip_ref, even_ref, beside_ref, far_ref, text_ref, gain_ref, text_hbm, keep_out, send_out, part_ref, packed_ref, sems
 ):
     width = gain_ref.shape[1]
     scale = jnp.exp(knobs_ref[:, :1])
-    rows = jnp.concatenate([near_ref[...], far_ref[...]], axis=0)
+    rows = jnp.concatenate([chip_ref[...], even_ref[...], beside_ref[...], far_ref[...]], axis=0)
     image, text = rows[:, :width], text_ref[:, :width]
     contract = (((1,), (1,)), ((), ()))
     scaled = scale * lax.dot_general(image, text, contract, preferred_element_type=F32)
@@ -168,10 +168,8 @@
     rest.start()
     image_part = scale * jnp.dot(coeffs.astype(BF16), text, preferred_element_type=F32)
     for k in range(keep_out.shape[0] // 8):
-        own = 16 * k + (8 if k % 4 == 3 else 0)
-        far = 32 * k + 8 - own
-        keep_out[8 * k : 8 * (k + 1)] = image_part[own : own + 8]
-        send_out[8 * k : 8 * (k + 1)] = image_part[far : far + 8].astype(BF16)
+        keep_out[8 * k : 8 * (k + 1)] = image_part[16 * k : 16 * k + 8]
+        send_out[8 * k : 8 * (k + 1)] = image_part[16 * k + 8 : 16 * (k + 1)].astype(BF16)
     move.wait()
     rest.wait()
 
@@ -199,10 +197,11 @@
         rest, cells = rest - part, jnp.where(row == r, part, cells)
     packed = jnp.concatenate([total[:, :LANES], cells], axis=1).astype(BF16)
     for k in range(places):
-        there = k ^ 2 if k % 2 else k
+        moved = k % 4 in (1, 2)
+        there = k ^ 3 if moved else k
         block = keep_ref[pairs * k : pairs * (k + 1)]
         block = block + came_ref[pairs * there : pairs * (there + 1)].astype(F32)
-        turn = (1 - place_ref[0] % 2) * 4 if k % 2 else 0
+        turn = (1 - place_ref[0] % 2) * 6 if moved else 0
         place = places - 1 - ((place_ref[0] // 2) ^ FROM[k] ^ turn)
         out_ref[place, :, :width] = block.astype(BF16)
         out_ref[place, :, width:] = packed
@@ -273,11 +272,21 @@
     arrived = beside(spill, True)
     chip = jnp.concatenate([row[:pairs], other[:pairs]], axis=0)
     line = lax.axis_size((Z, C))
-    first = lax.ppermute(chip, (Z, C), [(i, i ^ (4 if i % 2 else 12)) for i in range(line)])
-    second = exchange(chip, Z, 4)
-    third = exchange(first, C, 1)
-    near = jnp.concatenate([chip, first, second, third], axis=0)
-    far = exchange(near, Z, 1)
+
+    def by_core(value, zero, one):
+        return lax.ppermute(value, (Z, C), [(i, i ^ 2 * (one if i % 2 else zero)) for i in range(line)])
+
+    def turned(block):
+        return jnp.concatenate([block[pairs:], block[:pairs]], axis=0)
+
+    first = by_core(chip, 4, 2)
+    second = by_core(chip, 1, 6)
+    crossed = exchange(jnp.concatenate([first, second], axis=0), C, 1)
+    third, fourth = turned(crossed[: 2 * pairs]), turned(crossed[2 * pairs :])
+    odd_core = lax.axis_index(C) == 1
+    six, beside_one = jnp.where(odd_core, second, fourth), jnp.where(odd_core, fourth, second)
+    even = jnp.concatenate([first, third, six], axis=0)
+    far = exchange(even, Z, 1)
     far, log_scale, logit_bias = lax.optimization_barrier((far, log_scale, logit_bias))
     lane = lax.broadcasted_iota(jnp.int32, (1, LANES), 1)
     knobs = jnp.where(lane == 0, log_scale[0], logit_bias[0])
@@ -289,14 +298,14 @@
     texts = to_all(rows, PLANE).reshape(plane * pairs, wide)
 
     text_part, keep, send = local(
-        pair_math, [VMEM] * 5,
+        pair_math, [VMEM] * 7,
         ((plane * pairs, wide + LANES), BF16), ((depth * pairs, width), F32), ((depth * pairs, width), BF16),
         to=[HBM, VMEM, VMEM],
         scratch=(
             pltpu.VMEM((plane * pairs, width), BF16), pltpu.VMEM((plane * pairs, 2 * LANES), BF16),
             pltpu.SemaphoreType.DMA((2,)),
         ),
-    )(knobs, near, far, texts, gain)
+    )(knobs, chip, even, beside_one, far, texts, gain)
 
     back = to_all(text_part.reshape(plane, pairs, wide + LANES), PLANE)
     came = exchange(send, C, 1)

time: 63.1 us -> 66.7 us (1.057)
  starting transfers between devices: 30.2 us -> 37.4 us
  waiting for transfers between devices: 23.5 us -> 20 us
    ppermute x2, starting transfers between devices: 4.89 us -> 8.62 us  [beside(): lax.ppermute(value, DP, across if ahead else [(b, a) for a, b in across])]
    ppermute x2, waiting for transfers between devices: 9.7 us -> 6.38 us  [beside(): lax.ppermute(value, DP, across if ahead else [(b, a) for a, b in across])]
    ppermute x1 -> x2, waiting for transfers between devices: 0.01 us -> 2.56 us  [by_core(): lax.ppermute(value, (Z, C), [(i, i ^ 2 * (one if i % 2 else zero)) for i...]
    ppermute x7 -> x6, waiting for transfers between devices: 8.46 us -> 5.91 us  [exchange(): lax.ppermute(value, axis, [(i, i ^ bit) for i in range(lax.axis_size(axis...]
    ppermute x1 -> x2, starting transfers between devices: 6.39 us -> 8.29 us  [by_core(): lax.ppermute(value, (Z, C), [(i, i ^ 2 * (one if i % 2 else zero)) for i...]
    all_to_all x3, starting transfers between devices: 18.7 us -> 20.2 us  [to_all(): lax.all_to_all(blocks, axes, 0, 0, tiled=True, axis_index_groups=backward)]
where the time goes in v13:
time: 66.7 us; the launch traced here: 66.3 us
  starting transfers between devices  37.4 us (56%)
  waiting for transfers between devices  20 us (30%)
  Pallas kernels  6.82 us (10%)
  between operations  2.06 us (3%)
    all_to_all x3, starting transfers between devices, to_all(): lax.all_to_all(blocks, axes, 0, 0, tiled=True, axis_index_groups=backward)  20.2 us
    ppermute x2, starting transfers between devices, beside(): lax.ppermute(value, DP, across if ahead else [(b, a) for a, b in across])  8.62 us
    ppermute x2, starting transfers between devices, by_core(): lax.ppermute(value, (Z, C), [(i, i ^ 2 * (one if i % 2 else zero)) for i...  8.29 us
    ppermute x2, waiting for transfers between devices, beside(): lax.ppermute(value, DP, across if ahead else [(b, a) for a, b in across])  6.38 us
    ppermute x6, waiting for transfers between devices, exchange(): lax.ppermute(value, axis, [(i, i ^ bit) for i in range(lax.axis_size(axis...  5.91 us
    all_to_all x3, waiting for transfers between devices, to_all(): lax.all_to_all(blocks, axes, 0, 0, tiled=True, axis_index_groups=backward)  5.12 us
    ppermute x2, waiting for transfers between devices, by_core(): lax.ppermute(value, (Z, C), [(i, i ^ 2 * (one if i % 2 else zero)) for i...  2.56 us
    pallas_call x1, Pallas kernels, per_device(): local(pair_math, [VMEM] * 7, ((plane * pairs, wide + LANES), BF16), ((dep...  1.48 us
  transfers between devices with their start and end apart: 13, of which 7 were waited for; matrix products, arithmetic and copies ran while one was open for 0% of the time, Pallas kernels for 4%

profile of v13, /device:TPU:8, one launch (start us, length us, event | category | flops | bytes accessed | tf_op | source)
XLA Modules:
  0.0 66.3 jit_solution(5175599707524816540)
XLA Ops:
  0.6 1.4 %shard_map.102 = (bf16[16,1280]{1,0:T(8,128)(2,1)S(1)}, f32[8,1152]{1,0:T(8,128)S(1)}, f32[8,1]{1,0:T(8,128)S(1)}, f32[8,1152]{1,0:T(8,128)S(1)}, f32[1,1152]{1,...) custom-call(s32[8]{0:T(128)} %groups_hbm.1, s32[1,256]{1,0:T(1,128)} %bitcast.9, ...), custom_call_target="tpu_custom_call" | custom-call | tf_op jit(solution)/shard_map/pallas_call | solution.py:255
  2.0 0.1 collective-permute-start
  2.1 1.2 %collective-permute-done.other_ref = bf16[16,1280]{1,0:T(8,128)(2,1)S(1)} collective-permute-done((bf16[16,1280]{1,0:T(8,128)(2,1)S(1)}, bf16[16,1280]{1,0:T(8,128)(2,1)S(1)}, u32[]{:S(2)}, u32[]{:S(2)}) %collective-permute-start) | collective-permute-done | bytes 40992 | tf_op jit(solution)/shard_map/ppermute | solution.py:31
  3.3 2.0 %collective-permute-start.2 = (bf16[16,1280]{1,0:T(8,128)(2,1)S(1)}, bf16[16,1280]{1,0:T(8,128)(2,1)S(1)}, u32[]{:S(2)}, u32[]{:S(2)}) collective-permute-start(bf16[16,1280]{1,0:T(8,128)(2,1)S(1)} %pad_maximum_fusion.2.chip_ref), channel_id=1, source_target_pairs={{0,2},{1,13},{2,0},{3,15},{4,6},{5,9},{6,4},{7,11},{8,10},{9,5},{1... | collective-permute-start | bytes 122888 | tf_op jit(solution)/shard_map/ppermute | solution.py:277
  5.3 6.3 %collective-permute-start.1 = (bf16[16,1280]{1,0:T(8,128)(2,1)S(1)}, bf16[16,1280]{1,0:T(8,128)(2,1)S(1)}, u32[]{:S(2)}, u32[]{:S(2)}) collective-permute-start(bf16[16,1280]{1,0:T(8,128)(2,1)S(1)} %pad_maximum_fusion.2.chip_ref), channel_id=1, source_target_pairs={{0,8},{1,5},{2,10},{3,7},{4,12},{5,1},{6,14},{7,3},{8,0},{9,13},{1... | collective-permute-start | bytes 122888 | tf_op jit(solution)/shard_map/ppermute | solution.py:277
  11.6 0.0 collective-permute-done.2
  11.6 2.6 %collective-permute-done.1 = bf16[16,1280]{1,0:T(8,128)(2,1)S(1)} collective-permute-done((bf16[16,1280]{1,0:T(8,128)(2,1)S(1)}, bf16[16,1280]{1,0:T(8,128)(2,1)S(1)}, u32[]{:S(2)}, u32[]{:S(2)}) %collective-permute-start.1) | collective-permute-done | bytes 40992 | tf_op jit(solution)/shard_map/ppermute | solution.py:277
  14.2 0.0 collective-permute-start.3
  14.2 6.2 %collective-permute-start.5 = (f32[1,1152]{1,0:T(1,128)S(1)}, f32[1,1152]{1,0:T(1,128)S(1)}, u32[]{:S(2)}, u32[]{:S(2)}) collective-permute-start(f32[1,1152]{1,0:T(1,128)S(1)} %get-tuple-element.34), channel_id=1, source_target_pairs={{2,1},{3,4},{4,3},{5,6},{6,5},{7,8},{8,7},{9,10},{10,9},{11,12},{1... | collective-permute-start | bytes 13832 | tf_op jit(solution)/shard_map/ppermute | solution.py:27
  20.4 1.3 %collective-permute-done.5.chip_ref = f32[1,1152]{1,0:T(1,128)S(1)} collective-permute-done((f32[1,1152]{1,0:T(1,128)S(1)}, f32[1,1152]{1,0:T(1,128)S(1)}, u32[]{:S(2)}, u32[]{:S(2)}) %collective-permute-start.5) | collective-permute-done | bytes 4640 | tf_op jit(solution)/shard_map/ppermute | solution.py:27
  21.7 0.9 %shard_map.103 = (bf16[16,8,1280]{2,1,0:T(8,128)(2,1)}, f32[8,1152]{1,0:T(8,128)S(1)}, f32[8,1]{1,0:T(8,128)S(1)}) custom-call(bf16[8,128]{1,0:T(8,128)(2,1)S(1)} %get-tuple-element.31.tile_ref, s32[1,128]{1,0:T(1,128)S(1)} %get-tuple-element.32.sides_ref, f32[8,1152]{1,0:T(8,128)S(1)} %get-tuple-element.33.pooled_ref, ...), custom_call_target="tpu_custom_call" | custom-call | tf_op jit(solution)/shard_map/pallas_call | solution.py:294
  22.7 6.9 %all-to-all-start = ((bf16[16,8,1280]{2,1,0:T(8,128)(2,1)}), bf16[16,8,1280]{2,1,0:T(8,128)(2,1)S(1)}, u32[]{:S(2)}, u32[]{:S(2)}) async-start(bf16[16,8,1280]{2,1,0:T(8,128)(2,1)} %get-tuple-element.36), calls=%async_computation | async-start | bytes 655360 | tf_op jit(solution)/shard_map/all_to_all | solution.py:37
  29.6 0.0 collective-permute-done.3
  29.7 0.1 collective-permute-start.4
  31.1 3.6 %collective-permute-done.4.far_ref = bf16[48,1280]{1,0:T(8,128)(2,1)S(1)} collective-permute-done((bf16[48,1280]{1,0:T(8,128)(2,1)S(1)}, bf16[48,1280]{1,0:T(8,128)(2,1)S(1)}, u32[]{:S(2)}, u32[]{:S(2)}) %collective-permute-start.4) | collective-permute-done | bytes 122912 | tf_op jit(solution)/shard_map/ppermute | solution.py:31
  34.6 0.0 all-to-all-done
  34.6 1.5 %shard_map.104 = (bf16[128,1408]{1,0:T(8,128)(2,1)}, f32[64,1152]{1,0:T(8,128)S(1)}, bf16[64,1152]{1,0:T(8,128)(2,1)S(1)}) custom-call(f32[1,128]{1,0:T(1,128)S(1)} %compare_select_fusion.knobs_ref, bf16[16,1280]{1,0:T(8,128)(2,1)S(1)} %pad_maximum_fusion.2.chip_ref, bf16[48,1280]{1,0:T(8,128)(2,1)S(1)} %pad_maximum_fusion.even_ref, ...), custom_call_target="tpu_custom_call" | custom-call | tf_op jit(solution)/shard_map/pallas_call | solution.py:300
  36.1 0.0 copy-start
  36.1 7.5 %all-to-all-start.1 = ((bf16[16,8,1408]{2,1,0:T(8,128)(2,1)}), bf16[16,8,1408]{2,1,0:T(8,128)(2,1)S(1)}, u32[]{:S(2)}, u32[]{:S(2)}) async-start(bf16[16,8,1408]{2,1,0:T(8,128)(2,1)} %bitcast.5), calls=%async_computation.1 | async-start | bytes 720896 | tf_op jit(solution)/shard_map/all_to_all | solution.py:37
  43.6 0.0 collective-permute-start.6
  43.7 5.1 %all-to-all-done.1.back_ref = bf16[16,8,1408]{2,1,0:T(8,128)(2,1)S(1)} async-done(((bf16[16,8,1408]{2,1,0:T(8,128)(2,1)}), bf16[16,8,1408]{2,1,0:T(8,128)(2,1)S(1)}, u32[]{:S(2)}, u32[]{:S(2)}) %all-to-all-start.1) | async-done | bytes 360480 | tf_op jit(solution)/shard_map/all_to_all | solution.py:37
  48.8 0.1 shard_map.105
  48.9 0.1 collective-permute-start.7
  49.0 0.0 collective-permute-done.6.came_ref
  49.0 1.1 %collective-permute-done.7.other_ref = f32[8,256]{1,0:T(8,128)S(1)} collective-permute-done((f32[8,256]{1,0:T(8,128)S(1)}, f32[8,256]{1,0:T(8,128)S(1)}, u32[]{:S(2)}, u32[]{:S(2)}) %collective-permute-start.7) | collective-permute-done | bytes 8224 | tf_op jit(solution)/shard_map/ppermute | solution.py:31
  50.2 0.7 %shard_map.106 = bf16[8,8,1408]{2,1,0:T(8,128)(2,1)} custom-call(s32[1]{0:T(128)} %bitcast.place_ref, f32[64,1152]{1,0:T(8,128)S(1)} %get-tuple-element.37.keep_ref, bf16[64,1152]{1,0:T(8,128)(2,1)S(1)} %collective-permute-done.6.came_ref, f32[8,256]{1,0:T(8,128)S(1)} %get-tuple-element.42.totals_ref, f32[8,256]{1,0:T(8,128)S(1)} %collective-permute-done.7.other_ref), custom_call_target="tpu_custom_call" | custom-call | tf_op jit(solution)/shard_map/pallas_call | solution.py:317
  50.9 5.8 %all-to-all-start.2 = ((bf16[8,8,1408]{2,1,0:T(8,128)(2,1)}), bf16[8,8,1408]{2,1,0:T(8,128)(2,1)S(1)}, u32[]{:S(2)}, u32[]{:S(2)}) async-start(bf16[8,8,1408]{2,1,0:T(8,128)(2,1)} %shard_map.106), calls=%async_computation.2 | async-start | bytes 360448 | tf_op jit(solution)/shard_map/all_to_all | solution.py:37
  56.6 0.0 collective-permute-start.9
  56.6 2.4 %collective-permute-start.8 = (f32[1,1152]{1,0:T(1,128)S(1)}, f32[1,1152]{1,0:T(1,128)S(1)}, u32[]{:S(2)}, u32[]{:S(2)}) collective-permute-start(f32[1,1152]{1,0:T(1,128)S(1)} %get-tuple-element.47), channel_id=1, source_target_pairs={{1,2},{4,3},{3,4},{6,5},{5,6},{8,7},{7,8},{10,9},{9,10},{12,11},{1... | collective-permute-start | bytes 13832 | tf_op jit(solution)/shard_map/ppermute | solution.py:27
  59.1 5.0 %collective-permute-done.8.chip_ref = f32[1,1152]{1,0:T(1,128)S(1)} collective-permute-done((f32[1,1152]{1,0:T(1,128)S(1)}, f32[1,1152]{1,0:T(1,128)S(1)}, u32[]{:S(2)}, u32[]{:S(2)}) %collective-permute-start.8) | collective-permute-done | bytes 4640 | tf_op jit(solution)/shard_map/ppermute | solution.py:27
  64.1 1.4 %shard_map.108 = f32[256,1152]{1,0:T(8,128)} custom-call(s32[1,256]{1,0:T(1,128)S(1)} %bitcast.10, s32[1,128]{1,0:T(1,128)S(1)} %get-tuple-element.32.sides_ref, f32[8,1152]{1,0:T(8,128)S(1)} %get-tuple-element.46.grad_ref, f32[1,1152]{1,0:T(1,128)S(1)} %collective-permute-done.8.chip_ref, f32[1,1152]{1,0:T(1,128)S(1)} %collective-permute-done.9.core_ref), custom_call_target="tpu_custom_call" | custom-call | tf_op jit(solution)/shard_map/pallas_call | solution.py:323
  65.6 0.7 %shard_map.107 = (f32[8,1152]{1,0:T(8,128)}, f32[1152]{0:T(1024)}, f32[3]{0:T(128)}) custom-call(bf16[8,8,1408]{2,1,0:T(8,128)(2,1)S(1)} %all-to-all-done.2.back_ref, f32[8,1152]{1,0:T(8,128)S(1)} %get-tuple-element.43.unit_ref, f32[8,1]{1,0:T(8,128)S(1)} %get-tuple-element.44.norm_ref), custom_call_target="tpu_custom_call" | custom-call | tf_op jit(solution)/shard_map/pallas_call | solution.py:324
  (11 shorter events, 0.1 us)
Async XLA Ops:
  2.0 1.3 %collective-permute-start = (bf16[16,1280]{1,0:T(8,128)(2,1)S(1)}, bf16[16,1280]{1,0:T(8,128)(2,1)S(1)}, u32[]{:S(2)}, u32[]{:S(2)}) collective-permute-start(bf16[16,1280]{1,0:T(8,128)(2,1)S(1)} %get-tuple-element.27), channel_id=1, source_target_pairs={{0,1},{1,0},{2,3},{3,2},{4,5},{5,4},{6,7},{7,6},{8,9},{9,8},{10,11... | collective-permute-start | bytes 122888 | tf_op jit(solution)/shard_map/ppermute | solution.py:31
  3.3 8.3 %collective-permute-start.2 = (bf16[16,1280]{1,0:T(8,128)(2,1)S(1)}, bf16[16,1280]{1,0:T(8,128)(2,1)S(1)}, u32[]{:S(2)}, u32[]{:S(2)}) collective-permute-start(bf16[16,1280]{1,0:T(8,128)(2,1)S(1)} %pad_maximum_fusion.2.chip_ref), channel_id=1, source_target_pairs={{0,2},{1,13},{2,0},{3,15},{4,6},{5,9},{6,4},{7,11},{8,10},{9,5},{1... | collective-permute-start | bytes 122888 | tf_op jit(solution)/shard_map/ppermute | solution.py:277
  5.3 8.9 %collective-permute-start.1 = (bf16[16,1280]{1,0:T(8,128)(2,1)S(1)}, bf16[16,1280]{1,0:T(8,128)(2,1)S(1)}, u32[]{:S(2)}, u32[]{:S(2)}) collective-permute-start(bf16[16,1280]{1,0:T(8,128)(2,1)S(1)} %pad_maximum_fusion.2.chip_ref), channel_id=1, source_target_pairs={{0,8},{1,5},{2,10},{3,7},{4,12},{5,1},{6,14},{7,3},{8,0},{9,13},{1... | collective-permute-start | bytes 122888 | tf_op jit(solution)/shard_map/ppermute | solution.py:277
  14.2 15.4 %collective-permute-start.3 = (bf16[32,1280]{1,0:T(8,128)(2,1)S(1)}, bf16[32,1280]{1,0:T(8,128)(2,1)S(1)}, u32[]{:S(2)}, u32[]{:S(2)}) collective-permute-start(bf16[32,1280]{1,0:T(8,128)(2,1)S(1)} %pad_maximum_fusion.1), channel_id=1, source_target_pairs={{0,1},{1,0},{2,3},{3,2},{4,5},{5,4},{6,7},{7,6},{8,9},{9,8},{10,11... | collective-permute-start | bytes 245768 | tf_op jit(solution)/shard_map/ppermute | solution.py:31
  14.2 7.5 %collective-permute-start.5 = (f32[1,1152]{1,0:T(1,128)S(1)}, f32[1,1152]{1,0:T(1,128)S(1)}, u32[]{:S(2)}, u32[]{:S(2)}) collective-permute-start(f32[1,1152]{1,0:T(1,128)S(1)} %get-tuple-element.34), channel_id=1, source_target_pairs={{2,1},{3,4},{4,3},{5,6},{6,5},{7,8},{8,7},{9,10},{10,9},{11,12},{1... | collective-permute-start | bytes 13832 | tf_op jit(solution)/shard_map/ppermute | solution.py:27
  22.7 12.0 %all-to-all-start = ((bf16[16,8,1280]{2,1,0:T(8,128)(2,1)}), bf16[16,8,1280]{2,1,0:T(8,128)(2,1)S(1)}, u32[]{:S(2)}, u32[]{:S(2)}) async-start(bf16[16,8,1280]{2,1,0:T(8,128)(2,1)} %get-tuple-element.36), calls=%async_computation | async-start | bytes 655360 | tf_op jit(solution)/shard_map/all_to_all | solution.py:37
  29.7 5.0 %collective-permute-start.4 = (bf16[48,1280]{1,0:T(8,128)(2,1)S(1)}, bf16[48,1280]{1,0:T(8,128)(2,1)S(1)}, u32[]{:S(2)}, u32[]{:S(2)}) collective-permute-start(bf16[48,1280]{1,0:T(8,128)(2,1)S(1)} %pad_maximum_fusion.even_ref), channel_id=1, source_target_pairs={{0,2},{2,0},{4,6},{6,4},{8,10},{10,8},{12,14},{14,12},{1,3},{3,1},... | collective-permute-start | bytes 368648 | tf_op jit(solution)/shard_map/ppermute | solution.py:31
  36.1 28.0 %copy-start = (s32[256]{0:T(256)S(1)}, s32[256]{0:T(256)}, u32[]{:S(2)}) copy-start(s32[256]{0:T(256)} %param.9) | copy-start | bytes 3076
  36.1 12.6 %all-to-all-start.1 = ((bf16[16,8,1408]{2,1,0:T(8,128)(2,1)}), bf16[16,8,1408]{2,1,0:T(8,128)(2,1)S(1)}, u32[]{:S(2)}, u32[]{:S(2)}) async-start(bf16[16,8,1408]{2,1,0:T(8,128)(2,1)} %bitcast.5), calls=%async_computation.1 | async-start | bytes 720896 | tf_op jit(solution)/shard_map/all_to_all | solution.py:37
  43.6 5.4 %collective-permute-start.6 = (bf16[64,1152]{1,0:T(8,128)(2,1)S(1)}, bf16[64,1152]{1,0:T(8,128)(2,1)S(1)}, u32[]{:S(2)}, u32[]{:S(2)}) collective-permute-start(bf16[64,1152]{1,0:T(8,128)(2,1)S(1)} %get-tuple-element.38), channel_id=1, source_target_pairs={{0,1},{1,0},{2,3},{3,2},{4,5},{5,4},{6,7},{7,6},{8,9},{9,8},{10,11... | collective-permute-start | bytes 442376 | tf_op jit(solution)/shard_map/ppermute | solution.py:31
  48.9 1.3 %collective-permute-start.7 = (f32[8,256]{1,0:T(8,128)S(1)}, f32[8,256]{1,0:T(8,128)S(1)}, u32[]{:S(2)}, u32[]{:S(2)}) collective-permute-start(f32[8,256]{1,0:T(8,128)S(1)} %get-tuple-element.42.totals_ref), channel_id=1, source_target_pairs={{0,1},{1,0},{2,3},{3,2},{4,5},{5,4},{6,7},{7,6},{8,9},{9,8},{10,11... | collective-permute-start | bytes 24584 | tf_op jit(solution)/shard_map/ppermute | solution.py:31
  50.9 14.7 %all-to-all-start.2 = ((bf16[8,8,1408]{2,1,0:T(8,128)(2,1)}), bf16[8,8,1408]{2,1,0:T(8,128)(2,1)S(1)}, u32[]{:S(2)}, u32[]{:S(2)}) async-start(bf16[8,8,1408]{2,1,0:T(8,128)(2,1)} %shard_map.106), calls=%async_computation.2 | async-start | bytes 360448 | tf_op jit(solution)/shard_map/all_to_all | solution.py:37
  56.6 2.4 %collective-permute-start.9 = (f32[1,1152]{1,0:T(1,128)S(1)}, f32[1,1152]{1,0:T(1,128)S(1)}, u32[]{:S(2)}, u32[]{:S(2)}) collective-permute-start(f32[1,1152]{1,0:T(1,128)S(1)} %get-tuple-element.47), channel_id=1, source_target_pairs={{0,1},{1,0},{2,3},{3,2},{4,5},{5,4},{6,7},{7,6},{8,9},{9,8},{10,11... | collective-permute-start | bytes 13832 | tf_op jit(solution)/shard_map/ppermute | solution.py:31
  56.6 7.5 %collective-permute-start.8 = (f32[1,1152]{1,0:T(1,128)S(1)}, f32[1,1152]{1,0:T(1,128)S(1)}, u32[]{:S(2)}, u32[]{:S(2)}) collective-permute-start(f32[1,1152]{1,0:T(1,128)S(1)} %get-tuple-element.47), channel_id=1, source_target_pairs={{1,2},{4,3},{3,4},{6,5},{5,6},{8,7},{7,8},{10,9},{9,10},{12,11},{1... | collective-permute-start | bytes 13832 | tf_op jit(solution)/shard_map/ppermute | solution.py:27
